TPU v7x, 32 devices: a whole 2x2x4 slice. The times are simulated.
32 devices in a mesh: rows: 32 (over z, y, x, core).
Axes of the slice: x: 2, y: 2, z: 4, core: 2. Of those that a mesh axis runs over, the one named last changes fastest.
Arguments:
- elevation_grid: float32 [2048, 640], P('rows'), may hold values from -200 to 200
Outputs:
- slope_field: float32 [2048, 640], P('rows')
- bend_field: float32 [2048, 640], P('rows')
All inputs are finite; a program needn't handle non-finite values.
Results may differ from a plain program's by a relative error of at most 0.0003.
Values sent between devices are 32-bit elements; how exact they have to be, the bound alone decides.
No kernel may reach another device: no remote copies, remote signals or barrier semaphores. Data moves between devices by JAX's collectives and lax.ppermute only.
A program may use at most 64 MiB of HBM per device.

v0:
```python
import jax
import jax.numpy as jnp
from jax import lax
from jax.sharding import PartitionSpec as P

LEVELS = 4


TAPS = (0.0625, 0.25, 0.375, 0.25, 0.0625)
epsilon = 1e-06


def padded_2(block, sides, width):
    for axis, dim in sides:
        count = lax.axis_size(axis)
        forward = [(i, i + 1) for i in range(count - 1)]
        backward = [(target, source) for source, target in forward]
        low = lax.ppermute(
            lax.slice_in_dim(block, block.shape[dim] - width, None, axis=dim), axis, forward
        )
        high = lax.ppermute(lax.slice_in_dim(block, 0, width, axis=dim), axis, backward)
        block = jnp.concatenate([low, block, high], axis=dim)
    return block


def coarsen_axis(padded, axis):
    length = padded.shape[axis] - 4
    result = None
    for offset in range(5):
        piece = lax.slice_in_dim(padded, offset, offset + length, 2, axis)
        term = TAPS[offset] * piece
        result = term if result is None else result + term
    return result


def coarsen(padded_rows):
    halfway = coarsen_axis(padded_rows, 0)
    wider = jnp.pad(halfway, ((0, 0), (2, 2)), mode="edge")
    return coarsen_axis(wider, 1)


def derive(extended, spacing):
    padded = jnp.pad(extended, ((0, 0), (1, 1)), mode="edge")
    upper = padded[:-2]
    middle = padded[1:-1]
    lower = padded[2:]
    eastern = upper[:, 2:] + 2.0 * middle[:, 2:] + lower[:, 2:]
    western = upper[:, :-2] + 2.0 * middle[:, :-2] + lower[:, :-2]
    southern = lower[:, :-2] + 2.0 * lower[:, 1:-1] + lower[:, 2:]
    northern = upper[:, :-2] + 2.0 * upper[:, 1:-1] + upper[:, 2:]
    grad_x = (eastern - western) / (8.0 * spacing)
    grad_y = (southern - northern) / (8.0 * spacing)
    centre = middle[:, 1:-1]
    second_xx = (middle[:, 2:] - 2.0 * centre + middle[:, :-2]) / (spacing * spacing)
    second_yy = (lower[:, 1:-1] - 2.0 * centre + upper[:, 1:-1]) / (spacing * spacing)
    second_xy = (lower[:, 2:] - lower[:, :-2] - upper[:, 2:] + upper[:, :-2]) / (
        4.0 * spacing * spacing
    )
    steepness = grad_x * grad_x + grad_y * grad_y
    slope_part = jnp.arctan(jnp.sqrt(steepness))
    numerator = (
        grad_x * grad_x * second_xx
        + 2.0 * grad_x * grad_y * second_xy
        + grad_y * grad_y * second_yy
    )
    bend_part = -numerator / (1.0 + steepness) ** 1.5
    return (slope_part, bend_part)


def settle(extended, margin, begin_at, limit_rows):
    inside = extended.shape[0] - 2 * margin
    global_row = begin_at - margin + jnp.arange(extended.shape[0], dtype=jnp.int32)
    first_row = extended[margin : margin + 1]
    bottom = extended[margin + inside - 1 : margin + inside]
    extended = jnp.where((global_row < 0)[:, None], first_row, extended)
    return jnp.where((global_row >= limit_rows)[:, None], bottom, extended)


def refine_axis(padded, factor, axis):
    length = padded.shape[axis] - 2
    pieces = []
    for sub_row in range(factor):
        position = (sub_row + 0.5) / factor
        if sub_row < factor // 2:
            offset = 0
            fraction = position + 0.5
        else:
            offset = 1
            fraction = position - 0.5
        lower_side = lax.slice_in_dim(padded, offset, offset + length, 1, axis)
        upper_side = lax.slice_in_dim(padded, offset + 1, offset + 1 + length, 1, axis)
        pieces.append((1.0 - fraction) * lower_side + fraction * upper_side)
    stacked = jnp.stack(pieces, axis + 1)
    new_shape = list(padded.shape)
    new_shape[axis] = length * factor
    return stacked.reshape(new_shape)


def spread(part, octave):
    if octave == 0:
        return part[1:-1]
    factor = 2**octave
    taller = refine_axis(part, factor, 0)
    return refine_axis(jnp.pad(taller, ((0, 0), (1, 1)), mode="edge"), factor, 1)


def finish(slope_parts, bend_parts, slope_sums, square_sums, cell_counts):
    slope_total = None
    bend_total = None
    for octave in range(len(slope_parts)):
        mean_slope = slope_sums[octave] / cell_counts[octave]
        rms_bend = jnp.sqrt(square_sums[octave] / cell_counts[octave] + epsilon)
        slope_term = spread(slope_parts[octave], octave) / (mean_slope + epsilon)
        bend_term = spread(bend_parts[octave], octave) / rms_bend
        slope_total = slope_term if slope_total is None else slope_total + slope_term
        bend_total = bend_term if bend_total is None else bend_total + bend_term
    return (slope_total, bend_total)


def level_parts(window, octave, begin_at, limit_rows):
    slope_part, bend_part = derive(window, float(2**octave))
    return (settle(slope_part, 1, begin_at, limit_rows), settle(bend_part, 1, begin_at, limit_rows))


def local(elevation_grid):
    slab_line_number, present_span = elevation_grid.shape
    devices = lax.axis_size("rows")
    position = lax.axis_index("rows")
    slope_parts = []
    bend_parts = []
    height_now = slab_line_number
    surface_level = elevation_grid
    for octave in range(LEVELS + 1):
        begin_at = position * height_now
        limit_rows = devices * height_now
        window = padded_2(surface_level, (("rows", 0),), 2)
        window = settle(window, 2, begin_at, limit_rows)
        slope_part, bend_part = level_parts(window, octave, begin_at, limit_rows)
        slope_parts.append(slope_part)
        bend_parts.append(bend_part)
        if octave < LEVELS:
            surface_level = coarsen(window)
            height_now = height_now // 2
    local_first = jnp.stack([jnp.sum(part[1:-1]) for part in slope_parts])
    local_second = jnp.stack([jnp.sum(part[1:-1] * part[1:-1]) for part in bend_parts])
    slope_sums, square_sums = lax.psum((local_first, local_second), "rows")
    cell_counts = [
        devices * slab_line_number // 2**octave * (present_span // 2**octave)
        for octave in range(LEVELS + 1)
    ]
    return finish(slope_parts, bend_parts, slope_sums, square_sums, cell_counts)


def solution(mesh):
    return jax.shard_map(
        local,
        mesh=mesh,
        in_specs=(P("rows", None),),
        out_specs=(P("rows", None), P("rows", None)),
        check_vma=False,
    )
```

profile of v0, /device:TPU:0, one launch (start us, length us, event | category | flops | bytes accessed | tf_op | source)
XLA Modules:
  0.0 156.1 jit_solution(9525391565599252662)
XLA Ops:
  0.6 0.8 fusion.71
  1.6 1.3 collective-permute-start.1
  3.1 3.1 %collective-permute-start = (f32[2,640]{0,1:T(8,128)S(1)}, f32[2,640]{0,1:T(8,128)S(1)}, u32[]{:S(2)}, u32[]{:S(2)}) collective-permute-start(f32[2,640]{0,1:T(8,128)S(1)} %copy.215), channel_id=1, source_target_pairs={{0,1},{1,2},{2,3},{3,4},{4,5},{5,6},{6,7},{7,8},{8,9},{9,10},{10,1... | collective-permute-start | bytes 15368 | tf_op jit(solution)/shard_map/ppermute | solution.py:18
  7.7 0.7 power_multiply_fusion
  8.5 0.9 sqrt_atan2_fusion
  9.4 3.7 %slice.1089 = f32[32,640]{0,1:T(8,128)S(1)} slice(f32[68,640]{0,1:T(8,128)S(1)} %fusion.6), slice={[1:65:2], [0:640:1]} | slice | bytes 163840 | tf_op jit(solution)/shard_map/slice | solution.py:30
  13.0 3.4 %slice.1088 = f32[32,640]{0,1:T(8,128)S(1)} slice(f32[68,640]{0,1:T(8,128)S(1)} %fusion.6), slice={[0:64:2], [0:640:1]} | slice | bytes 163840 | tf_op jit(solution)/shard_map/slice | solution.py:30
  16.4 3.5 %slice.1092 = f32[32,640]{0,1:T(8,128)S(1)} slice(f32[68,640]{0,1:T(8,128)S(1)} %fusion.6), slice={[4:68:2], [0:640:1]} | slice | bytes 163840 | tf_op jit(solution)/shard_map/slice | solution.py:30
  19.9 3.5 %slice.1091 = f32[32,640]{0,1:T(8,128)S(1)} slice(f32[68,640]{0,1:T(8,128)S(1)} %fusion.6), slice={[3:67:2], [0:640:1]} | slice | bytes 163840 | tf_op jit(solution)/shard_map/slice | solution.py:30
  23.4 3.5 %slice.1090 = f32[32,640]{0,1:T(8,128)S(1)} slice(f32[68,640]{0,1:T(8,128)S(1)} %fusion.6), slice={[2:66:2], [0:640:1]} | slice | bytes 163840 | tf_op jit(solution)/shard_map/slice | solution.py:30
  27.4 1.4 slice.1101
  28.8 1.4 slice.1100
  30.2 1.4 slice.1099
  31.6 1.4 slice.1098
  33.0 1.4 slice.1097
  35.4 10.5 %collective-permute-start.2 = (f32[2,320]{1,0:T(2,128)S(1)}, f32[2,320]{1,0:T(2,128)S(1)}, u32[]{:S(2)}, u32[]{:S(2)}) collective-permute-start(f32[2,320]{1,0:T(2,128)S(1)} %get-tuple-element.72), channel_id=1, source_target_pairs={{0,1},{1,2},{2,3},{3,4},{4,5},{5,6},{6,7},{7,8},{8,9},{9,10},{10,1... | collective-permute-start | bytes 7688 | tf_op jit(solution)/shard_map/ppermute | solution.py:18
  45.9 1.5 collective-permute-start.3
  47.5 1.2 multiply_reduce_fusion
  48.8 2.2 %collective-permute-done.3 = f32[2,320]{1,0:T(2,128)S(1)} collective-permute-done((f32[2,320]{1,0:T(2,128)S(1)}, f32[2,320]{1,0:T(2,128)S(1)}, u32[]{:S(2)}, u32[]{:S(2)}) %collective-permute-start.3) | collective-permute-done | bytes 2592 | tf_op jit(solution)/shard_map/ppermute | solution.py:21
  54.2 4.3 %collective-permute-start.4 = (f32[2,160]{1,0:T(2,128)S(1)}, f32[2,160]{1,0:T(2,128)S(1)}, u32[]{:S(2)}, u32[]{:S(2)}) collective-permute-start(f32[2,160]{1,0:T(2,128)S(1)} %get-tuple-element.116), channel_id=1, source_target_pairs={{0,1},{1,2},{2,3},{3,4},{4,5},{5,6},{6,7},{7,8},{8,9},{9,10},{10,1... | collective-permute-start | bytes 3848 | tf_op jit(solution)/shard_map/ppermute | solution.py:18
  58.5 1.3 collective-permute-start.5
  64.0 3.4 %collective-permute-start.6 = (f32[2,80]{1,0:T(2,128)S(1)}, f32[2,80]{1,0:T(2,128)S(1)}, u32[]{:S(2)}, u32[]{:S(2)}) collective-permute-start(f32[2,80]{1,0:T(2,128)S(1)} %get-tuple-element.188), channel_id=1, source_target_pairs={{0,1},{1,2},{2,3},{3,4},{4,5},{5,6},{6,7},{7,8},{8,9},{9,10},{10,1... | collective-permute-start | bytes 1928 | tf_op jit(solution)/shard_map/ppermute | solution.py:18
  67.4 1.3 collective-permute-start.7
  72.8 4.2 %collective-permute-start.8 = (f32[2,40]{1,0:T(2,128)S(1)}, f32[2,40]{1,0:T(2,128)S(1)}, u32[]{:S(2)}, u32[]{:S(2)}) collective-permute-start(f32[2,40]{1,0:T(2,128)S(1)} %get-tuple-element.192), channel_id=1, source_target_pairs={{0,1},{1,2},{2,3},{3,4},{4,5},{5,6},{6,7},{7,8},{8,9},{9,10},{10,1... | collective-permute-start | bytes 968 | tf_op jit(solution)/shard_map/ppermute | solution.py:18
  77.0 1.3 collective-permute-start.9
  83.6 3.2 %stack.523 = f32[5]{0:T(128)S(1)} concatenate(f32[1]{0:T(128)} %bitcast.129, f32[1]{0:T(128)} %bitcast.130, f32[1]{0:T(128)} %bitcast.133, f32[1]{0:T(128)} %bitcast.136, f32[1]{0:T(128)} %bitcast.139), dimensions={0} | concatenate | bytes 40 | tf_op jit(solution)/shard_map/stack | solution.py:145
  86.8 3.3 %stack.449 = f32[5]{0:T(128)S(1)} concatenate(f32[1]{0:T(128)} %bitcast, f32[1]{0:T(128)} %bitcast.3, f32[1]{0:T(128)} %bitcast.8, f32[1]{0:T(128)} %bitcast.13, f32[1]{0:T(128)} %bitcast.18), dimensions={0} | concatenate | bytes 40 | tf_op jit(solution)/shard_map/stack | solution.py:144
  90.1 48.6 %all-reduce = (f32[5]{0:T(128)S(1)}, f32[5]{0:T(128)S(1)}) all-reduce(f32[5]{0:T(128)S(1)} %stack.449, f32[5]{0:T(128)S(1)} %stack.523), channel_id=1, replica_groups=mesh['rows'=32] {'rows'}, use_global_device_ids=true, to_apply=%region_5.6 | all-reduce | flops 10 | bytes 80 | tf_op jit(solution)/shard_map/psum | solution.py:146
  150.2 1.2 stack.517
  152.2 1.3 bitcast_add_fusion
  153.5 1.8 %copy.319 = f32[64,640]{1,0:T(8,128)} copy(f32[64,640]{0,1:T(8,128)} %get-tuple-element.194) | data formatting | bytes 327680
  155.3 0.8 copy.318
  (247 shorter events, 25.3 us)
Async XLA Ops:
  1.6 5.1 %collective-permute-start.1 = (f32[2,640]{0,1:T(8,128)S(1)}, f32[2,640]{0,1:T(8,128)S(1)}, u32[]{:S(2)}, u32[]{:S(2)}) collective-permute-start(f32[2,640]{0,1:T(8,128)S(1)} %copy.216), channel_id=1, source_target_pairs={{1,0},{2,1},{3,2},{4,3},{5,4},{6,5},{7,6},{8,7},{9,8},{10,9},{11,1... | collective-permute-start | bytes 15368 | tf_op jit(solution)/shard_map/ppermute | solution.py:21
  2.9 3.3 %copy-start = (f32[64,640]{1,0:T(8,128)S(1)}, f32[64,640]{1,0:T(8,128)}, u32[]{:S(2)}) copy-start(f32[64,640]{1,0:T(8,128)} %param.1) | copy-start | bytes 491524
  3.1 4.3 %collective-permute-start = (f32[2,640]{0,1:T(8,128)S(1)}, f32[2,640]{0,1:T(8,128)S(1)}, u32[]{:S(2)}, u32[]{:S(2)}) collective-permute-start(f32[2,640]{0,1:T(8,128)S(1)} %copy.215), channel_id=1, source_target_pairs={{0,1},{1,2},{2,3},{3,4},{4,5},{5,6},{6,7},{7,8},{8,9},{9,10},{10,1... | collective-permute-start | bytes 15368 | tf_op jit(solution)/shard_map/ppermute | solution.py:18
  6.5 40.9 %copy-start.14 = (pred[64]{0:T(512)(128)(4,1)}, pred[64]{0:T(512)(128)(4,1)S(1)}, u32[]{:S(2)}) copy-start(pred[64]{0:T(512)(128)(4,1)S(1)} %slice.1304) | copy-start | bytes 196
  6.6 40.8 %copy-start.16 = (pred[64]{0:T(512)(128)(4,1)}, pred[64]{0:T(512)(128)(4,1)S(1)}, u32[]{:S(2)}) copy-start(pred[64]{0:T(512)(128)(4,1)S(1)} %slice.1306) | copy-start | bytes 196
  34.9 12.6 %copy-start.8 = (f32[640]{0:T(1024)}, f32[640]{0:T(1024)S(1)}, u32[]{:S(2)}) copy-start(f32[640]{0:T(1024)S(1)} %get-tuple-element.13) | copy-start | bytes 7684
  35.3 12.1 %copy-start.10 = (f32[640]{0:T(1024)}, f32[640]{0:T(1024)S(1)}, u32[]{:S(2)}) copy-start(f32[640]{0:T(1024)S(1)} %get-tuple-element.14) | copy-start | bytes 7684
  35.3 12.1 %copy-start.12 = (f32[640]{0:T(1024)}, f32[640]{0:T(1024)S(1)}, u32[]{:S(2)}) copy-start(f32[640]{0:T(1024)S(1)} %get-tuple-element.15) | copy-start | bytes 7684
  35.4 13.4 %collective-permute-start.2 = (f32[2,320]{1,0:T(2,128)S(1)}, f32[2,320]{1,0:T(2,128)S(1)}, u32[]{:S(2)}, u32[]{:S(2)}) collective-permute-start(f32[2,320]{1,0:T(2,128)S(1)} %get-tuple-element.72), channel_id=1, source_target_pairs={{0,1},{1,2},{2,3},{3,4},{4,5},{5,6},{6,7},{7,8},{8,9},{9,10},{10,1... | collective-permute-start | bytes 7688 | tf_op jit(solution)/shard_map/ppermute | solution.py:18
  45.9 5.0 %collective-permute-start.3 = (f32[2,320]{1,0:T(2,128)S(1)}, f32[2,320]{1,0:T(2,128)S(1)}, u32[]{:S(2)}, u32[]{:S(2)}) collective-permute-start(f32[2,320]{1,0:T(2,128)S(1)} %get-tuple-element.73), channel_id=1, source_target_pairs={{1,0},{2,1},{3,2},{4,3},{5,4},{6,5},{7,6},{8,7},{9,8},{10,9},{11,1... | collective-permute-start | bytes 7688 | tf_op jit(solution)/shard_map/ppermute | solution.py:21
  54.2 8.0 %collective-permute-start.4 = (f32[2,160]{1,0:T(2,128)S(1)}, f32[2,160]{1,0:T(2,128)S(1)}, u32[]{:S(2)}, u32[]{:S(2)}) collective-permute-start(f32[2,160]{1,0:T(2,128)S(1)} %get-tuple-element.116), channel_id=1, source_target_pairs={{0,1},{1,2},{2,3},{3,4},{4,5},{5,6},{6,7},{7,8},{8,9},{9,10},{10,1... | collective-permute-start | bytes 3848 | tf_op jit(solution)/shard_map/ppermute | solution.py:18
  58.5 3.8 %collective-permute-start.5 = (f32[2,160]{1,0:T(2,128)S(1)}, f32[2,160]{1,0:T(2,128)S(1)}, u32[]{:S(2)}, u32[]{:S(2)}) collective-permute-start(f32[2,160]{1,0:T(2,128)S(1)} %get-tuple-element.117), channel_id=1, source_target_pairs={{1,0},{2,1},{3,2},{4,3},{5,4},{6,5},{7,6},{8,7},{9,8},{10,9},{11,1... | collective-permute-start | bytes 3848 | tf_op jit(solution)/shard_map/ppermute | solution.py:21
  64.0 6.7 %collective-permute-start.6 = (f32[2,80]{1,0:T(2,128)S(1)}, f32[2,80]{1,0:T(2,128)S(1)}, u32[]{:S(2)}, u32[]{:S(2)}) collective-permute-start(f32[2,80]{1,0:T(2,128)S(1)} %get-tuple-element.188), channel_id=1, source_target_pairs={{0,1},{1,2},{2,3},{3,4},{4,5},{5,6},{6,7},{7,8},{8,9},{9,10},{10,1... | collective-permute-start | bytes 1928 | tf_op jit(solution)/shard_map/ppermute | solution.py:18
  67.4 3.8 %collective-permute-start.7 = (f32[2,80]{1,0:T(2,128)S(1)}, f32[2,80]{1,0:T(2,128)S(1)}, u32[]{:S(2)}, u32[]{:S(2)}) collective-permute-start(f32[2,80]{1,0:T(2,128)S(1)} %get-tuple-element.189), channel_id=1, source_target_pairs={{1,0},{2,1},{3,2},{4,3},{5,4},{6,5},{7,6},{8,7},{9,8},{10,9},{11,1... | collective-permute-start | bytes 1928 | tf_op jit(solution)/shard_map/ppermute | solution.py:21
  72.8 8.7 %collective-permute-start.8 = (f32[2,40]{1,0:T(2,128)S(1)}, f32[2,40]{1,0:T(2,128)S(1)}, u32[]{:S(2)}, u32[]{:S(2)}) collective-permute-start(f32[2,40]{1,0:T(2,128)S(1)} %get-tuple-element.192), channel_id=1, source_target_pairs={{0,1},{1,2},{2,3},{3,4},{4,5},{5,6},{6,7},{7,8},{8,9},{9,10},{10,1... | collective-permute-start | bytes 968 | tf_op jit(solution)/shard_map/ppermute | solution.py:18
  77.0 4.5 %collective-permute-start.9 = (f32[2,40]{1,0:T(2,128)S(1)}, f32[2,40]{1,0:T(2,128)S(1)}, u32[]{:S(2)}, u32[]{:S(2)}) collective-permute-start(f32[2,40]{1,0:T(2,128)S(1)} %get-tuple-element.193), channel_id=1, source_target_pairs={{1,0},{2,1},{3,2},{4,3},{5,4},{6,5},{7,6},{8,7},{9,8},{10,9},{11,1... | collective-permute-start | bytes 968 | tf_op jit(solution)/shard_map/ppermute | solution.py:21
  149.3 0.7 copy-start.4
  149.4 0.7 copy-start.5
  149.4 0.7 copy-start.6
  149.4 0.7 copy-start.7
  149.5 0.7 copy-start.3
  149.5 0.7 copy-start.2
  149.5 0.7 copy-start.1
  151.5 0.7 copy-start.13
  151.5 0.7 copy-start.11
  151.5 0.7 copy-start.9
  151.5 0.7 copy-start.15
  151.6 0.7 copy-start.17
where the time goes:
time: 157 us; the launch traced here: 156 us
  blocking collectives  48.6 us (31%)
  local copies, waits for them, and re-layouts  47.8 us (30%)
  starting transfers between devices  32.1 us (20%)
  other arithmetic  16.1 us (10%)
  between operations  8.23 us (5%)
  waiting for transfers between devices  3.38 us (2%)
    psum x1, blocking collectives, local(): slope_sums, square_sums = lax.psum((local_first, local_second), 'rows')  48.6 us
    slice x40, local copies, waits for them, and re-layouts, coarsen_axis(): piece = lax.slice_in_dim(padded, offset, offset + length, 2, axis)  28.3 us
    ppermute x5, starting transfers between devices, padded_2(): lax.ppermute(lax.slice_in_dim(block, block.shape[dim] - width, None, axis...  25.4 us
    ppermute x5, starting transfers between devices, padded_2(): lax.ppermute(lax.slice_in_dim(block, 0, width, axis=dim), axis, backward)  6.68 us
    unnamed x39, local copies, waits for them, and re-layouts  4.22 us
    another operation x1, local copies, waits for them, and re-layouts, local(): local_first = jnp.stack([jnp.sum(part[1:-1]) for part in slope_parts])  3.26 us
    add x7, other arithmetic, refine_axis(): pieces.append((1.0 - fraction) * lower_side + fraction * upper_side)  3.24 us
    another operation x1, local copies, waits for them, and re-layouts, local(): jnp.stack([jnp.sum(part[1:-1] * part[1:-1]) for part in bend_parts])  3.2 us
  transfers between devices with their start and end apart: 10, of which 3 were waited for; matrix products, arithmetic and copies ran while one was open for 6% of the time, Pallas kernels for 0%

commit v1 on v0

v1 whole, which is shorter than its diff:
```python
import functools

import jax
import jax.numpy as jnp
from jax import lax
from jax.experimental import pallas as pl
from jax.experimental.pallas import tpu as pltpu
from jax.sharding import PartitionSpec as P

LEVELS = 4
EPS = 1e-06
OFF = 8
MSG_ROWS = 16
f32 = jnp.float32
bf16 = jnp.bfloat16
ATAN = (
    1.0,
    -0.3333314528,
    0.1999355085,
    -0.1420889944,
    0.1065626393,
    -0.0752896400,
    0.0429096138,
    -0.0161657367,
    0.0028662257,
)


def up128(n):
    return -(-n // 128) * 128


def up16(n):
    return -(-n // 16) * 16


def lane_of(v):
    return lax.broadcasted_iota(jnp.int32, v.shape, 1)


def row_of(v):
    return lax.broadcasted_iota(jnp.int32, v.shape, 0)


def west(v):
    return jnp.where(lane_of(v) == 0, v, pltpu.roll(v, 1, 1))


def east(v, width):
    return jnp.where(lane_of(v) == width - 1, v, pltpu.roll(v, v.shape[1] - 1, 1))


def split3(v):
    hi = v.astype(bf16)
    rest = v - hi.astype(f32)
    mid = rest.astype(bf16)
    low = (rest - mid.astype(f32)).astype(bf16)
    return hi, mid, low


def split2(v):
    hi = v.astype(bf16)
    return hi, (v - hi.astype(f32)).astype(bf16)


def mm(a, b):
    return jnp.dot(a, b, preferred_element_type=f32)


def picker():
    rows = lax.broadcasted_iota(jnp.int32, (256, 128), 0)
    cols = lax.broadcasted_iota(jnp.int32, (256, 128), 1)
    return (rows == 2 * cols).astype(f32).astype(bf16)


def take(ref, at, count):
    return jnp.concatenate([ref[c, at : at + count, :] for c in range(ref.shape[0])], axis=1)


def store(ref, at, v):
    for c in range(ref.shape[0]):
        ref[c, at : at + v.shape[0], :] = v[:, 128 * c : 128 * c + 128]


def rows_sum(ref, start, count):
    out = []
    for c in range(ref.shape[0]):
        part = [ref[c, pl.ds(start + a, count, 2), :] for a in range(5)]
        out.append((part[0] + part[4]) * 0.0625 + (part[1] + part[3]) * 0.25 + part[2] * 0.375)
    return jnp.concatenate(out, axis=1)


def cols_coarsen(v, width, pick):
    w1 = west(v)
    e1 = east(v, width)
    y = (west(w1) + east(e1, width)) * 0.0625 + (w1 + e1) * 0.25 + v * 0.375
    out = []
    for at in range(0, v.shape[1], 256):
        part = y[:, at : at + 256]
        sel = pick[: part.shape[1]]
        hi, mid, low = split3(part)
        out.append(mm(hi, sel) + (mm(mid, sel) + mm(low, sel)))
    return out[0] if len(out) == 1 else jnp.concatenate(out, axis=1)


def pyramid_kernel(sizes, x_ref, m1_ref, m2_ref, z1, z2, z3, z4, z0, tmp):
    pick = picker()
    store(z0, 0, x_ref[...])
    zs = [z0, z1, z2, z3, z4]
    low, high = 0, sizes[0][0] - 1
    spans = []
    for k in range(LEVELS):
        low, high = (low + 3) // 2, (high - 2) // 2
        spans.append((low, high))
        wp = up128(sizes[k][1])
        count = high - low + 1
        rows = -(-(high + 1) // 8) * 8
        tmp[low : high + 1, :wp] = rows_sum(zs[k], 2 * low - 2, count)
        store(zs[k + 1], 0, cols_coarsen(tmp[0:rows, :wp], sizes[k][1], pick))
    odd = lax.rem(lax.axis_index("rows"), 2) == 1
    h = sizes[0][0]

    def put(row, level, top_at, bottom_at, count):
        wp = up128(sizes[level][1])
        top = take(zs[level], top_at, count)
        bottom = take(zs[level], bottom_at, count)
        m1_ref[row : row + count, :wp] = jnp.where(odd, top, bottom)
        m2_ref[row : row + count, :wp] = jnp.where(odd, bottom, top)

    put(0, 0, 0, h - 4, 4)
    row = 4
    for k in range(1, LEVELS):
        low, high = spans[k - 1]
        put(row, k, low, high - 3, 4)
        row += 4
    m = spans[LEVELS - 1][1]
    wp = up128(sizes[LEVELS][1])
    at = m1_ref.shape[1] - wp
    m1_ref[12:13, at:] = take(zs[LEVELS], m, 1)
    m2_ref[12:13, at:] = take(zs[LEVELS], m, 1)


def relief(upper, middle, lower, width, spacing):
    diff = lower - upper
    ends = lower + upper
    tall = ends + 2.0 * middle
    m_e, m_w = east(middle, width), west(middle)
    d_e, d_w = east(diff, width), west(diff)
    p = (east(tall, width) - west(tall)) * (1.0 / (8.0 * spacing))
    q = (d_e + d_w + 2.0 * diff) * (1.0 / (8.0 * spacing))
    inv = 1.0 / (spacing * spacing)
    r = ((m_e - middle) - (middle - m_w)) * inv
    t = ((lower - middle) - (middle - upper)) * inv
    u = (d_e - d_w) * (0.25 * inv)
    pp, qq = p * p, q * q
    steep = pp + qq
    base = 1.0 + steep
    root = jnp.sqrt(base)
    y = jnp.sqrt(steep) / (1.0 + root)
    y2 = y * y
    acc = ATAN[-1]
    for c in ATAN[-2::-1]:
        acc = acc * y2 + c
    slope = 2.0 * y * acc
    bend = -(pp * r + 2.0 * (p * q) * u + qq * t) / (base * root)
    return slope, bend


def relief_kernel(sizes, mid, x_ref, z1, z2, z3, z4, r1_ref, r2_ref, r3_ref, s0_ref, b0_ref, f1, f2, f3, f4, sum_ref,
                  up, lo, ztop, zbot, w1, w2, w3, w4, tmp):
    me = lax.axis_index("rows")
    last_id = lax.axis_size("rows") - 1
    odd = lax.rem(me, 2) == 1
    first, last = me == 0, me == last_id
    r2 = r2_ref[...]
    if mid:
        r2 = jnp.where((me == mid) | (me == mid - 1), r3_ref[...], r2)
    r1 = r1_ref[...]
    up[...] = jnp.where(odd, r1, r2)
    lo[...] = jnp.where(odd, r2, r1)
    pick = picker()
    h0, width0 = sizes[0]

    store(ztop, 8, x_ref[0:8, :])
    store(ztop, 4, jnp.where(first, jnp.broadcast_to(x_ref[0:1, :], (4, width0)), up[0:4, :]))
    store(zbot, 0, x_ref[h0 - 8 : h0, :])
    store(zbot, 8, jnp.where(last, jnp.broadcast_to(x_ref[h0 - 1 : h0, :], (4, width0)), lo[0:4, :]))

    work = [None, w1, w2, w3, w4]
    given = [None, z1, z2, z3, z4]
    last_at = up.shape[1] - up128(sizes[LEVELS][1])
    for k in range(1, LEVELS + 1):
        h, width = sizes[k]
        wp, wq = up128(width), up128(sizes[k - 1][1])
        z = work[k]
        store(z, OFF, take(given[k], 0, given[k].shape[1]))
        if k == 1:
            tmp[0:3, :wq] = rows_sum(ztop, 4, 3)
            tmp[3:5, :wq] = rows_sum(zbot, 4, 2)
        else:
            prev_h = sizes[k - 1][0]
            tmp[0:3, :wq] = rows_sum(work[k - 1], OFF - 4, 3)
            tmp[3:6, :wq] = rows_sum(work[k - 1], OFF + prev_h - 4, 3)
        edge = cols_coarsen(tmp[0:8, :wq], sizes[k - 1][1], pick)
        row0, bottom = edge[1:2], edge[3:4]
        store(z, OFF, edge[1:3])
        store(z, OFF - 1, jnp.where(first, row0, edge[0:1]))
        store(z, OFF + h - 1, bottom)
        store(z, OFF + h, jnp.where(last, bottom, edge[4:5]))
        at = 4 * k
        if k == 1:
            store(z, OFF + h + 1, jnp.where(last, jnp.broadcast_to(bottom, (4, wp)), lo[at : at + 4, :wp]))
        else:
            store(z, OFF + h + 1, jnp.where(last, bottom, edge[5:6]))
            if k < LEVELS:
                store(z, OFF + h + 2, jnp.where(last, jnp.broadcast_to(bottom, (3, wp)), lo[at : at + 3, :wp]))
        if k < LEVELS:
            store(z, OFF - 4, jnp.where(first, jnp.broadcast_to(row0, (3, wp)), up[at + 1 : at + 4, :wp]))
        else:
            store(z, OFF - 2, jnp.where(first, row0, up[12:13, last_at:]))

    slope_sums, bend_sums = [], []

    def fold(v):
        total = v[:, 0:128]
        for at in range(128, v.shape[1], 128):
            total = total + v[:, at : at + 128]
        return total

    s_sum, b_sum = None, None
    for at in range(0, h0, 8):
        top, end = at == 0, at == h0 - 8
        upper = take(ztop, 7, 8) if top else x_ref[at - 1 : at + 7, :]
        middle = x_ref[at : at + 8, :]
        lower = take(zbot, 1, 8) if end else x_ref[at + 1 : at + 9, :]
        slope, bend = relief(upper, middle, lower, width0, 1.0)
        s0_ref[at : at + 8, :] = slope
        b0_ref[at : at + 8, :] = bend
        fs, fb = fold(slope), fold(bend * bend)
        s_sum = fs if top else s_sum + fs
        b_sum = fb if top else b_sum + fb
    slope_sums.append(s_sum)
    bend_sums.append(b_sum)
    for k, out in zip(range(1, LEVELS + 1), (f1, f2, f3, f4)):
        h, width = sizes[k]
        wp = up128(width)
        z = work[k]
        s_sum = b_sum = jnp.zeros((8, 128), f32)
        tiles = -(-(h + 2) // 8)
        for tile in range(tiles):
            at = OFF - 1 + 8 * tile
            slope, bend = relief(take(z, at - 1, 8), take(z, at, 8), take(z, at + 1, 8), width, float(2**k))
            row = row_of(slope) + (8 * tile - 1)
            kept = row <= h
            inner = (row >= 0) & (row < h) & (lane_of(slope) < width)
            s_sum = s_sum + fold(jnp.where(inner, slope, 0.0))
            b_sum = b_sum + fold(jnp.where(inner, bend * bend, 0.0))
            slope, bend = jnp.where(kept, slope, 0.0), jnp.where(kept, bend, 0.0)
            out[0, 8 * tile : 8 * tile + 8, :] = slope
            out[1, 8 * tile : 8 * tile + 8, :] = bend
        for field in range(2):
            if out.shape[1] > 8 * tiles:
                out[field, 8 * tiles :, :] = jnp.zeros((out.shape[1] - 8 * tiles, wp), f32)
            out[field, 0:1, :] = jnp.where(first, out[field, 1:2, :], out[field, 0:1, :])
            out[field, h + 1 : h + 2, :] = jnp.where(last, out[field, h : h + 1, :], out[field, h + 1 : h + 2, :])
        slope_sums.append(s_sum)
        bend_sums.append(b_sum)
    lane = lax.broadcasted_iota(jnp.int32, (1, 128), 1)
    line = jnp.zeros((1, 128), f32)
    for i, v in enumerate(slope_sums + bend_sums):
        total = jnp.sum(jnp.sum(v, axis=0, keepdims=True), axis=1, keepdims=True)
        line = jnp.where(lane == i, total, line)
    sum_ref[...] = jnp.broadcast_to(line.reshape(1, 1, 128), sum_ref.shape)


def hat(shape, factor, count, shift, along):
    fine = lax.broadcasted_iota(jnp.int32, shape, along).astype(f32)
    coarse = lax.broadcasted_iota(jnp.int32, shape, 1 - along).astype(f32)
    y = (fine + 0.5) * (1.0 / factor) - 0.5
    if count is not None:
        y = jnp.clip(y, 0.0, count - 1.0)
    return jnp.maximum(0.0, 1.0 - jnp.abs(y + shift - coarse)).astype(bf16)


def spread_kernel(sizes, f1, f2, f3, f4, u1, u2, u3, u4):
    h0, width0 = sizes[0]
    for k, f, u in zip(range(1, LEVELS + 1), (f1, f2, f3, f4), (u1, u2, u3, u4)):
        rows, wp = f.shape[1], f.shape[2]
        across = hat((wp, width0), 2**k, sizes[k][1], 0.0, 1)
        down = hat((h0, rows), 2**k, None, 1.0, 0)
        for field in range(2):
            hi, low = split2(f[field])
            wide = mm(hi, across) + mm(low, across)
            hi, low = split2(wide)
            u[field] = mm(down, hi) + mm(down, low)


def blend_kernel(cells, v_ref, s0, b0, u1, u2, u3, u4, slope_ref, bend_ref, slope_buf, bend_buf, sems):
    sums = jnp.sum(v_ref[...], axis=0)
    lane = lax.broadcasted_iota(jnp.int32, (1, 128), 1)
    count = jnp.ones((1, 128), f32)
    for k, c in enumerate(cells):
        count = jnp.where((lane == k) | (lane == k + LEVELS + 1), float(c), count)
    mean = sums / count
    scale = jnp.where(lane <= LEVELS, 1.0 / (mean + EPS), 1.0 / jnp.sqrt(mean + EPS))
    rows = slope_buf.shape[0]
    copies = []
    for field, (base, buf, out) in enumerate(((s0, slope_buf, slope_ref), (b0, bend_buf, bend_ref))):
        factors = [jnp.broadcast_to(scale[:, i : i + 1], (8, 128)) for i in range(field * (LEVELS + 1), (field + 1) * (LEVELS + 1))]
        for half in range(2):
            for at in range(half * rows // 2, (half + 1) * rows // 2, 8):
                for c in range(0, buf.shape[1], 128):
                    total = base[at : at + 8, c : c + 128] * factors[0]
                    for factor, u in zip(factors[1:], (u1, u2, u3, u4)):
                        total = total + u[field, at : at + 8, c : c + 128] * factor
                    buf[at : at + 8, c : c + 128] = total
            part = pl.ds(half * rows // 2, rows // 2)
            copy = pltpu.make_async_copy(buf.at[part], out.at[part], sems.at[2 * field + half])
            copy.start()
            copies.append(copy)
    for copy in copies:
        copy.wait()


def halo_pairs(count):
    both = lambda pairs: [(a, b) for a, b in pairs] + [(b, a) for a, b in pairs]
    even = [(i, i + 1) for i in range(0, count - 1, 2)]
    odd = [(i, i + 1) for i in range(1, count - 1, 2)]
    if count % 4 or count < 8:
        return both(even), both(odd), None, 0
    mid = count // 2
    second = [e for e in odd if e[0] != mid - 1] + [(0, mid), (mid - 1, count - 1)]
    third = [e for e in even if e[0] not in (mid - 2, mid)] + [(mid - 1, mid), (mid - 2, mid + 1)]
    return both(even), both(second), both(third), mid


VM = pl.BlockSpec(memory_space=pltpu.VMEM)
HBM = pl.BlockSpec(memory_space=pl.ANY)


def call(kernel, name, outs, scratch, out_specs=None, flops=0, limit=8 << 20):
    return lambda *args: pl.pallas_call(
        kernel,
        name=name,
        out_shape=[jax.ShapeDtypeStruct(s, f32) for s in outs],
        in_specs=[VM] * len(args),
        out_specs=out_specs or [VM] * len(outs),
        scratch_shapes=scratch,
        compiler_params=pltpu.CompilerParams(vmem_limit_bytes=limit),
        cost_estimate=pl.CostEstimate(flops=flops, bytes_accessed=1 << 19, transcendentals=0),
    )(*args)


def local(grid):
    h0, width0 = grid.shape
    count = lax.axis_size("rows")
    sizes = [(h0 >> k, width0 >> k) for k in range(LEVELS + 1)]
    rows8 = lambda n: -(-n // 8) * 8
    blocks = lambda rows, width: (up128(width) // 128, rows8(rows), 128)
    z_shapes = [blocks(h, w) for h, w in sizes[1:]]
    msg = (MSG_ROWS, width0)
    m1, m2, *zs = call(
        functools.partial(pyramid_kernel, sizes),
        "pyramid",
        [msg, msg] + z_shapes,
        [pltpu.VMEM(blocks(h0, width0), f32), pltpu.VMEM((rows8(h0 // 2), width0), f32)],
        flops=10**7,
    )(grid)
    pairs1, pairs2, pairs3, mid = halo_pairs(count)
    r2 = lax.ppermute(m2, "rows", pairs2)
    r3 = lax.ppermute(m2, "rows", pairs3) if mid else m2
    r1 = lax.ppermute(m1, "rows", pairs1)
    f_shapes = [(2, up16(h + 2), up128(w)) for h, w in sizes[1:]]
    s0, b0, f1, f2, f3, f4, sums = call(
        functools.partial(relief_kernel, sizes, mid),
        "relief",
        [grid.shape, grid.shape] + f_shapes + [(count, 1, 128)],
        [pltpu.VMEM(msg, f32)] * 2
        + [pltpu.VMEM(blocks(16, width0), f32)] * 2
        + [pltpu.VMEM(blocks(h + 16, w), f32) for h, w in sizes[1:]]
        + [pltpu.VMEM((8, width0), f32)],
        flops=2 * 10**7,
    )(grid, *zs, r1, r2, r3)
    seen = lax.all_to_all(sums, "rows", 0, 0, tiled=True)
    us = call(
        functools.partial(spread_kernel, sizes),
        "spread",
        [(2, h0, width0)] * LEVELS,
        [],
        flops=10**9,
        limit=16 << 20,
    )(f1, f2, f3, f4)
    cells = [count * h * w for h, w in sizes]
    return tuple(
        call(
            functools.partial(blend_kernel, cells),
            "blend",
            [grid.shape, grid.shape],
            [pltpu.VMEM(grid.shape, f32)] * 2 + [pltpu.SemaphoreType.DMA((4,))],
            out_specs=[HBM, HBM],
            flops=10**6,
        )(seen, s0, b0, *us)
    )


def solution(mesh):
    return jax.shard_map(
        local,
        mesh=mesh,
        in_specs=(P("rows", None),),
        out_specs=(P("rows", None), P("rows", None)),
        check_vma=False,
    )
```

time: 157 us -> 25.7 us (0.16)
  blocking collectives: 48.6 us -> 0 us
  local copies, waits for them, and re-layouts: 47.8 us -> 0.91 us
  starting transfers between devices: 32.1 us -> 9.38 us
  other arithmetic: 16.1 us -> 0 us
  between operations: 8.23 us -> 0.66 us
  Pallas kernels: 0 us -> 7.31 us
  waiting for transfers between devices: 3.38 us -> 7.3 us
    psum x1 -> x0, blocking collectives: 48.6 us -> none  [local(): slope_sums, square_sums = lax.psum((local_first, local_second), 'rows')]
    slice x77 -> x0, local copies, waits for them, and re-layouts: 33.2 us -> none  [the longest x40 28.3 us: coarsen_axis(): piece = lax.slice_in_dim(padded, offset, offset + length, 2, axis)]
    ppermute x10 -> x3, starting transfers between devices: 32.1 us -> 6.53 us  [the longest x1 5.99 us: local(): r2 = lax.ppermute(m2, 'rows', pairs2)]
    another operation x11 -> x0, local copies, waits for them, and re-layouts: 8.21 us -> none  [the longest x1 3.26 us: local(): local_first = jnp.stack([jnp.sum(part[1:-1]) for part in slope_parts])]
    pallas_call x0 -> x4, Pallas kernels: none -> 7.31 us  [call(): pl.pallas_call(kernel, name=name, out_shape=[jax.ShapeDtypeStruct(s, f32)...]
    all_to_all x0 -> x1, waiting for transfers between devices: none -> 4.89 us  [local(): seen = lax.all_to_all(sums, 'rows', 0, 0, tiled=True)]
    add x16 -> x0, other arithmetic: 4.72 us -> none  [the longest x7 3.24 us: refine_axis(): pieces.append((1.0 - fraction) * lower_side + fraction * upper_side)]
    another operation x19 -> x0, other arithmetic: 4.56 us -> none  [the longest x15 3.15 us: refine_axis(): stacked = jnp.stack(pieces, axis + 1)]
  transfers between devices with their start and end apart: 10 -> 4, of which waited for: 3 -> 2; matrix products, arithmetic and copies ran while one was open for 6% -> 0% of each run, Pallas kernels for 0% -> 9%
where the time goes in v1:
time: 25.7 us; the launch traced here: 25.5 us
  starting transfers between devices  9.38 us (36%)
  Pallas kernels  7.31 us (28%)
  waiting for transfers between devices  7.3 us (28%)
  local copies, waits for them, and re-layouts  0.91 us (4%)
  between operations  0.66 us (3%)
    pallas_call x4, Pallas kernels, call(): pl.pallas_call(kernel, name=name, out_shape=[jax.ShapeDtypeStruct(s, f32)...  7.31 us
    ppermute x1, starting transfers between devices, local(): r2 = lax.ppermute(m2, 'rows', pairs2)  5.99 us
    all_to_all x1, waiting for transfers between devices, local(): seen = lax.all_to_all(sums, 'rows', 0, 0, tiled=True)  4.89 us
    all_to_all x1, starting transfers between devices, local(): seen = lax.all_to_all(sums, 'rows', 0, 0, tiled=True)  2.85 us
    ppermute x1, waiting for transfers between devices, local(): r2 = lax.ppermute(m2, 'rows', pairs2)  2.41 us
    unnamed x2, local copies, waits for them, and re-layouts  0.91 us
  transfers between devices with their start and end apart: 4, of which 2 were waited for; matrix products, arithmetic and copies ran while one was open for 0% of the time, Pallas kernels for 9%

profile of v1, /device:TPU:0, one launch (start us, length us, event | category | flops | bytes accessed | tf_op | source)
XLA Modules:
  0.0 25.5 jit_solution(10374642380058451935)
XLA Ops:
  0.6 0.0 copy-start
  0.6 0.9 %copy-done = f32[64,640]{1,0:T(8,128)S(1)} copy-done((f32[64,640]{1,0:T(8,128)S(1)}, f32[64,640]{1,0:T(8,128)}, u32[]{:S(2)}) %copy-start) | copy-done | bytes 163864
  1.5 1.4 %pyramid.1 = (f32[16,640]{1,0:T(8,128)S(1)}, f32[16,640]{1,0:T(8,128)S(1)}, f32[3,32,128]{2,1,0:T(8,128)S(1)}, f32[2,16,128]{2,1,0:T(8,128)S(1)}, f32[1,8,128]{2,1,0:T(8,128)S(1)}, /*index=5*/f32[1,8,128]{2,1,0:T(8,128)S(1)}) custom-call(f32[64,640]{1,0:T(8,128)S(1)} %copy-done), custom_call_target="tpu_custom_call" | custom-call | flops 10000000 | bytes 524288 | tf_op jit(solution)/shard_map/pyramid/pallas_call | solution.py:342
  2.9 0.5 %collective-permute-start = (f32[16,640]{1,0:T(8,128)S(1)}, f32[16,640]{1,0:T(8,128)S(1)}, u32[]{:S(2)}, u32[]{:S(2)}) collective-permute-start(f32[16,640]{1,0:T(8,128)S(1)} %get-tuple-element.23), channel_id=1, source_target_pairs={{0,1},{2,3},{4,5},{6,7},{8,9},{10,11},{12,13},{14,15},{16,17},{18,... | collective-permute-start | bytes 122888 | tf_op jit(solution)/shard_map/ppermute | solution.py:372
  3.4 0.0 collective-permute-start.2
  3.4 6.0 %collective-permute-start.1 = (f32[16,640]{1,0:T(8,128)S(1)}, f32[16,640]{1,0:T(8,128)S(1)}, u32[]{:S(2)}, u32[]{:S(2)}) collective-permute-start(f32[16,640]{1,0:T(8,128)S(1)} %get-tuple-element.24), channel_id=1, source_target_pairs={{1,2},{3,4},{5,6},{7,8},{9,10},{11,12},{13,14},{17,18},{19,20},{21... | collective-permute-start | bytes 122888 | tf_op jit(solution)/shard_map/ppermute | solution.py:370
  9.4 0.0 collective-permute-done.r1_ref
  9.4 0.0 collective-permute-done.2.r3_ref
  9.4 2.4 %collective-permute-done.1.r2_ref = f32[16,640]{1,0:T(8,128)S(1)} collective-permute-done((f32[16,640]{1,0:T(8,128)S(1)}, f32[16,640]{1,0:T(8,128)S(1)}, u32[]{:S(2)}, u32[]{:S(2)}) %collective-permute-start.1) | collective-permute-done | bytes 40992 | tf_op jit(solution)/shard_map/ppermute | solution.py:370
  11.8 2.8 %relief.1 = (f32[64,640]{1,0:T(8,128)S(1)}, f32[64,640]{1,0:T(8,128)S(1)}, f32[2,48,384]{2,1,0:T(8,128)S(1)}, f32[2,32,256]{2,1,0:T(8,128)S(1)}, f32[2,16,128]{2...) custom-call(f32[64,640]{1,0:T(8,128)S(1)} %copy-done, f32[3,32,128]{2,1,0:T(8,128)S(1)} %get-tuple-element.19.z1, ...), custom_call_target="tpu_custom_call" | custom-call | flops 20000000 | bytes 524288 | tf_op jit(solution)/shard_map/relief/pallas_call | solution.py:342
  14.7 2.9 %all-to-all-start = ((f32[32,1,128]{2,1,0:T(1,128)}), f32[32,1,128]{2,1,0:T(1,128)S(1)}, u32[]{:S(2)}, u32[]{:S(2)}) async-start(f32[32,1,128]{2,1,0:T(1,128)} %get-tuple-element.25), calls=%async_computation | async-start | bytes 32768 | tf_op jit(solution)/shard_map/all_to_all | solution.py:384
  17.5 2.2 %spread.1 = (f32[2,64,640]{2,1,0:T(8,128)S(1)}, f32[2,64,640]{2,1,0:T(8,128)S(1)}, f32[2,64,640]{2,1,0:T(8,128)S(1)}, f32[2,64,640]{2,1,0:T(8,128)S(1)}) custom-call(f32[2,48,384]{2,1,0:T(8,128)S(1)} %get-tuple-element.28.f1, f32[2,32,256]{2,1,0:T(8,128)S(1)} %get-tuple-element.29.f2, f32[2,16,128]{2,1,0:T(8,128)S(1)} %get-tuple-element.30.f3, ...), custom_call_target="tpu_custom_call" | custom-call | flops 1000000000 | bytes 524288 | tf_op jit(solution)/shard_map/spread/pallas_call | solution.py:342
  19.7 4.9 %all-to-all-done.v_ref = f32[32,1,128]{2,1,0:T(1,128)S(1)} async-done(((f32[32,1,128]{2,1,0:T(1,128)}), f32[32,1,128]{2,1,0:T(1,128)S(1)}, u32[]{:S(2)}, u32[]{:S(2)}) %all-to-all-start) | async-done | bytes 16416 | tf_op jit(solution)/shard_map/all_to_all | solution.py:384
  24.6 0.9 %blend.1 = (f32[64,640]{1,0:T(8,128)}, f32[64,640]{1,0:T(8,128)}) custom-call(f32[32,1,128]{2,1,0:T(1,128)S(1)} %all-to-all-done.v_ref, f32[64,640]{1,0:T(8,128)S(1)} %get-tuple-element.26.s0, f32[64,640]{1,0:T(8,128)S(1)} %get-tuple-element.27.b0, f32[2,64,640]{2,1,0:T(8,128)S(1)} %get-tuple-element.32.u1, f32[2,64,640]{2,1,0:T(8,128)S(1)} %get-tuple-element.33.u2, ...), custom_call_target="tpu_custom_call" | custom-call | flops 1000000 | bytes 524288 | tf_op jit(solution)/shard_map/blend/pallas_call | solution.py:342
Async XLA Ops:
  0.6 0.9 %copy-start = (f32[64,640]{1,0:T(8,128)S(1)}, f32[64,640]{1,0:T(8,128)}, u32[]{:S(2)}) copy-start(f32[64,640]{1,0:T(8,128)} %x_ref.3) | copy-start | bytes 491524
  2.9 6.5 %collective-permute-start = (f32[16,640]{1,0:T(8,128)S(1)}, f32[16,640]{1,0:T(8,128)S(1)}, u32[]{:S(2)}, u32[]{:S(2)}) collective-permute-start(f32[16,640]{1,0:T(8,128)S(1)} %get-tuple-element.23), channel_id=1, source_target_pairs={{0,1},{2,3},{4,5},{6,7},{8,9},{10,11},{12,13},{14,15},{16,17},{18,... | collective-permute-start | bytes 122888 | tf_op jit(solution)/shard_map/ppermute | solution.py:372
  3.4 6.0 %collective-permute-start.2 = (f32[16,640]{1,0:T(8,128)S(1)}, f32[16,640]{1,0:T(8,128)S(1)}, u32[]{:S(2)}, u32[]{:S(2)}) collective-permute-start(f32[16,640]{1,0:T(8,128)S(1)} %get-tuple-element.24), channel_id=1, source_target_pairs={{0,1},{2,3},{4,5},{6,7},{8,9},{10,11},{12,13},{18,19},{20,21},{22,... | collective-permute-start | bytes 122888 | tf_op jit(solution)/shard_map/ppermute | solution.py:371
  3.4 8.4 %collective-permute-start.1 = (f32[16,640]{1,0:T(8,128)S(1)}, f32[16,640]{1,0:T(8,128)S(1)}, u32[]{:S(2)}, u32[]{:S(2)}) collective-permute-start(f32[16,640]{1,0:T(8,128)S(1)} %get-tuple-element.24), channel_id=1, source_target_pairs={{1,2},{3,4},{5,6},{7,8},{9,10},{11,12},{13,14},{17,18},{19,20},{21... | collective-permute-start | bytes 122888 | tf_op jit(solution)/shard_map/ppermute | solution.py:370
  14.7 10.0 %all-to-all-start = ((f32[32,1,128]{2,1,0:T(1,128)}), f32[32,1,128]{2,1,0:T(1,128)S(1)}, u32[]{:S(2)}, u32[]{:S(2)}) async-start(f32[32,1,128]{2,1,0:T(1,128)} %get-tuple-element.25), calls=%async_computation | async-start | bytes 32768 | tf_op jit(solution)/shard_map/all_to_all | solution.py:384

commit v2 on v1

v2 whole, which is shorter than its diff:
```python
import functools

import jax
import jax.numpy as jnp
from jax import lax
from jax.experimental import pallas as pl
from jax.experimental.pallas import tpu as pltpu
from jax.sharding import PartitionSpec as P

LEVELS = 4
EPS = 1e-06
f32 = jnp.float32
bf16 = jnp.bfloat16
ATAN = (
    1.0,
    -0.3333314528,
    0.1999355085,
    -0.1420889944,
    0.1065626393,
    -0.0752896400,
    0.0429096138,
    -0.0161657367,
    0.0028662257,
)


def up128(n):
    return -(-n // 128) * 128


def up16(n):
    return -(-n // 16) * 16


def lane_of(v):
    return lax.broadcasted_iota(jnp.int32, v.shape, 1)


def row_of(v):
    return lax.broadcasted_iota(jnp.int32, v.shape, 0)


def west(v):
    return jnp.where(lane_of(v) == 0, v, pltpu.roll(v, 1, 1))


def east(v, width):
    return jnp.where(lane_of(v) == width - 1, v, pltpu.roll(v, v.shape[1] - 1, 1))


def split3(v):
    hi = v.astype(bf16)
    rest = v - hi.astype(f32)
    mid = rest.astype(bf16)
    low = (rest - mid.astype(f32)).astype(bf16)
    return hi, mid, low


def split2(v):
    hi = v.astype(bf16)
    return hi, (v - hi.astype(f32)).astype(bf16)


def mm(a, b):
    return jnp.dot(a, b, preferred_element_type=f32)


def picker():
    rows = lax.broadcasted_iota(jnp.int32, (256, 128), 0)
    cols = lax.broadcasted_iota(jnp.int32, (256, 128), 1)
    return (rows == 2 * cols).astype(f32).astype(bf16)


def take(ref, at, count):
    return jnp.concatenate([ref[c, at : at + count, :] for c in range(ref.shape[0])], axis=1)


def store(ref, at, v):
    for c in range(ref.shape[0]):
        ref[c, at : at + v.shape[0], :] = v[:, 128 * c : 128 * c + 128]


def rows_sum(ref, start, count):
    out = []
    for c in range(ref.shape[0]):
        part = [ref[c, pl.ds(start + a, count, 2), :] for a in range(5)]
        out.append((part[0] + part[4]) * 0.0625 + (part[1] + part[3]) * 0.25 + part[2] * 0.375)
    return jnp.concatenate(out, axis=1)


def cols_coarsen(v, width, pick):
    w1 = west(v)
    e1 = east(v, width)
    y = (west(w1) + east(e1, width)) * 0.0625 + (w1 + e1) * 0.25 + v * 0.375
    out = []
    for at in range(0, v.shape[1], 256):
        part = y[:, at : at + 256]
        sel = pick[: part.shape[1]]
        hi, mid, low = split3(part)
        out.append(mm(hi, sel) + (mm(mid, sel) + mm(low, sel)))
    return out[0] if len(out) == 1 else jnp.concatenate(out, axis=1)


def pyramid_kernel(sizes, x_ref, m1_ref, m2_ref, z0, z1, z2, tmp, sems):
    copies = [
        pltpu.make_async_copy(x_ref.at[:, pl.ds(128 * c, 128)], z0.at[c], sems.at[c]) for c in range(z0.shape[0])
    ]
    for copy in copies:
        copy.start()
    pick = picker()
    odd = lax.rem(lax.axis_index("rows"), 2) == 1
    h = sizes[0][0]
    for copy in copies:
        copy.wait()

    def put(row, z, top_at, bottom_at, count):
        for c in range(z.shape[0]):
            top, bottom = z[c, top_at : top_at + count, :], z[c, bottom_at : bottom_at + count, :]
            m1_ref[row : row + count, :] = jnp.where(odd, top, bottom)
            m2_ref[row : row + count, :] = jnp.where(odd, bottom, top)
            row += count
        return row

    row = put(0, z0, 0, h - 4, 4)
    for k, z in ((0, z1), (1, z2)):
        half, wp = sizes[k + 1][0], up128(sizes[k][1])
        low = k + 1
        tmp[low : half - 1, :wp] = rows_sum((z0, z1)[k], 2 * low - 2, half - 1 - low)
        store(z, 0, cols_coarsen(tmp[0:half, :wp], sizes[k][1], pick))
    row = put(row, z1, 1, sizes[1][0] - 5, 4)
    put(row, z2, 0, 0, sizes[2][0])


def relief(upper, middle, lower, width, spacing):
    diff = lower - upper
    ends = lower + upper
    tall = ends + 2.0 * middle
    m_e, m_w = east(middle, width), west(middle)
    d_e, d_w = east(diff, width), west(diff)
    p = (east(tall, width) - west(tall)) * (1.0 / (8.0 * spacing))
    q = (d_e + d_w + 2.0 * diff) * (1.0 / (8.0 * spacing))
    inv = 1.0 / (spacing * spacing)
    r = ((m_e - middle) - (middle - m_w)) * inv
    t = ((lower - middle) - (middle - upper)) * inv
    u = (d_e - d_w) * (0.25 * inv)
    pp, qq = p * p, q * q
    steep = pp + qq
    base = 1.0 + steep
    root = jnp.sqrt(base)
    y = jnp.sqrt(steep) / (1.0 + root)
    y2 = y * y
    acc = ATAN[-1]
    for c in ATAN[-2::-1]:
        acc = acc * y2 + c
    slope = 2.0 * y * acc
    bend = -(pp * r + 2.0 * (p * q) * u + qq * t) / (base * root)
    return slope, bend


def fold(v):
    total = None
    for row in range(0, v.shape[0], 8):
        for at in range(0, v.shape[1], 128):
            part = v[row : row + 8, at : at + 128]
            total = part if total is None else total + part
    return total


def inner_kernel(sizes, z0, z1, z2, s0_ref, b0_ref, f1, f2, acc_ref):
    for k, z in enumerate((z0, z1, z2)):
        h, width = sizes[k]
        s_sum = b_sum = None
        for at in range(0, h, 8):
            middle = take(z, at, 8)
            upper = take(z, at - 1, 8) if at else pltpu.roll(middle, 1, 0)
            lower = take(z, at + 1, 8) if at < h - 8 else pltpu.roll(middle, 7, 0)
            slope, bend = relief(upper, middle, lower, width, float(2**k))
            if k == 0:
                s0_ref[at : at + 8, :] = slope
                b0_ref[at : at + 8, :] = bend
            else:
                f = (f1, f2)[k - 1]
                f[0, at + 1 : at + 9, :] = slope
                f[1, at + 1 : at + 9, :] = bend
            skip = 3 if k else 1
            if at == 0 or at == h - 8 or width % 128:
                row = row_of(slope) + at
                kept = (row >= skip) & (row < h - skip) & (lane_of(slope) < width)
                slope, bend = jnp.where(kept, slope, 0.0), jnp.where(kept, bend, 0.0)
            fs, fb = fold(slope), fold(bend * bend)
            s_sum = fs if at == 0 else s_sum + fs
            b_sum = fb if at == 0 else b_sum + fb
        acc_ref[k] = s_sum
        acc_ref[LEVELS + 1 + k] = b_sum
        if k:
            f = (f1, f2)[k - 1]
            for field in range(2):
                f[field, h + 2 :, :] = jnp.zeros((f.shape[1] - h - 2, f.shape[2]), f32)
    for k in range(3, LEVELS + 1):
        acc_ref[k] = jnp.zeros((8, 128), f32)
        acc_ref[LEVELS + 1 + k] = jnp.zeros((8, 128), f32)


def edge_kernel(sizes, mid, z0, z1, z2, r1_ref, r2_ref, r3_ref, acc_ref, s0_in, b0_in, f1_in, f2_in,
                s0_ref, b0_ref, f1, f2, f3, f4, sum_ref, up, lo, t0, e0, t1, e1, w2, w3, w4, tmp):
    me = lax.axis_index("rows")
    odd = lax.rem(me, 2) == 1
    first, last = me == 0, me == lax.axis_size("rows") - 1
    r1, r2 = r1_ref[...], r2_ref[...]
    if mid:
        r2 = jnp.where((me == mid) | (me == mid - 1), r3_ref[...], r2)
    up[...] = jnp.where(odd, r1, r2)
    lo[...] = jnp.where(odd, r2, r1)
    pick = picker()

    h0, width0 = sizes[0]
    for c in range(z0.shape[0]):
        t0[c, 8:16, :] = z0[c, 0:8, :]
        t0[c, 4:8, :] = jnp.where(first, jnp.broadcast_to(z0[c, 0:1, :], (4, 128)), up[4 * c : 4 * c + 4, :])
        e0[c, 8:16, :] = z0[c, h0 - 8 : h0, :]
        e0[c, 16:20, :] = jnp.where(last, jnp.broadcast_to(z0[c, h0 - 1 : h0, :], (4, 128)), lo[4 * c : 4 * c + 4, :])
    base = 4 * z0.shape[0]
    h1, width1 = sizes[1]
    tmp[0:3, :] = rows_sum(t0, 4, 3)
    tmp[3:5, :] = rows_sum(e0, 12, 2)
    edge = cols_coarsen(tmp[...], width0, pick)
    for c in range(z1.shape[0]):
        part = edge[:, 128 * c : 128 * c + 128]
        row0, end = part[1:2], part[3:4]
        t1[c, 8:16, :] = z1[c, 0:8, :]
        t1[c, 8:9, :] = row0
        t1[c, 7:8, :] = jnp.where(first, row0, part[0:1])
        t1[c, 4:7, :] = jnp.where(first, jnp.broadcast_to(row0, (3, 128)), up[base + 4 * c + 1 : base + 4 * c + 4, :])
        e1[c, 8:16, :] = z1[c, h1 - 8 : h1, :]
        e1[c, 15:16, :] = end
        e1[c, 16:17, :] = jnp.where(last, end, part[4:5])
        e1[c, 17:21, :] = jnp.where(last, jnp.broadcast_to(end, (4, 128)), lo[base + 4 * c : base + 4 * c + 4, :])
    base += 4 * z1.shape[0]
    h2, width2 = sizes[2]
    wq = up128(width1)
    tmp[0:3, :wq] = rows_sum(t1, 4, 3)
    tmp[3:6, :wq] = rows_sum(e1, 12, 3)
    edge = cols_coarsen(tmp[:, :wq], width1, pick)
    for c in range(z2.shape[0]):
        part = edge[:, 128 * c : 128 * c + 128]
        row0, end = part[1:2], part[3:4]
        at = base + h2 * c
        w2[c, 0:h2, :] = jnp.where(first, jnp.broadcast_to(row0, (h2, 128)), up[at : at + h2, :])
        w2[c, h2 : 2 * h2, :] = z2[c]
        w2[c, 2 * h2 : 3 * h2, :] = jnp.where(last, jnp.broadcast_to(end, (h2, 128)), lo[at : at + h2, :])
        w2[c, h2 - 1 : h2, :] = jnp.where(first, row0, part[0:1])
        w2[c, h2 : h2 + 2, :] = part[1:3]
        w2[c, 2 * h2 - 1 : 2 * h2, :] = end
        w2[c, 2 * h2 : 2 * h2 + 1, :] = jnp.where(last, end, part[4:5])
        w2[c, 2 * h2 + 1 : 2 * h2 + 2, :] = jnp.where(last, end, part[5:6])
    h3, width3 = sizes[3]
    wq = up128(width2)
    v = cols_coarsen(pad_rows(rows_sum(w2, h2 - 14, h3 + 11)), width2, pick)
    row = row_of(v) - 6
    v = jnp.where(first & (row < 0), v[6:7], jnp.where(last & (row >= h3), v[h3 + 5 : h3 + 6], v))
    w3[0] = v
    h4, width4 = sizes[4]
    v = cols_coarsen(pad_rows(rows_sum(w3, 0, h4 + 4)), width3, pick)
    row = row_of(v) - 2
    v = jnp.where(first & (row < 0), v[2:3], jnp.where(last & (row >= h4), v[h4 + 1 : h4 + 2], v))
    w4[0, 0:8, :] = v
    w4[0, 8:16, :] = v

    totals = []

    def add(k, slope, bend, kept):
        kept = kept & (lane_of(slope) < sizes[k][1])
        totals.append((acc_ref[k] + fold(jnp.where(kept, slope, 0.0)),
                       acc_ref[LEVELS + 1 + k] + fold(jnp.where(kept, bend * bend, 0.0))))

    def ends(top, top_at, bottom, bottom_at):
        a, b = take(top, top_at, 8), take(bottom, bottom_at - 4, 8)
        return jnp.where(row_of(a) < 4, a, b)

    slope, bend = relief(*(ends(t0, 7 + i, e0, 11 + i) for i in range(3)), width0, 1.0)
    for ref, v in ((s0_ref, slope), (b0_ref, bend)):
        ref[0:4, :] = v[0:4]
        ref[h0 - 4 : h0, :] = v[4:8]
    add(0, slope, bend, (row_of(slope) == 0) | (row_of(slope) == 7))
    for k, top, bottom, top_at, bottom_at, f in ((1, t1, e1, 7, 13, f1), (2, w2, w2, h2 - 1, 2 * h2 - 3, f2)):
        h, width = sizes[k]
        slope, bend = relief(*(ends(top, top_at - 1 + i, bottom, bottom_at - 1 + i) for i in range(3)), width, float(2**k))
        add(k, slope, bend, (row_of(slope) > 0) & (row_of(slope) < 7))
        for field, v in enumerate((slope, bend)):
            row = row_of(v)
            v = jnp.where(first & (row == 0), v[1:2], jnp.where(last & (row == 7), v[6:7], v))
            f[field, 0:4, :] = v[0:4]
            f[field, h - 2 : h + 2, :] = v[4:8]
    for k, z, at, f in ((3, w3, 5, f3), (4, w4, 1, f4)):
        h, width = sizes[k]
        rows = -(-(h + 2) // 8) * 8
        slope, bend = relief(take(z, at - 1, rows), take(z, at, rows), take(z, at + 1, rows), width, float(2**k))
        row = row_of(slope) - 1
        add(k, slope, bend, (row >= 0) & (row < h))
        for field, v in enumerate((slope, bend)):
            v = jnp.where(first & (row < 0), v[1:2], jnp.where(last & (row >= h), v[h : h + 1], v))
            f[field, 0:rows, :] = jnp.where(row <= h, v, 0.0)
            if rows < f.shape[1]:
                f[field, rows:, :] = jnp.zeros((f.shape[1] - rows, f.shape[2]), f32)
    table = jnp.zeros((16, 128), f32)
    table_row = row_of(table)
    for i, v in enumerate([t[0] for t in totals] + [t[1] for t in totals]):
        table = jnp.where(table_row == i, jnp.sum(v, axis=0, keepdims=True), table)
    table = jnp.where(table_row == lane_of(table), jnp.sum(table, axis=1, keepdims=True), 0.0)
    line = jnp.sum(table, axis=0, keepdims=True)
    sum_ref[...] = jnp.broadcast_to(line.reshape(1, 1, 128), sum_ref.shape)


def pad_rows(v):
    short = -v.shape[0] % 8
    return jnp.concatenate([v, jnp.zeros((short, v.shape[1]), f32)], axis=0) if short else v


def hat(shape, factor, count, shift, along):
    fine = lax.broadcasted_iota(jnp.int32, shape, along).astype(f32)
    coarse = lax.broadcasted_iota(jnp.int32, shape, 1 - along).astype(f32)
    y = (fine + 0.5) * (1.0 / factor) - 0.5
    if count is not None:
        y = jnp.clip(y, 0.0, count - 1.0)
    return jnp.maximum(0.0, 1.0 - jnp.abs(y + shift - coarse)).astype(bf16)


def spread_kernel(sizes, f1, f2, f3, f4, u1, u2, u3, u4):
    h0, width0 = sizes[0]
    for k, f, u in zip(range(1, LEVELS + 1), (f1, f2, f3, f4), (u1, u2, u3, u4)):
        rows, wp = f.shape[1], f.shape[2]
        across = hat((wp, width0), 2**k, sizes[k][1], 0.0, 1)
        down = hat((h0, rows), 2**k, None, 1.0, 0)
        for field in range(2):
            hi, low = split2(f[field])
            wide = mm(hi, across) + mm(low, across)
            hi, low = split2(wide)
            u[field] = mm(down, hi) + mm(down, low)


def blend_kernel(cells, v_ref, s0, b0, u1, u2, u3, u4, slope_ref, bend_ref, slope_buf, bend_buf, sems):
    sums = jnp.sum(v_ref[...], axis=0)
    lane = lax.broadcasted_iota(jnp.int32, (1, 128), 1)
    count = jnp.ones((1, 128), f32)
    for k, c in enumerate(cells):
        count = jnp.where((lane == k) | (lane == k + LEVELS + 1), float(c), count)
    mean = sums / count
    scale = jnp.where(lane <= LEVELS, 1.0 / (mean + EPS), 1.0 / jnp.sqrt(mean + EPS))
    rows = slope_buf.shape[0]
    copies = []
    for field, (base, buf, out) in enumerate(((s0, slope_buf, slope_ref), (b0, bend_buf, bend_ref))):
        factors = [jnp.broadcast_to(scale[:, i : i + 1], (8, 128)) for i in range(field * (LEVELS + 1), (field + 1) * (LEVELS + 1))]
        for half in range(2):
            for at in range(half * rows // 2, (half + 1) * rows // 2, 8):
                for c in range(0, buf.shape[1], 128):
                    total = base[at : at + 8, c : c + 128] * factors[0]
                    for factor, u in zip(factors[1:], (u1, u2, u3, u4)):
                        total = total + u[field, at : at + 8, c : c + 128] * factor
                    buf[at : at + 8, c : c + 128] = total
            part = pl.ds(half * rows // 2, rows // 2)
            copy = pltpu.make_async_copy(buf.at[part], out.at[part], sems.at[2 * field + half])
            copy.start()
            copies.append(copy)
    for copy in copies:
        copy.wait()


def halo_pairs(count):
    both = lambda pairs: [(a, b) for a, b in pairs] + [(b, a) for a, b in pairs]
    even = [(i, i + 1) for i in range(0, count - 1, 2)]
    odd = [(i, i + 1) for i in range(1, count - 1, 2)]
    if count % 4 or count < 8:
        return both(even), both(odd), None, 0
    mid = count // 2
    second = [e for e in odd if e[0] != mid - 1] + [(0, mid), (mid - 1, count - 1)]
    third = [e for e in even if e[0] not in (mid - 2, mid)] + [(mid - 1, mid), (mid - 2, mid + 1)]
    return both(even), both(second), both(third), mid


VM = pl.BlockSpec(memory_space=pltpu.VMEM)
ANY = pl.BlockSpec(memory_space=pl.ANY)


def call(kernel, name, outs, scratch=(), in_specs=None, out_specs=None, flops=10**6, limit=8 << 20, aliases=None):
    return lambda *args: pl.pallas_call(
        kernel,
        name=name,
        out_shape=[jax.ShapeDtypeStruct(s, f32) for s in outs],
        in_specs=in_specs or [VM] * len(args),
        out_specs=out_specs or [VM] * len(outs),
        scratch_shapes=list(scratch),
        input_output_aliases=aliases or {},
        compiler_params=pltpu.CompilerParams(vmem_limit_bytes=limit),
        cost_estimate=pl.CostEstimate(flops=flops, bytes_accessed=1 << 19, transcendentals=0),
    )(*args)


def local(grid):
    h0, width0 = grid.shape
    count = lax.axis_size("rows")
    sizes = [(h0 >> k, width0 >> k) for k in range(LEVELS + 1)]

    def blocks(rows, width):
        return (up128(width) // 128, -(-rows // 8) * 8, 128)

    z_shapes = [blocks(*size) for size in sizes]
    msg = (4 * z_shapes[0][0] + 4 * z_shapes[1][0] + sizes[2][0] * z_shapes[2][0], 128)
    m1, m2, z0, z1, z2 = call(
        functools.partial(pyramid_kernel, sizes),
        "pyramid",
        [msg, msg] + z_shapes[:3],
        [pltpu.VMEM((h0 // 2, width0), f32), pltpu.SemaphoreType.DMA((z_shapes[0][0],))],
        in_specs=[pl.BlockSpec(memory_space=pltpu.HBM)],
    )(pltpu.with_memory_space_constraint(grid, pltpu.HBM))
    pairs1, pairs2, pairs3, mid = halo_pairs(count)
    r2 = lax.ppermute(m2, "rows", pairs2)
    r3 = lax.ppermute(m2, "rows", pairs3) if mid else m2
    r1 = lax.ppermute(m1, "rows", pairs1)
    f_shapes = [(2, up16(h + 2), up128(w)) for h, w in sizes[1:]]
    acc = (2 * LEVELS + 2, 8, 128)
    s0, b0, f1, f2, sums = call(
        functools.partial(inner_kernel, sizes),
        "inner",
        [grid.shape, grid.shape] + f_shapes[:2] + [acc],
        flops=10**8,
    )(z0, z1, z2)
    s0, b0, f1, f2, f3, f4, sums = call(
        functools.partial(edge_kernel, sizes, mid),
        "edge",
        [grid.shape, grid.shape] + f_shapes + [(count, 1, 128)],
        [pltpu.VMEM(msg, f32)] * 2
        + [pltpu.VMEM(blocks(rows, sizes[k][1]), f32) for k in range(2) for rows in (24, 24)]
        + [pltpu.VMEM(blocks(3 * sizes[2][0], sizes[2][1]), f32)]
        + [pltpu.VMEM(blocks(sizes[3][0] + 16, sizes[3][1]), f32)]
        + [pltpu.VMEM(blocks(16, sizes[4][1]), f32), pltpu.VMEM((8, width0), f32)],
        aliases={7: 0, 8: 1, 9: 2, 10: 3},
    )(z0, z1, z2, r1, r2, r3, sums, s0, b0, f1, f2)
    sums = pltpu.with_memory_space_constraint(sums, pltpu.VMEM)
    seen = lax.all_to_all(sums, "rows", 0, 0, tiled=True)
    us = call(
        functools.partial(spread_kernel, sizes),
        "spread",
        [(2, h0, width0)] * LEVELS,
        flops=10**9,
        limit=16 << 20,
    )(f1, f2, f3, f4)
    cells = [count * h * w for h, w in sizes]
    return tuple(
        call(
            functools.partial(blend_kernel, cells),
            "blend",
            [grid.shape, grid.shape],
            [pltpu.VMEM(grid.shape, f32)] * 2 + [pltpu.SemaphoreType.DMA((4,))],
            out_specs=[ANY, ANY],
        )(seen, s0, b0, *us)
    )


def solution(mesh):
    return jax.shard_map(
        local,
        mesh=mesh,
        in_specs=(P("rows", None),),
        out_specs=(P("rows", None), P("rows", None)),
        check_vma=False,
    )
```

time: 25.7 us -> 24.4 us (0.949)
  waiting for transfers between devices: 7.3 us -> 6.38 us
  local copies, waits for them, and re-layouts: 0.91 us -> 0 us
  Pallas kernels: 7.31 us -> 7.62 us
    ppermute x1, waiting for transfers between devices: 2.41 us -> 1.49 us  [local(): r2 = lax.ppermute(m2, 'rows', pairs2)]
    unnamed x2 -> x0, local copies, waits for them, and re-layouts: 0.91 us -> none
    pallas_call x4 -> x5, Pallas kernels: 7.31 us -> 7.62 us  [call(): pl.pallas_call(kernel, name=name, out_shape=[jax.ShapeDtypeStruct(s, f32)...]
  transfers between devices with their start and end apart: 4 -> 4, of which waited for: 2 -> 2; matrix products, arithmetic and copies ran while one was open for 0% -> 0% of each run, Pallas kernels for 9% -> 12%
where the time goes in v2:
time: 24.4 us; the launch traced here: 24.2 us
  starting transfers between devices  9.52 us (39%)
  Pallas kernels  7.62 us (31%)
  waiting for transfers between devices  6.38 us (26%)
  between operations  0.68 us (3%)
    pallas_call x5, Pallas kernels, call(): pl.pallas_call(kernel, name=name, out_shape=[jax.ShapeDtypeStruct(s, f32)...  7.62 us
    ppermute x1, starting transfers between devices, local(): r2 = lax.ppermute(m2, 'rows', pairs2)  5.94 us
    all_to_all x1, waiting for transfers between devices, local(): seen = lax.all_to_all(sums, 'rows', 0, 0, tiled=True)  4.89 us
    all_to_all x1, starting transfers between devices, local(): seen = lax.all_to_all(sums, 'rows', 0, 0, tiled=True)  2.94 us
    ppermute x1, waiting for transfers between devices, local(): r2 = lax.ppermute(m2, 'rows', pairs2)  1.49 us
    ppermute x1, starting transfers between devices, local(): r1 = lax.ppermute(m1, 'rows', pairs1)  0.56 us
  transfers between devices with their start and end apart: 4, of which 2 were waited for; matrix products, arithmetic and copies ran while one was open for 0% of the time, Pallas kernels for 12%

profile of v2, /device:TPU:0, one launch (start us, length us, event | category | flops | bytes accessed | tf_op | source)
XLA Modules:
  0.0 24.2 jit_solution(1562470129111546564)
XLA Ops:
  0.6 1.6 %pyramid.1 = (f32[64,128]{1,0:T(8,128)S(1)}, f32[64,128]{1,0:T(8,128)S(1)}, f32[5,64,128]{2,1,0:T(8,128)S(1)}, f32[3,32,128]{2,1,0:T(8,128)S(1)}, f32[2,16,128]{2,1,0:T(8,128)S(1)}) custom-call(f32[64,640]{1,0:T(8,128)} %x_ref.1), custom_call_target="tpu_custom_call" | custom-call | flops 1000000 | bytes 524288 | tf_op jit(solution)/shard_map/pyramid/pallas_call | solution.py:385
  2.2 0.6 %collective-permute-start = (f32[64,128]{1,0:T(8,128)S(1)}, f32[64,128]{1,0:T(8,128)S(1)}, u32[]{:S(2)}, u32[]{:S(2)}) collective-permute-start(f32[64,128]{1,0:T(8,128)S(1)} %get-tuple-element.26), channel_id=1, source_target_pairs={{0,1},{2,3},{4,5},{6,7},{8,9},{10,11},{12,13},{14,15},{16,17},{18,... | collective-permute-start | bytes 98312 | tf_op jit(solution)/shard_map/ppermute | solution.py:418
  2.8 0.1 collective-permute-start.2
  2.9 5.9 %collective-permute-start.1 = (f32[64,128]{1,0:T(8,128)S(1)}, f32[64,128]{1,0:T(8,128)S(1)}, u32[]{:S(2)}, u32[]{:S(2)}) collective-permute-start(f32[64,128]{1,0:T(8,128)S(1)} %get-tuple-element.27), channel_id=1, source_target_pairs={{1,2},{3,4},{5,6},{7,8},{9,10},{11,12},{13,14},{17,18},{19,20},{21... | collective-permute-start | bytes 98312 | tf_op jit(solution)/shard_map/ppermute | solution.py:416
  8.8 0.7 %inner.1 = (f32[64,640]{1,0:T(8,128)S(1)}, f32[64,640]{1,0:T(8,128)S(1)}, f32[2,48,384]{2,1,0:T(8,128)S(1)}, f32[2,32,256]{2,1,0:T(8,128)S(1)}, f32[10,8,128]{2,1,0:T(8,128)S(1)}) custom-call(f32[5,64,128]{2,1,0:T(8,128)S(1)} %get-tuple-element.23.z0, f32[3,32,128]{2,1,0:T(8,128)S(1)} %get-tuple-element.24.z1, f32[2,16,128]{2,1,0:T(8,128)S(1)} %get-tuple-element.25.z2), custom_call_target="tpu_custom_call" | custom-call | flops 100000000 | bytes 524288 | tf_op jit(solution)/shard_map/inner/pallas_call | solution.py:385
  9.5 0.0 collective-permute-done.r1_ref
  9.5 0.0 collective-permute-done.2.r3_ref
  9.6 1.5 %collective-permute-done.1.r2_ref = f32[64,128]{1,0:T(8,128)S(1)} collective-permute-done((f32[64,128]{1,0:T(8,128)S(1)}, f32[64,128]{1,0:T(8,128)S(1)}, u32[]{:S(2)}, u32[]{:S(2)}) %collective-permute-start.1) | collective-permute-done | bytes 32800 | tf_op jit(solution)/shard_map/ppermute | solution.py:416
  11.0 2.2 %edge.1 = (f32[64,640]{1,0:T(8,128)S(1)}, f32[64,640]{1,0:T(8,128)S(1)}, f32[2,48,384]{2,1,0:T(8,128)S(1)}, f32[2,32,256]{2,1,0:T(8,128)S(1)}, f32[2,16,128]{2,1...) custom-call(f32[5,64,128]{2,1,0:T(8,128)S(1)} %get-tuple-element.23., ...), custom_call_target="tpu_custom_call", output_to_operand_aliasing={{0}: (7, {}), {1}: (8, {}), {2}: (9, {}), {3}: (10, {})} | custom-call | flops 1000000 | bytes 524288 | tf_op jit(solution)/shard_map/edge/pallas_call | solution.py:385
  13.2 2.9 %all-to-all-start = ((f32[32,1,128]{2,1,0:T(1,128)}), f32[32,1,128]{2,1,0:T(1,128)S(1)}, u32[]{:S(2)}, u32[]{:S(2)}) async-start(f32[32,1,128]{2,1,0:T(1,128)} %get-tuple-element.33), calls=%async_computation | async-start | bytes 32768 | tf_op jit(solution)/shard_map/all_to_all | solution.py:439
  16.2 2.2 %spread.1 = (f32[2,64,640]{2,1,0:T(8,128)S(1)}, f32[2,64,640]{2,1,0:T(8,128)S(1)}, f32[2,64,640]{2,1,0:T(8,128)S(1)}, f32[2,64,640]{2,1,0:T(8,128)S(1)}) custom-call(f32[2,48,384]{2,1,0:T(8,128)S(1)} %get-tuple-element.36.f1, f32[2,32,256]{2,1,0:T(8,128)S(1)} %get-tuple-element.37.f2, f32[2,16,128]{2,1,0:T(8,128)S(1)} %get-tuple-element.38.f3, ...), custom_call_target="tpu_custom_call" | custom-call | flops 1000000000 | bytes 524288 | tf_op jit(solution)/shard_map/spread/pallas_call | solution.py:385
  18.4 4.9 %all-to-all-done.v_ref = f32[32,1,128]{2,1,0:T(1,128)S(1)} async-done(((f32[32,1,128]{2,1,0:T(1,128)}), f32[32,1,128]{2,1,0:T(1,128)S(1)}, u32[]{:S(2)}, u32[]{:S(2)}) %all-to-all-start) | async-done | bytes 16416 | tf_op jit(solution)/shard_map/all_to_all | solution.py:439
  23.3 0.9 %blend.1 = (f32[64,640]{1,0:T(8,128)}, f32[64,640]{1,0:T(8,128)}) custom-call(f32[32,1,128]{2,1,0:T(1,128)S(1)} %all-to-all-done.v_ref, f32[64,640]{1,0:T(8,128)S(1)} %get-tuple-element.34.s0, f32[64,640]{1,0:T(8,128)S(1)} %get-tuple-element.35.b0, f32[2,64,640]{2,1,0:T(8,128)S(1)} %get-tuple-element.40.u1, f32[2,64,640]{2,1,0:T(8,128)S(1)} %get-tuple-element.41.u2, ...), custom_call_target="tpu_custom_call" | custom-call | flops 1000000 | bytes 524288 | tf_op jit(solution)/shard_map/blend/pallas_call | solution.py:385
Async XLA Ops:
  2.2 7.3 %collective-permute-start = (f32[64,128]{1,0:T(8,128)S(1)}, f32[64,128]{1,0:T(8,128)S(1)}, u32[]{:S(2)}, u32[]{:S(2)}) collective-permute-start(f32[64,128]{1,0:T(8,128)S(1)} %get-tuple-element.26), channel_id=1, source_target_pairs={{0,1},{2,3},{4,5},{6,7},{8,9},{10,11},{12,13},{14,15},{16,17},{18,... | collective-permute-start | bytes 98312 | tf_op jit(solution)/shard_map/ppermute | solution.py:418
  2.8 6.8 %collective-permute-start.2 = (f32[64,128]{1,0:T(8,128)S(1)}, f32[64,128]{1,0:T(8,128)S(1)}, u32[]{:S(2)}, u32[]{:S(2)}) collective-permute-start(f32[64,128]{1,0:T(8,128)S(1)} %get-tuple-element.27), channel_id=1, source_target_pairs={{0,1},{2,3},{4,5},{6,7},{8,9},{10,11},{12,13},{18,19},{20,21},{22,... | collective-permute-start | bytes 98312 | tf_op jit(solution)/shard_map/ppermute | solution.py:417
  2.9 8.2 %collective-permute-start.1 = (f32[64,128]{1,0:T(8,128)S(1)}, f32[64,128]{1,0:T(8,128)S(1)}, u32[]{:S(2)}, u32[]{:S(2)}) collective-permute-start(f32[64,128]{1,0:T(8,128)S(1)} %get-tuple-element.27), channel_id=1, source_target_pairs={{1,2},{3,4},{5,6},{7,8},{9,10},{11,12},{13,14},{17,18},{19,20},{21... | collective-permute-start | bytes 98312 | tf_op jit(solution)/shard_map/ppermute | solution.py:416
  13.2 10.0 %all-to-all-start = ((f32[32,1,128]{2,1,0:T(1,128)}), f32[32,1,128]{2,1,0:T(1,128)S(1)}, u32[]{:S(2)}, u32[]{:S(2)}) async-start(f32[32,1,128]{2,1,0:T(1,128)} %get-tuple-element.33), calls=%async_computation | async-start | bytes 32768 | tf_op jit(solution)/shard_map/all_to_all | solution.py:439

commit v3 on v2

--- a/solution.py
+++ b/solution.py
@@ -48,14 +48,6 @@
     return jnp.where(lane_of(v) == width - 1, v, pltpu.roll(v, v.shape[1] - 1, 1))
 
 
-def split3(v):
-    hi = v.astype(bf16)
-    rest = v - hi.astype(f32)
-    mid = rest.astype(bf16)
-    low = (rest - mid.astype(f32)).astype(bf16)
-    return hi, mid, low
-
-
 def split2(v):
     hi = v.astype(bf16)
     return hi, (v - hi.astype(f32)).astype(bf16)
@@ -63,12 +55,6 @@
 
 def mm(a, b):
     return jnp.dot(a, b, preferred_element_type=f32)
-
-
-def picker():
-    rows = lax.broadcasted_iota(jnp.int32, (256, 128), 0)
-    cols = lax.broadcasted_iota(jnp.int32, (256, 128), 1)
-    return (rows == 2 * cols).astype(f32).astype(bf16)
 
 
 def take(ref, at, count):
@@ -88,17 +74,28 @@
     return jnp.concatenate(out, axis=1)
 
 
-def cols_coarsen(v, width, pick):
-    w1 = west(v)
-    e1 = east(v, width)
-    y = (west(w1) + east(e1, width)) * 0.0625 + (w1 + e1) * 0.25 + v * 0.375
-    out = []
-    for at in range(0, v.shape[1], 256):
-        part = y[:, at : at + 256]
-        sel = pick[: part.shape[1]]
-        hi, mid, low = split3(part)
-        out.append(mm(hi, sel) + (mm(mid, sel) + mm(low, sel)))
-    return out[0] if len(out) == 1 else jnp.concatenate(out, axis=1)
+def every_second(blocks):
+    shape = blocks[0].shape
+    lane = lax.broadcasted_iota(jnp.int32, shape, 1)
+    at = lax.rem(2 * lane, 128)
+    out = ([], [])
+    for i in range(0, len(blocks), 2):
+        for side in range(2):
+            part = jnp.take_along_axis(blocks[i], at + side, axis=1, mode="promise_in_bounds")
+            if i + 1 < len(blocks):
+                other = jnp.take_along_axis(blocks[i + 1], at + side, axis=1, mode="promise_in_bounds")
+                part = jnp.where(lane < 64, part, other)
+            out[side].append(part)
+    return [jnp.concatenate(v, axis=1) for v in out]
+
+
+def cols_coarsen(v, width):
+    even, odd = every_second([v[:, at : at + 128] for at in range(0, v.shape[1], 128)])
+    lane = lane_of(even)
+    even_w = jnp.where(lane == 0, even, pltpu.roll(even, 1, 1))
+    odd_w = jnp.where(lane == 0, even, pltpu.roll(odd, 1, 1))
+    even_e = jnp.where(lane == width // 2 - 1, odd, pltpu.roll(even, even.shape[1] - 1, 1))
+    return (even_w + even_e) * 0.0625 + (odd_w + odd) * 0.25 + even * 0.375
 
 
 def pyramid_kernel(sizes, x_ref, m1_ref, m2_ref, z0, z1, z2, tmp, sems):
@@ -107,7 +104,6 @@
     ]
     for copy in copies:
         copy.start()
-    pick = picker()
     odd = lax.rem(lax.axis_index("rows"), 2) == 1
     h = sizes[0][0]
     for copy in copies:
@@ -126,7 +122,7 @@
         half, wp = sizes[k + 1][0], up128(sizes[k][1])
         low = k + 1
         tmp[low : half - 1, :wp] = rows_sum((z0, z1)[k], 2 * low - 2, half - 1 - low)
-        store(z, 0, cols_coarsen(tmp[0:half, :wp], sizes[k][1], pick))
+        store(z, 0, cols_coarsen(tmp[0:half, :wp], sizes[k][1]))
     row = put(row, z1, 1, sizes[1][0] - 5, 4)
     put(row, z2, 0, 0, sizes[2][0])
 
@@ -211,7 +207,6 @@
         r2 = jnp.where((me == mid) | (me == mid - 1), r3_ref[...], r2)
     up[...] = jnp.where(odd, r1, r2)
     lo[...] = jnp.where(odd, r2, r1)
-    pick = picker()
 
     h0, width0 = sizes[0]
     for c in range(z0.shape[0]):
@@ -223,7 +218,7 @@
     h1, width1 = sizes[1]
     tmp[0:3, :] = rows_sum(t0, 4, 3)
     tmp[3:5, :] = rows_sum(e0, 12, 2)
-    edge = cols_coarsen(tmp[...], width0, pick)
+    edge = cols_coarsen(tmp[...], width0)
     for c in range(z1.shape[0]):
         part = edge[:, 128 * c : 128 * c + 128]
         row0, end = part[1:2], part[3:4]
@@ -240,7 +235,7 @@
     wq = up128(width1)
     tmp[0:3, :wq] = rows_sum(t1, 4, 3)
     tmp[3:6, :wq] = rows_sum(e1, 12, 3)
-    edge = cols_coarsen(tmp[:, :wq], width1, pick)
+    edge = cols_coarsen(tmp[:, :wq], width1)
     for c in range(z2.shape[0]):
         part = edge[:, 128 * c : 128 * c + 128]
         row0, end = part[1:2], part[3:4]
@@ -255,12 +250,12 @@
         w2[c, 2 * h2 + 1 : 2 * h2 + 2, :] = jnp.where(last, end, part[5:6])
     h3, width3 = sizes[3]
     wq = up128(width2)
-    v = cols_coarsen(pad_rows(rows_sum(w2, h2 - 14, h3 + 11)), width2, pick)
+    v = cols_coarsen(pad_rows(rows_sum(w2, h2 - 14, h3 + 11)), width2)
     row = row_of(v) - 6
     v = jnp.where(first & (row < 0), v[6:7], jnp.where(last & (row >= h3), v[h3 + 5 : h3 + 6], v))
     w3[0] = v
-    h4, width4 = sizes[4]
-    v = cols_coarsen(pad_rows(rows_sum(w3, 0, h4 + 4)), width3, pick)
+    h4, _ = sizes[4]
+    v = cols_coarsen(pad_rows(rows_sum(w3, 0, h4 + 4)), width3)
     row = row_of(v) - 2
     v = jnp.where(first & (row < 0), v[2:3], jnp.where(last & (row >= h4), v[h4 + 1 : h4 + 2], v))
     w4[0, 0:8, :] = v
@@ -369,10 +364,10 @@
     both = lambda pairs: [(a, b) for a, b in pairs] + [(b, a) for a, b in pairs]
     even = [(i, i + 1) for i in range(0, count - 1, 2)]
     odd = [(i, i + 1) for i in range(1, count - 1, 2)]
-    if count % 4 or count < 8:
+    if count % 2 or count < 8:
         return both(even), both(odd), None, 0
-    mid = count // 2
-    second = [e for e in odd if e[0] != mid - 1] + [(0, mid), (mid - 1, count - 1)]
+    mid = (2 * count // 3 | 1) + 1
+    second = [e for e in odd if e[1] != mid] + [(0, mid - 1), (mid, count - 1)]
     third = [e for e in even if e[0] not in (mid - 2, mid)] + [(mid - 1, mid), (mid - 2, mid + 1)]
     return both(even), both(second), both(third), mid
 
@@ -381,10 +376,9 @@
 ANY = pl.BlockSpec(memory_space=pl.ANY)
 
 
-def call(kernel, name, outs, scratch=(), in_specs=None, out_specs=None, flops=10**6, limit=8 << 20, aliases=None):
+def call(kernel, outs, scratch=(), in_specs=None, out_specs=None, flops=10**6, limit=8 << 20, aliases=None):
     return lambda *args: pl.pallas_call(
         kernel,
-        name=name,
         out_shape=[jax.ShapeDtypeStruct(s, f32) for s in outs],
         in_specs=in_specs or [VM] * len(args),
         out_specs=out_specs or [VM] * len(outs),
@@ -407,26 +401,21 @@
     msg = (4 * z_shapes[0][0] + 4 * z_shapes[1][0] + sizes[2][0] * z_shapes[2][0], 128)
     m1, m2, z0, z1, z2 = call(
         functools.partial(pyramid_kernel, sizes),
-        "pyramid",
         [msg, msg] + z_shapes[:3],
         [pltpu.VMEM((h0 // 2, width0), f32), pltpu.SemaphoreType.DMA((z_shapes[0][0],))],
         in_specs=[pl.BlockSpec(memory_space=pltpu.HBM)],
     )(pltpu.with_memory_space_constraint(grid, pltpu.HBM))
     pairs1, pairs2, pairs3, mid = halo_pairs(count)
     r2 = lax.ppermute(m2, "rows", pairs2)
+    r1 = lax.ppermute(m1, "rows", pairs1)
     r3 = lax.ppermute(m2, "rows", pairs3) if mid else m2
-    r1 = lax.ppermute(m1, "rows", pairs1)
     f_shapes = [(2, up16(h + 2), up128(w)) for h, w in sizes[1:]]
     acc = (2 * LEVELS + 2, 8, 128)
     s0, b0, f1, f2, sums = call(
-        functools.partial(inner_kernel, sizes),
-        "inner",
-        [grid.shape, grid.shape] + f_shapes[:2] + [acc],
-        flops=10**8,
+        functools.partial(inner_kernel, sizes), [grid.shape, grid.shape] + f_shapes[:2] + [acc], flops=10**8
     )(z0, z1, z2)
     s0, b0, f1, f2, f3, f4, sums = call(
         functools.partial(edge_kernel, sizes, mid),
-        "edge",
         [grid.shape, grid.shape] + f_shapes + [(count, 1, 128)],
         [pltpu.VMEM(msg, f32)] * 2
         + [pltpu.VMEM(blocks(rows, sizes[k][1]), f32) for k in range(2) for rows in (24, 24)]
@@ -438,17 +427,12 @@
     sums = pltpu.with_memory_space_constraint(sums, pltpu.VMEM)
     seen = lax.all_to_all(sums, "rows", 0, 0, tiled=True)
     us = call(
-        functools.partial(spread_kernel, sizes),
-        "spread",
-        [(2, h0, width0)] * LEVELS,
-        flops=10**9,
-        limit=16 << 20,
+        functools.partial(spread_kernel, sizes), [(2, h0, width0)] * LEVELS, flops=10**9, limit=16 << 20
     )(f1, f2, f3, f4)
     cells = [count * h * w for h, w in sizes]
     return tuple(
         call(
             functools.partial(blend_kernel, cells),
-            "blend",
             [grid.shape, grid.shape],
             [pltpu.VMEM(grid.shape, f32)] * 2 + [pltpu.SemaphoreType.DMA((4,))],
             out_specs=[ANY, ANY],

time: 24.4 us -> 23.7 us (0.971)
  Pallas kernels: 7.62 us -> 6.77 us
  starting transfers between devices: 9.52 us -> 10.3 us
  waiting for transfers between devices: 6.38 us -> 5.74 us
    all_to_all x1, starting transfers between devices: 2.94 us -> 3.9 us  [local(): seen = lax.all_to_all(sums, 'rows', 0, 0, tiled=True)]
    pallas_call x5, Pallas kernels: 7.62 us -> 6.77 us  [call(): pl.pallas_call(kernel, out_shape=[jax.ShapeDtypeStruct(s, f32) for s in o...]
    ppermute x1, waiting for transfers between devices: 1.49 us -> 0.85 us  [local(): r2 = lax.ppermute(m2, 'rows', pairs2)]
where the time goes in v3:
time: 23.7 us; the launch traced here: 23.5 us
  starting transfers between devices  10.3 us (43%)
  Pallas kernels  6.77 us (29%)
  waiting for transfers between devices  5.74 us (24%)
  between operations  0.68 us (3%)
    pallas_call x5, Pallas kernels, call(): pl.pallas_call(kernel, out_shape=[jax.ShapeDtypeStruct(s, f32) for s in o...  6.77 us
    ppermute x1, starting transfers between devices, local(): r2 = lax.ppermute(m2, 'rows', pairs2)  5.74 us
    all_to_all x1, waiting for transfers between devices, local(): seen = lax.all_to_all(sums, 'rows', 0, 0, tiled=True)  4.89 us
    all_to_all x1, starting transfers between devices, local(): seen = lax.all_to_all(sums, 'rows', 0, 0, tiled=True)  3.9 us
    ppermute x1, waiting for transfers between devices, local(): r2 = lax.ppermute(m2, 'rows', pairs2)  0.85 us
    ppermute x1, starting transfers between devices, local(): r1 = lax.ppermute(m1, 'rows', pairs1)  0.56 us
  transfers between devices with their start and end apart: 4, of which 2 were waited for; matrix products, arithmetic and copies ran while one was open for 0% of the time, Pallas kernels for 12%

profile of v3, /device:TPU:0, one launch (start us, length us, event | category | flops | bytes accessed | tf_op | source)
XLA Modules:
  0.0 23.5 jit_solution(7455416227624693241)
XLA Ops:
  0.6 1.3 %shard_map.30 = (f32[64,128]{1,0:T(8,128)S(1)}, f32[64,128]{1,0:T(8,128)S(1)}, f32[5,64,128]{2,1,0:T(8,128)S(1)}, f32[3,32,128]{2,1,0:T(8,128)S(1)}, f32[2,16,128]{2,1,0:T(8,128)S(1)}) custom-call(f32[64,640]{1,0:T(8,128)} %x_ref.1), custom_call_target="tpu_custom_call" | custom-call | flops 1000000 | bytes 524288 | tf_op jit(solution)/shard_map/pallas_call | solution.py:380
  1.9 0.6 %collective-permute-start = (f32[64,128]{1,0:T(8,128)S(1)}, f32[64,128]{1,0:T(8,128)S(1)}, u32[]{:S(2)}, u32[]{:S(2)}) collective-permute-start(f32[64,128]{1,0:T(8,128)S(1)} %get-tuple-element.26), channel_id=1, source_target_pairs={{0,1},{2,3},{4,5},{6,7},{8,9},{10,11},{12,13},{14,15},{16,17},{18,... | collective-permute-start | bytes 98312 | tf_op jit(solution)/shard_map/ppermute | solution.py:410
  2.5 0.1 collective-permute-start.2
  2.6 5.7 %collective-permute-start.1 = (f32[64,128]{1,0:T(8,128)S(1)}, f32[64,128]{1,0:T(8,128)S(1)}, u32[]{:S(2)}, u32[]{:S(2)}) collective-permute-start(f32[64,128]{1,0:T(8,128)S(1)} %get-tuple-element.27), channel_id=1, source_target_pairs={{1,2},{3,4},{5,6},{7,8},{9,10},{11,12},{13,14},{15,16},{17,18},{19... | collective-permute-start | bytes 98312 | tf_op jit(solution)/shard_map/ppermute | solution.py:409
  8.3 0.7 %shard_map.31 = (f32[64,640]{1,0:T(8,128)S(1)}, f32[64,640]{1,0:T(8,128)S(1)}, f32[2,48,384]{2,1,0:T(8,128)S(1)}, f32[2,32,256]{2,1,0:T(8,128)S(1)}, f32[10,8,128]{2,1,0:T(8,128)S(1)}) custom-call(f32[5,64,128]{2,1,0:T(8,128)S(1)} %get-tuple-element.23.z0, f32[3,32,128]{2,1,0:T(8,128)S(1)} %get-tuple-element.24.z1, f32[2,16,128]{2,1,0:T(8,128)S(1)} %get-tuple-element.25.z2), custom_call_target="tpu_custom_call" | custom-call | flops 100000000 | bytes 524288 | tf_op jit(solution)/shard_map/pallas_call | solution.py:380
  9.1 0.0 collective-permute-done.r1_ref
  9.1 0.0 collective-permute-done.2.r3_ref
  9.1 0.8 %collective-permute-done.1.r2_ref = f32[64,128]{1,0:T(8,128)S(1)} collective-permute-done((f32[64,128]{1,0:T(8,128)S(1)}, f32[64,128]{1,0:T(8,128)S(1)}, u32[]{:S(2)}, u32[]{:S(2)}) %collective-permute-start.1) | collective-permute-done | bytes 32800 | tf_op jit(solution)/shard_map/ppermute | solution.py:409
  9.9 1.6 %shard_map.32 = (f32[64,640]{1,0:T(8,128)S(1)}, f32[64,640]{1,0:T(8,128)S(1)}, f32[2,48,384]{2,1,0:T(8,128)S(1)}, f32[2,32,256]{2,1,0:T(8,128)S(1)}, f32[2,16,12...) custom-call(f32[5,64,128]{2,1,0:T(8,128)S(1)} %get-tuple-element.23., ...), custom_call_target="tpu_custom_call", output_to_operand_aliasing={{0}: (7, {}), {1}: (8, {}), {2}: (9, {}), {3}: (10, {})} | custom-call | flops 1000000 | bytes 524288 | tf_op jit(solution)/shard_map/pallas_call | solution.py:380
  11.5 3.9 %all-to-all-start = ((f32[32,1,128]{2,1,0:T(1,128)}), f32[32,1,128]{2,1,0:T(1,128)S(1)}, u32[]{:S(2)}, u32[]{:S(2)}) async-start(f32[32,1,128]{2,1,0:T(1,128)} %get-tuple-element.33), calls=%async_computation | async-start | bytes 32768 | tf_op jit(solution)/shard_map/all_to_all | solution.py:428
  15.4 2.2 %shard_map.33 = (f32[2,64,640]{2,1,0:T(8,128)S(1)}, f32[2,64,640]{2,1,0:T(8,128)S(1)}, f32[2,64,640]{2,1,0:T(8,128)S(1)}, f32[2,64,640]{2,1,0:T(8,128)S(1)}) custom-call(f32[2,48,384]{2,1,0:T(8,128)S(1)} %get-tuple-element.36.f1, f32[2,32,256]{2,1,0:T(8,128)S(1)} %get-tuple-element.37.f2, f32[2,16,128]{2,1,0:T(8,128)S(1)} %get-tuple-element.38.f3, ...), custom_call_target="tpu_custom_call" | custom-call | flops 1000000000 | bytes 524288 | tf_op jit(solution)/shard_map/pallas_call | solution.py:380
  17.6 4.9 %all-to-all-done.v_ref = f32[32,1,128]{2,1,0:T(1,128)S(1)} async-done(((f32[32,1,128]{2,1,0:T(1,128)}), f32[32,1,128]{2,1,0:T(1,128)S(1)}, u32[]{:S(2)}, u32[]{:S(2)}) %all-to-all-start) | async-done | bytes 16416 | tf_op jit(solution)/shard_map/all_to_all | solution.py:428
  22.5 0.9 %shard_map.34 = (f32[64,640]{1,0:T(8,128)}, f32[64,640]{1,0:T(8,128)}) custom-call(f32[32,1,128]{2,1,0:T(1,128)S(1)} %all-to-all-done.v_ref, f32[64,640]{1,0:T(8,128)S(1)} %get-tuple-element.34.s0, f32[64,640]{1,0:T(8,128)S(1)} %get-tuple-element.35.b0, f32[2,64,640]{2,1,0:T(8,128)S(1)} %get-tuple-element.40.u1, f32[2,64,640]{2,1,0:T(8,128)S(1)} %get-tuple-element.41.u2, ...), custom_call_target="tpu_custom_call" | custom-call | flops 1000000 | bytes 524288 | tf_op jit(solution)/shard_map/pallas_call | solution.py:380
Async XLA Ops:
  1.9 7.1 %collective-permute-start = (f32[64,128]{1,0:T(8,128)S(1)}, f32[64,128]{1,0:T(8,128)S(1)}, u32[]{:S(2)}, u32[]{:S(2)}) collective-permute-start(f32[64,128]{1,0:T(8,128)S(1)} %get-tuple-element.26), channel_id=1, source_target_pairs={{0,1},{2,3},{4,5},{6,7},{8,9},{10,11},{12,13},{14,15},{16,17},{18,... | collective-permute-start | bytes 98312 | tf_op jit(solution)/shard_map/ppermute | solution.py:410
  2.5 6.6 %collective-permute-start.2 = (f32[64,128]{1,0:T(8,128)S(1)}, f32[64,128]{1,0:T(8,128)S(1)}, u32[]{:S(2)}, u32[]{:S(2)}) collective-permute-start(f32[64,128]{1,0:T(8,128)S(1)} %get-tuple-element.27), channel_id=1, source_target_pairs={{0,1},{2,3},{4,5},{6,7},{8,9},{10,11},{12,13},{14,15},{16,17},{18,... | collective-permute-start | bytes 98312 | tf_op jit(solution)/shard_map/ppermute | solution.py:411
  2.6 7.3 %collective-permute-start.1 = (f32[64,128]{1,0:T(8,128)S(1)}, f32[64,128]{1,0:T(8,128)S(1)}, u32[]{:S(2)}, u32[]{:S(2)}) collective-permute-start(f32[64,128]{1,0:T(8,128)S(1)} %get-tuple-element.27), channel_id=1, source_target_pairs={{1,2},{3,4},{5,6},{7,8},{9,10},{11,12},{13,14},{15,16},{17,18},{19... | collective-permute-start | bytes 98312 | tf_op jit(solution)/shard_map/ppermute | solution.py:409
  11.5 11.0 %all-to-all-start = ((f32[32,1,128]{2,1,0:T(1,128)}), f32[32,1,128]{2,1,0:T(1,128)S(1)}, u32[]{:S(2)}, u32[]{:S(2)}) async-start(f32[32,1,128]{2,1,0:T(1,128)} %get-tuple-element.33), calls=%async_computation | async-start | bytes 32768 | tf_op jit(solution)/shard_map/all_to_all | solution.py:428

commit v4 on v3

--- a/solution.py
+++ b/solution.py
@@ -74,28 +74,32 @@
     return jnp.concatenate(out, axis=1)
 
 
-def every_second(blocks):
-    shape = blocks[0].shape
-    lane = lax.broadcasted_iota(jnp.int32, shape, 1)
-    at = lax.rem(2 * lane, 128)
-    out = ([], [])
-    for i in range(0, len(blocks), 2):
-        for side in range(2):
-            part = jnp.take_along_axis(blocks[i], at + side, axis=1, mode="promise_in_bounds")
-            if i + 1 < len(blocks):
-                other = jnp.take_along_axis(blocks[i + 1], at + side, axis=1, mode="promise_in_bounds")
-                part = jnp.where(lane < 64, part, other)
-            out[side].append(part)
-    return [jnp.concatenate(v, axis=1) for v in out]
+def lanes(v, at):
+    return jnp.take_along_axis(v, at, axis=1, mode="promise_in_bounds")
 
 
 def cols_coarsen(v, width):
-    even, odd = every_second([v[:, at : at + 128] for at in range(0, v.shape[1], 128)])
-    lane = lane_of(even)
-    even_w = jnp.where(lane == 0, even, pltpu.roll(even, 1, 1))
-    odd_w = jnp.where(lane == 0, even, pltpu.roll(odd, 1, 1))
-    even_e = jnp.where(lane == width // 2 - 1, odd, pltpu.roll(even, even.shape[1] - 1, 1))
-    return (even_w + even_e) * 0.0625 + (odd_w + odd) * 0.25 + even * 0.375
+    blocks = [v[:, at : at + 128] for at in range(0, v.shape[1], 128)]
+    lane = lax.broadcasted_iota(jnp.int32, blocks[0].shape, 1)
+    patterns = [(2 * lane + tap + 128) & 127 for tap in (-2, -1, 0, 1, 2)]
+    out = []
+    for c in range(0, len(blocks), 2):
+        taps = []
+        for tap, at in zip((-2, -1, 0, 1, 2), patterns):
+            part = lanes(blocks[c], at)
+            if c + 1 < len(blocks):
+                part = jnp.where(2 * lane + tap < 128, part, lanes(blocks[c + 1], at))
+            if tap < 0 and c:
+                part = jnp.where(lane == 0, lanes(blocks[c - 1], at), part)
+            if tap > 1 and c + 2 < len(blocks):
+                part = jnp.where(lane == 127, lanes(blocks[c + 2], at), part)
+            taps.append(part)
+        if c == 0:
+            taps[0] = jnp.where(lane == 0, taps[2], taps[0])
+            taps[1] = jnp.where(lane == 0, taps[2], taps[1])
+        taps[4] = jnp.where(lane == width // 2 - 1 - 64 * c, taps[3], taps[4])
+        out.append((taps[0] + taps[4]) * 0.0625 + (taps[1] + taps[3]) * 0.25 + taps[2] * 0.375)
+    return out[0] if len(out) == 1 else jnp.concatenate(out, axis=1)
 
 
 def pyramid_kernel(sizes, x_ref, m1_ref, m2_ref, z0, z1, z2, tmp, sems):
@@ -297,11 +301,9 @@
             f[field, 0:rows, :] = jnp.where(row <= h, v, 0.0)
             if rows < f.shape[1]:
                 f[field, rows:, :] = jnp.zeros((f.shape[1] - rows, f.shape[2]), f32)
-    table = jnp.zeros((16, 128), f32)
-    table_row = row_of(table)
+    table = jnp.zeros((8, 128), f32)
     for i, v in enumerate([t[0] for t in totals] + [t[1] for t in totals]):
-        table = jnp.where(table_row == i, jnp.sum(v, axis=0, keepdims=True), table)
-    table = jnp.where(table_row == lane_of(table), jnp.sum(table, axis=1, keepdims=True), 0.0)
+        table = jnp.where(lane_of(table) == i, jnp.sum(v, axis=1, keepdims=True), table)
     line = jnp.sum(table, axis=0, keepdims=True)
     sum_ref[...] = jnp.broadcast_to(line.reshape(1, 1, 128), sum_ref.shape)
 
@@ -366,7 +368,7 @@
     odd = [(i, i + 1) for i in range(1, count - 1, 2)]
     if count % 2 or count < 8:
         return both(even), both(odd), None, 0
-    mid = (2 * count // 3 | 1) + 1
+    mid = count * 13 // 16 & ~1
     second = [e for e in odd if e[1] != mid] + [(0, mid - 1), (mid, count - 1)]
     third = [e for e in even if e[0] not in (mid - 2, mid)] + [(mid - 1, mid), (mid - 2, mid + 1)]
     return both(even), both(second), both(third), mid

time: 23.7 us -> 23.8 us (level)
  starting transfers between devices: 10.3 us -> 10.7 us
  Pallas kernels: 6.77 us -> 6.51 us
    all_to_all x1, starting transfers between devices: 3.9 us -> 4.22 us  [local(): seen = lax.all_to_all(sums, 'rows', 0, 0, tiled=True)]
    pallas_call x5, Pallas kernels: 6.77 us -> 6.51 us  [call(): pl.pallas_call(kernel, out_shape=[jax.ShapeDtypeStruct(s, f32) for s in o...]
where the time goes in v4:
time: 23.8 us; the launch traced here: 23.6 us
  starting transfers between devices  10.7 us (45%)
  Pallas kernels  6.51 us (27%)
  waiting for transfers between devices  5.74 us (24%)
  between operations  0.68 us (3%)
    pallas_call x5, Pallas kernels, call(): pl.pallas_call(kernel, out_shape=[jax.ShapeDtypeStruct(s, f32) for s in o...  6.51 us
    ppermute x1, starting transfers between devices, local(): r2 = lax.ppermute(m2, 'rows', pairs2)  5.8 us
    all_to_all x1, waiting for transfers between devices, local(): seen = lax.all_to_all(sums, 'rows', 0, 0, tiled=True)  4.89 us
    all_to_all x1, starting transfers between devices, local(): seen = lax.all_to_all(sums, 'rows', 0, 0, tiled=True)  4.22 us
    ppermute x1, waiting for transfers between devices, local(): r2 = lax.ppermute(m2, 'rows', pairs2)  0.85 us
    ppermute x1, starting transfers between devices, local(): r1 = lax.ppermute(m1, 'rows', pairs1)  0.56 us
  transfers between devices with their start and end apart: 4, of which 2 were waited for; matrix products, arithmetic and copies ran while one was open for 0% of the time, Pallas kernels for 12%

profile of v4, /device:TPU:0, one launch (start us, length us, event | category | flops | bytes accessed | tf_op | source)
XLA Modules:
  0.0 23.6 jit_solution(10409348714931520109)
XLA Ops:
  0.6 1.2 %shard_map.30 = (f32[64,128]{1,0:T(8,128)S(1)}, f32[64,128]{1,0:T(8,128)S(1)}, f32[5,64,128]{2,1,0:T(8,128)S(1)}, f32[3,32,128]{2,1,0:T(8,128)S(1)}, f32[2,16,128]{2,1,0:T(8,128)S(1)}) custom-call(f32[64,640]{1,0:T(8,128)} %x_ref.1), custom_call_target="tpu_custom_call" | custom-call | flops 1000000 | bytes 524288 | tf_op jit(solution)/shard_map/pallas_call | solution.py:382
  1.9 0.6 %collective-permute-start = (f32[64,128]{1,0:T(8,128)S(1)}, f32[64,128]{1,0:T(8,128)S(1)}, u32[]{:S(2)}, u32[]{:S(2)}) collective-permute-start(f32[64,128]{1,0:T(8,128)S(1)} %get-tuple-element.26), channel_id=1, source_target_pairs={{0,1},{2,3},{4,5},{6,7},{8,9},{10,11},{12,13},{14,15},{16,17},{18,... | collective-permute-start | bytes 98312 | tf_op jit(solution)/shard_map/ppermute | solution.py:412
  2.4 0.1 collective-permute-start.2
  2.5 5.8 %collective-permute-start.1 = (f32[64,128]{1,0:T(8,128)S(1)}, f32[64,128]{1,0:T(8,128)S(1)}, u32[]{:S(2)}, u32[]{:S(2)}) collective-permute-start(f32[64,128]{1,0:T(8,128)S(1)} %get-tuple-element.27), channel_id=1, source_target_pairs={{1,2},{3,4},{5,6},{7,8},{9,10},{11,12},{13,14},{15,16},{17,18},{19... | collective-permute-start | bytes 98312 | tf_op jit(solution)/shard_map/ppermute | solution.py:411
  8.3 0.7 %shard_map.31 = (f32[64,640]{1,0:T(8,128)S(1)}, f32[64,640]{1,0:T(8,128)S(1)}, f32[2,48,384]{2,1,0:T(8,128)S(1)}, f32[2,32,256]{2,1,0:T(8,128)S(1)}, f32[10,8,128]{2,1,0:T(8,128)S(1)}) custom-call(f32[5,64,128]{2,1,0:T(8,128)S(1)} %get-tuple-element.23.z0, f32[3,32,128]{2,1,0:T(8,128)S(1)} %get-tuple-element.24.z1, f32[2,16,128]{2,1,0:T(8,128)S(1)} %get-tuple-element.25.z2), custom_call_target="tpu_custom_call" | custom-call | flops 100000000 | bytes 524288 | tf_op jit(solution)/shard_map/pallas_call | solution.py:382
  9.0 0.0 collective-permute-done.r1_ref
  9.0 0.0 collective-permute-done.2.r3_ref
  9.1 0.8 %collective-permute-done.1.r2_ref = f32[64,128]{1,0:T(8,128)S(1)} collective-permute-done((f32[64,128]{1,0:T(8,128)S(1)}, f32[64,128]{1,0:T(8,128)S(1)}, u32[]{:S(2)}, u32[]{:S(2)}) %collective-permute-start.1) | collective-permute-done | bytes 32800 | tf_op jit(solution)/shard_map/ppermute | solution.py:411
  9.9 1.4 %shard_map.32 = (f32[64,640]{1,0:T(8,128)S(1)}, f32[64,640]{1,0:T(8,128)S(1)}, f32[2,48,384]{2,1,0:T(8,128)S(1)}, f32[2,32,256]{2,1,0:T(8,128)S(1)}, f32[2,16,12...) custom-call(f32[5,64,128]{2,1,0:T(8,128)S(1)} %get-tuple-element.23., ...), custom_call_target="tpu_custom_call", output_to_operand_aliasing={{0}: (7, {}), {1}: (8, {}), {2}: (9, {}), {3}: (10, {})} | custom-call | flops 1000000 | bytes 524288 | tf_op jit(solution)/shard_map/pallas_call | solution.py:382
  11.3 4.2 %all-to-all-start = ((f32[32,1,128]{2,1,0:T(1,128)}), f32[32,1,128]{2,1,0:T(1,128)S(1)}, u32[]{:S(2)}, u32[]{:S(2)}) async-start(f32[32,1,128]{2,1,0:T(1,128)} %get-tuple-element.33), calls=%async_computation | async-start | bytes 32768 | tf_op jit(solution)/shard_map/all_to_all | solution.py:430
  15.5 2.2 %shard_map.33 = (f32[2,64,640]{2,1,0:T(8,128)S(1)}, f32[2,64,640]{2,1,0:T(8,128)S(1)}, f32[2,64,640]{2,1,0:T(8,128)S(1)}, f32[2,64,640]{2,1,0:T(8,128)S(1)}) custom-call(f32[2,48,384]{2,1,0:T(8,128)S(1)} %get-tuple-element.36.f1, f32[2,32,256]{2,1,0:T(8,128)S(1)} %get-tuple-element.37.f2, f32[2,16,128]{2,1,0:T(8,128)S(1)} %get-tuple-element.38.f3, ...), custom_call_target="tpu_custom_call" | custom-call | flops 1000000000 | bytes 524288 | tf_op jit(solution)/shard_map/pallas_call | solution.py:382
  17.8 4.9 %all-to-all-done.v_ref = f32[32,1,128]{2,1,0:T(1,128)S(1)} async-done(((f32[32,1,128]{2,1,0:T(1,128)}), f32[32,1,128]{2,1,0:T(1,128)S(1)}, u32[]{:S(2)}, u32[]{:S(2)}) %all-to-all-start) | async-done | bytes 16416 | tf_op jit(solution)/shard_map/all_to_all | solution.py:430
  22.6 0.9 %shard_map.34 = (f32[64,640]{1,0:T(8,128)}, f32[64,640]{1,0:T(8,128)}) custom-call(f32[32,1,128]{2,1,0:T(1,128)S(1)} %all-to-all-done.v_ref, f32[64,640]{1,0:T(8,128)S(1)} %get-tuple-element.34.s0, f32[64,640]{1,0:T(8,128)S(1)} %get-tuple-element.35.b0, f32[2,64,640]{2,1,0:T(8,128)S(1)} %get-tuple-element.40.u1, f32[2,64,640]{2,1,0:T(8,128)S(1)} %get-tuple-element.41.u2, ...), custom_call_target="tpu_custom_call" | custom-call | flops 1000000 | bytes 524288 | tf_op jit(solution)/shard_map/pallas_call | solution.py:382
Async XLA Ops:
  1.9 7.2 %collective-permute-start = (f32[64,128]{1,0:T(8,128)S(1)}, f32[64,128]{1,0:T(8,128)S(1)}, u32[]{:S(2)}, u32[]{:S(2)}) collective-permute-start(f32[64,128]{1,0:T(8,128)S(1)} %get-tuple-element.26), channel_id=1, source_target_pairs={{0,1},{2,3},{4,5},{6,7},{8,9},{10,11},{12,13},{14,15},{16,17},{18,... | collective-permute-start | bytes 98312 | tf_op jit(solution)/shard_map/ppermute | solution.py:412
  2.4 6.6 %collective-permute-start.2 = (f32[64,128]{1,0:T(8,128)S(1)}, f32[64,128]{1,0:T(8,128)S(1)}, u32[]{:S(2)}, u32[]{:S(2)}) collective-permute-start(f32[64,128]{1,0:T(8,128)S(1)} %get-tuple-element.27), channel_id=1, source_target_pairs={{0,1},{2,3},{4,5},{6,7},{8,9},{10,11},{12,13},{14,15},{16,17},{18,... | collective-permute-start | bytes 98312 | tf_op jit(solution)/shard_map/ppermute | solution.py:413
  2.5 7.4 %collective-permute-start.1 = (f32[64,128]{1,0:T(8,128)S(1)}, f32[64,128]{1,0:T(8,128)S(1)}, u32[]{:S(2)}, u32[]{:S(2)}) collective-permute-start(f32[64,128]{1,0:T(8,128)S(1)} %get-tuple-element.27), channel_id=1, source_target_pairs={{1,2},{3,4},{5,6},{7,8},{9,10},{11,12},{13,14},{15,16},{17,18},{19... | collective-permute-start | bytes 98312 | tf_op jit(solution)/shard_map/ppermute | solution.py:411
  11.3 11.3 %all-to-all-start = ((f32[32,1,128]{2,1,0:T(1,128)}), f32[32,1,128]{2,1,0:T(1,128)S(1)}, u32[]{:S(2)}, u32[]{:S(2)}) async-start(f32[32,1,128]{2,1,0:T(1,128)} %get-tuple-element.33), calls=%async_computation | async-start | bytes 32768 | tf_op jit(solution)/shard_map/all_to_all | solution.py:430

commit v5 on v4

--- a/solution.py
+++ b/solution.py
@@ -10,7 +10,6 @@
 LEVELS = 4
 EPS = 1e-06
 f32 = jnp.float32
-bf16 = jnp.bfloat16
 ATAN = (
     1.0,
     -0.3333314528,
@@ -28,10 +27,6 @@
     return -(-n // 128) * 128
 
 
-def up16(n):
-    return -(-n // 16) * 16
-
-
 def lane_of(v):
     return lax.broadcasted_iota(jnp.int32, v.shape, 1)
 
@@ -46,15 +41,6 @@
 
 def east(v, width):
     return jnp.where(lane_of(v) == width - 1, v, pltpu.roll(v, v.shape[1] - 1, 1))
-
-
-def split2(v):
-    hi = v.astype(bf16)
-    return hi, (v - hi.astype(f32)).astype(bf16)
-
-
-def mm(a, b):
-    return jnp.dot(a, b, preferred_element_type=f32)
 
 
 def take(ref, at, count):
@@ -78,21 +64,26 @@
     return jnp.take_along_axis(v, at, axis=1, mode="promise_in_bounds")
 
 
+def split(v):
+    return [v[:, at : at + 128] for at in range(0, v.shape[1], 128)]
+
+
 def cols_coarsen(v, width):
-    blocks = [v[:, at : at + 128] for at in range(0, v.shape[1], 128)]
+    blocks = split(v)
     lane = lax.broadcasted_iota(jnp.int32, blocks[0].shape, 1)
     patterns = [(2 * lane + tap + 128) & 127 for tap in (-2, -1, 0, 1, 2)]
+    found = [[lanes(v, at) for v in blocks] for at in patterns]
     out = []
     for c in range(0, len(blocks), 2):
         taps = []
-        for tap, at in zip((-2, -1, 0, 1, 2), patterns):
-            part = lanes(blocks[c], at)
+        for tap, got in zip((-2, -1, 0, 1, 2), found):
+            part = got[c]
             if c + 1 < len(blocks):
-                part = jnp.where(2 * lane + tap < 128, part, lanes(blocks[c + 1], at))
+                part = jnp.where(2 * lane + tap < 128, part, got[c + 1])
             if tap < 0 and c:
-                part = jnp.where(lane == 0, lanes(blocks[c - 1], at), part)
+                part = jnp.where(lane == 0, got[c - 1], part)
             if tap > 1 and c + 2 < len(blocks):
-                part = jnp.where(lane == 127, lanes(blocks[c + 2], at), part)
+                part = jnp.where(lane == 127, got[c + 2], part)
             taps.append(part)
         if c == 0:
             taps[0] = jnp.where(lane == 0, taps[2], taps[0])
@@ -166,7 +157,7 @@
     return total
 
 
-def inner_kernel(sizes, z0, z1, z2, s0_ref, b0_ref, f1, f2, acc_ref):
+def inner_kernel(sizes, z0, z1, z2, s0_ref, b0_ref, t1, t2, acc_ref):
     for k, z in enumerate((z0, z1, z2)):
         h, width = sizes[k]
         s_sum = b_sum = None
@@ -179,9 +170,10 @@
                 s0_ref[at : at + 8, :] = slope
                 b0_ref[at : at + 8, :] = bend
             else:
-                f = (f1, f2)[k - 1]
-                f[0, at + 1 : at + 9, :] = slope
-                f[1, at + 1 : at + 9, :] = bend
+                t = (t1, t2)[k - 1]
+                for field, v in enumerate((slope, bend)):
+                    for c, part in enumerate(cols_refine(split(v), k, width, t.shape[1])):
+                        t[field, c, at + 1 : at + 9, :] = part
             skip = 3 if k else 1
             if at == 0 or at == h - 8 or width % 128:
                 row = row_of(slope) + at
@@ -192,16 +184,12 @@
             b_sum = fb if at == 0 else b_sum + fb
         acc_ref[k] = s_sum
         acc_ref[LEVELS + 1 + k] = b_sum
-        if k:
-            f = (f1, f2)[k - 1]
-            for field in range(2):
-                f[field, h + 2 :, :] = jnp.zeros((f.shape[1] - h - 2, f.shape[2]), f32)
     for k in range(3, LEVELS + 1):
         acc_ref[k] = jnp.zeros((8, 128), f32)
         acc_ref[LEVELS + 1 + k] = jnp.zeros((8, 128), f32)
 
 
-def edge_kernel(sizes, mid, z0, z1, z2, r1_ref, r2_ref, r3_ref, acc_ref, s0_in, b0_in, f1_in, f2_in,
+def edge_kernel(sizes, mid, z0, z1, z2, r1_ref, r2_ref, r3_ref, acc_ref, s0_in, b0_in,
                 s0_ref, b0_ref, f1, f2, f3, f4, sum_ref, up, lo, t0, e0, t1, e1, w2, w3, w4, tmp):
     me = lax.axis_index("rows")
     odd = lax.rem(me, 2) == 1
@@ -288,8 +276,7 @@
         for field, v in enumerate((slope, bend)):
             row = row_of(v)
             v = jnp.where(first & (row == 0), v[1:2], jnp.where(last & (row == 7), v[6:7], v))
-            f[field, 0:4, :] = v[0:4]
-            f[field, h - 2 : h + 2, :] = v[4:8]
+            f[field] = v
     for k, z, at, f in ((3, w3, 5, f3), (4, w4, 1, f4)):
         h, width = sizes[k]
         rows = -(-(h + 2) // 8) * 8
@@ -299,8 +286,6 @@
         for field, v in enumerate((slope, bend)):
             v = jnp.where(first & (row < 0), v[1:2], jnp.where(last & (row >= h), v[h : h + 1], v))
             f[field, 0:rows, :] = jnp.where(row <= h, v, 0.0)
-            if rows < f.shape[1]:
-                f[field, rows:, :] = jnp.zeros((f.shape[1] - rows, f.shape[2]), f32)
     table = jnp.zeros((8, 128), f32)
     for i, v in enumerate([t[0] for t in totals] + [t[1] for t in totals]):
         table = jnp.where(lane_of(table) == i, jnp.sum(v, axis=1, keepdims=True), table)
@@ -313,49 +298,82 @@
     return jnp.concatenate([v, jnp.zeros((short, v.shape[1]), f32)], axis=0) if short else v
 
 
-def hat(shape, factor, count, shift, along):
-    fine = lax.broadcasted_iota(jnp.int32, shape, along).astype(f32)
-    coarse = lax.broadcasted_iota(jnp.int32, shape, 1 - along).astype(f32)
-    y = (fine + 0.5) * (1.0 / factor) - 0.5
-    if count is not None:
-        y = jnp.clip(y, 0.0, count - 1.0)
-    return jnp.maximum(0.0, 1.0 - jnp.abs(y + shift - coarse)).astype(bf16)
-
-
-def spread_kernel(sizes, f1, f2, f3, f4, u1, u2, u3, u4):
+def cols_refine(blocks, k, width, count):
+    f = 1 << k
+    lane = lax.broadcasted_iota(jnp.int32, blocks[0].shape, 1)
+    west_side = (lane & (f - 1)) < f // 2
+    pos = ((lane & (f - 1)).astype(f32) + 0.5) * (1.0 / f)
+    other = jnp.abs(pos - 0.5)
+    out = []
+    for c in range(count):
+        at, first = divmod((128 * c) >> k, 128)
+        centre = first + (lane >> k)
+        near = jnp.where(west_side, centre - 1, centre + 1)
+        if c == 0:
+            near = jnp.maximum(near, 0)
+        if c == count - 1:
+            near = jnp.minimum(near, width - 1 - 128 * at)
+        near = near & 127
+        side = lanes(blocks[at], near)
+        if c and first == 0:
+            side = jnp.where(lane < f // 2, lanes(blocks[at - 1], near), side)
+        if c < count - 1 and first + (128 >> k) == 128:
+            side = jnp.where(lane >= 128 - f // 2, lanes(blocks[at + 1], near), side)
+        out.append((1.0 - other) * lanes(blocks[at], centre) + other * side)
+    return out
+
+
+def finish_kernel(sizes, cells, v_ref, s0, b0, f1, f2, f3, f4, t1_in, t2_in, slope_ref, bend_ref, t1, t2, t3, t4, u1, u2, slope_buf, bend_buf, sems):
     h0, width0 = sizes[0]
-    for k, f, u in zip(range(1, LEVELS + 1), (f1, f2, f3, f4), (u1, u2, u3, u4)):
-        rows, wp = f.shape[1], f.shape[2]
-        across = hat((wp, width0), 2**k, sizes[k][1], 0.0, 1)
-        down = hat((h0, rows), 2**k, None, 1.0, 0)
-        for field in range(2):
-            hi, low = split2(f[field])
-            wide = mm(hi, across) + mm(low, across)
-            hi, low = split2(wide)
-            u[field] = mm(down, hi) + mm(down, low)
-
-
-def blend_kernel(cells, v_ref, s0, b0, u1, u2, u3, u4, slope_ref, bend_ref, slope_buf, bend_buf, sems):
+    count = width0 // 128
     sums = jnp.sum(v_ref[...], axis=0)
     lane = lax.broadcasted_iota(jnp.int32, (1, 128), 1)
-    count = jnp.ones((1, 128), f32)
+    number = jnp.ones((1, 128), f32)
     for k, c in enumerate(cells):
-        count = jnp.where((lane == k) | (lane == k + LEVELS + 1), float(c), count)
-    mean = sums / count
+        number = jnp.where((lane == k) | (lane == k + LEVELS + 1), float(c), number)
+    mean = sums / number
     scale = jnp.where(lane <= LEVELS, 1.0 / (mean + EPS), 1.0 / jnp.sqrt(mean + EPS))
-    rows = slope_buf.shape[0]
+    sub = lax.broadcasted_iota(jnp.int32, (8, 128), 0)
     copies = []
     for field, (base, buf, out) in enumerate(((s0, slope_buf, slope_ref), (b0, bend_buf, bend_ref))):
-        factors = [jnp.broadcast_to(scale[:, i : i + 1], (8, 128)) for i in range(field * (LEVELS + 1), (field + 1) * (LEVELS + 1))]
-        for half in range(2):
-            for at in range(half * rows // 2, (half + 1) * rows // 2, 8):
-                for c in range(0, buf.shape[1], 128):
-                    total = base[at : at + 8, c : c + 128] * factors[0]
-                    for factor, u in zip(factors[1:], (u1, u2, u3, u4)):
-                        total = total + u[field, at : at + 8, c : c + 128] * factor
-                    buf[at : at + 8, c : c + 128] = total
-            part = pl.ds(half * rows // 2, rows // 2)
-            copy = pltpu.make_async_copy(buf.at[part], out.at[part], sems.at[2 * field + half])
+        for k, f, t in ((4, f4, t4), (3, f3, t3), (2, f2, t2), (1, f1, t1)):
+            for at in range(0, f.shape[1], 8):
+                for c, v in enumerate(cols_refine(split(f[field, at : at + 8, :]), k, sizes[k][1], count)):
+                    if k > 2:
+                        t[field, c, at : at + 8, :] = v
+                    else:
+                        t[field, c, 0:4, :] = v[0:4]
+                        t[field, c, sizes[k][0] - 2 : sizes[k][0] + 2, :] = v[4:8]
+        c0, c1, c2, c3, c4 = (
+            jnp.broadcast_to(scale[:, i : i + 1], (8, 128)) for i in range(field * (LEVELS + 1), (field + 1) * (LEVELS + 1))
+        )
+        pos = (sub.astype(f32) + 0.5) * 0.125
+        high = sub < 4
+        w3 = (jnp.where(high, 0.5 - pos, 0.0) * c3, jnp.where(high, 0.5 + pos, 1.5 - pos) * c3, jnp.where(high, 0.0, pos - 0.5) * c3)
+        half = pos * 0.5
+        w4 = (((0.5 - half) * c4, (0.5 + half) * c4), ((1.0 - half) * c4, half * c4))
+        for part in range(2):
+            begin, end = part * h0 // 2, (part + 1) * h0 // 2
+            for c in range(count):
+                for k, t, u, scaled in ((1, t1, u1, c1), (2, t2, u2, c2)):
+                    f = 1 << k
+                    near = [abs((s + 0.5) / f - 0.5) * scaled for s in range(f)]
+                    own = [(1.0 - abs((s + 0.5) / f - 0.5)) * scaled for s in range(f)]
+                    for at in range(begin >> k, end >> k, 8):
+                        before, centre, after = (t[field, c, at + i : at + i + 8, :] for i in range(3))
+                        for s in range(f):
+                            u[c, pl.ds(f * at + s, 8, f), :] = own[s] * centre + near[s] * (before if s < f // 2 else after)
+                for at in range(begin, end, 8):
+                    tile = at // 8
+                    total = base[at : at + 8, 128 * c : 128 * c + 128] * c0 + u1[c, at : at + 8, :] + u2[c, at : at + 8, :]
+                    for i in range(3):
+                        total = total + w3[i] * jnp.broadcast_to(t3[field, c, tile + i : tile + i + 1, :], (8, 128))
+                    for i in range(2):
+                        row = (tile + 1) // 2 + i
+                        total = total + w4[tile % 2][i] * jnp.broadcast_to(t4[field, c, row : row + 1, :], (8, 128))
+                    buf[at : at + 8, 128 * c : 128 * c + 128] = total
+            rows = pl.ds(begin, end - begin)
+            copy = pltpu.make_async_copy(buf.at[rows], out.at[rows], sems.at[2 * field + part])
             copy.start()
             copies.append(copy)
     for copy in copies:
@@ -411,10 +429,11 @@
     r2 = lax.ppermute(m2, "rows", pairs2)
     r1 = lax.ppermute(m1, "rows", pairs1)
     r3 = lax.ppermute(m2, "rows", pairs3) if mid else m2
-    f_shapes = [(2, up16(h + 2), up128(w)) for h, w in sizes[1:]]
     acc = (2 * LEVELS + 2, 8, 128)
-    s0, b0, f1, f2, sums = call(
-        functools.partial(inner_kernel, sizes), [grid.shape, grid.shape] + f_shapes[:2] + [acc], flops=10**8
+    fine = [(2, z_shapes[0][0], -(-(h + 2) // 8) * 8, 128) for h, _ in sizes[1:]]
+    f_shapes = [(2, 8, up128(w)) for _, w in sizes[1:3]] + [(2, -(-(h + 2) // 8) * 8, up128(w)) for h, w in sizes[3:]]
+    s0, b0, t1, t2, sums = call(
+        functools.partial(inner_kernel, sizes), [grid.shape, grid.shape] + fine[:2] + [acc], flops=10**8
     )(z0, z1, z2)
     s0, b0, f1, f2, f3, f4, sums = call(
         functools.partial(edge_kernel, sizes, mid),
@@ -424,21 +443,18 @@
         + [pltpu.VMEM(blocks(3 * sizes[2][0], sizes[2][1]), f32)]
         + [pltpu.VMEM(blocks(sizes[3][0] + 16, sizes[3][1]), f32)]
         + [pltpu.VMEM(blocks(16, sizes[4][1]), f32), pltpu.VMEM((8, width0), f32)],
-        aliases={7: 0, 8: 1, 9: 2, 10: 3},
-    )(z0, z1, z2, r1, r2, r3, sums, s0, b0, f1, f2)
-    sums = pltpu.with_memory_space_constraint(sums, pltpu.VMEM)
+        aliases={7: 0, 8: 1},
+    )(z0, z1, z2, r1, r2, r3, sums, s0, b0)
     seen = lax.all_to_all(sums, "rows", 0, 0, tiled=True)
-    us = call(
-        functools.partial(spread_kernel, sizes), [(2, h0, width0)] * LEVELS, flops=10**9, limit=16 << 20
-    )(f1, f2, f3, f4)
     cells = [count * h * w for h, w in sizes]
     return tuple(
         call(
-            functools.partial(blend_kernel, cells),
-            [grid.shape, grid.shape],
-            [pltpu.VMEM(grid.shape, f32)] * 2 + [pltpu.SemaphoreType.DMA((4,))],
-            out_specs=[ANY, ANY],
-        )(seen, s0, b0, *us)
+            functools.partial(finish_kernel, sizes, cells),
+            [grid.shape, grid.shape] + fine[:2],
+            [pltpu.VMEM(v, f32) for v in fine[2:] + z_shapes[:1] * 2 + [grid.shape] * 2] + [pltpu.SemaphoreType.DMA((4,))],
+            out_specs=[ANY, ANY, VM, VM],
+            aliases={7: 2, 8: 3},
+        )(seen, s0, b0, f1, f2, f3, f4, t1, t2)[:2]
     )
 
 

time: 23.8 us -> 23.4 us (0.983)
  blocking collectives: 0 us -> 11.2 us
  waiting for transfers between devices: 5.74 us -> 0.01 us
  starting transfers between devices: 10.7 us -> 6.43 us
  Pallas kernels: 6.51 us -> 4.91 us
    all_to_all x0 -> x1, blocking collectives: none -> 11.2 us  [local(): seen = lax.all_to_all(sums, 'rows', 0, 0, tiled=True)]
    all_to_all x1 -> x0, waiting for transfers between devices: 4.89 us -> none  [local(): seen = lax.all_to_all(sums, 'rows', 0, 0, tiled=True)]
    all_to_all x1 -> x0, starting transfers between devices: 4.22 us -> none  [local(): seen = lax.all_to_all(sums, 'rows', 0, 0, tiled=True)]
    pallas_call x5 -> x4, Pallas kernels: 6.51 us -> 4.91 us  [call(): pl.pallas_call(kernel, out_shape=[jax.ShapeDtypeStruct(s, f32) for s in o...]
    ppermute x1, waiting for transfers between devices: 0.85 us -> 0.01 us  [local(): r2 = lax.ppermute(m2, 'rows', pairs2)]
  transfers between devices with their start and end apart: 4 -> 3, of which waited for: 2 -> 0; matrix products, arithmetic and copies ran while one was open for 0% -> 0% of each run, Pallas kernels for 12% -> 7%
where the time goes in v5:
time: 23.4 us; the launch traced here: 23.2 us
  blocking collectives  11.2 us (48%)
  starting transfers between devices  6.43 us (27%)
  Pallas kernels  4.91 us (21%)
  between operations  0.67 us (3%)
    all_to_all x1, blocking collectives, local(): seen = lax.all_to_all(sums, 'rows', 0, 0, tiled=True)  11.2 us
    ppermute x1, starting transfers between devices, local(): r2 = lax.ppermute(m2, 'rows', pairs2)  5.8 us
    pallas_call x4, Pallas kernels, call(): pl.pallas_call(kernel, out_shape=[jax.ShapeDtypeStruct(s, f32) for s in o...  4.91 us
    ppermute x1, starting transfers between devices, local(): r1 = lax.ppermute(m1, 'rows', pairs1)  0.56 us
  transfers between devices with their start and end apart: 3, of which 0 were waited for; matrix products, arithmetic and copies ran while one was open for 0% of the time, Pallas kernels for 7%

profile of v5, /device:TPU:0, one launch (start us, length us, event | category | flops | bytes accessed | tf_op | source)
XLA Modules:
  0.0 23.2 jit_solution(1074766902802550799)
XLA Ops:
  0.6 1.2 %shard_map.30 = (f32[64,128]{1,0:T(8,128)S(1)}, f32[64,128]{1,0:T(8,128)S(1)}, f32[5,64,128]{2,1,0:T(8,128)S(1)}, f32[3,32,128]{2,1,0:T(8,128)S(1)}, f32[2,16,128]{2,1,0:T(8,128)S(1)}) custom-call(f32[64,640]{1,0:T(8,128)} %x_ref.1), custom_call_target="tpu_custom_call" | custom-call | flops 1000000 | bytes 524288 | tf_op jit(solution)/shard_map/pallas_call | solution.py:400
  1.9 0.6 %collective-permute-start = (f32[64,128]{1,0:T(8,128)S(1)}, f32[64,128]{1,0:T(8,128)S(1)}, u32[]{:S(2)}, u32[]{:S(2)}) collective-permute-start(f32[64,128]{1,0:T(8,128)S(1)} %get-tuple-element.24), channel_id=1, source_target_pairs={{0,1},{2,3},{4,5},{6,7},{8,9},{10,11},{12,13},{14,15},{16,17},{18,... | collective-permute-start | bytes 98312 | tf_op jit(solution)/shard_map/ppermute | solution.py:430
  2.4 0.1 collective-permute-start.2
  2.5 5.8 %collective-permute-start.1 = (f32[64,128]{1,0:T(8,128)S(1)}, f32[64,128]{1,0:T(8,128)S(1)}, u32[]{:S(2)}, u32[]{:S(2)}) collective-permute-start(f32[64,128]{1,0:T(8,128)S(1)} %get-tuple-element.25), channel_id=1, source_target_pairs={{1,2},{3,4},{5,6},{7,8},{9,10},{11,12},{13,14},{15,16},{17,18},{19... | collective-permute-start | bytes 98312 | tf_op jit(solution)/shard_map/ppermute | solution.py:429
  8.3 1.6 %shard_map.31 = (f32[64,640]{1,0:T(8,128)S(1)}, f32[64,640]{1,0:T(8,128)S(1)}, f32[2,5,40,128]{3,2,1,0:T(8,128)S(1)}, f32[2,5,24,128]{3,2,1,0:T(8,128)S(1)}, f32[10,8,128]{2,1,0:T(8,128)S(1)}) custom-call(f32[5,64,128]{2,1,0:T(8,128)S(1)} %get-tuple-element.21.z0, f32[3,32,128]{2,1,0:T(8,128)S(1)} %get-tuple-element.22.z1, ...), custom_call_target="tpu_custom_call" | custom-call | flops 100000000 | bytes 524288 | tf_op jit(solution)/shard_map/pallas_call | solution.py:400
  9.9 0.0 collective-permute-done.r1_ref
  9.9 0.0 collective-permute-done.2.r3_ref
  9.9 0.0 collective-permute-done.1.r2_ref
  9.9 0.8 %shard_map.32 = (f32[64,640]{1,0:T(8,128)S(1)}, f32[64,640]{1,0:T(8,128)S(1)}, f32[2,8,384]{2,1,0:T(8,128)S(1)}, f32[2,8,256]{2,1,0:T(8,128)S(1)}, f32[2,16,128]...) custom-call(f32[5,64,128]{2,1,0:T(8,128)S(1)} %get-tuple-element.21., ...), custom_call_target="tpu_custom_call", output_to_operand_aliasing={{0}: (7, {}), {1}: (8, {})} | custom-call | flops 1000000 | bytes 524288 | tf_op jit(solution)/shard_map/pallas_call | solution.py:400
  10.7 11.2 %all_to_all.5.v_ref = f32[32,1,128]{2,1,0:T(1,128)S(1)} all-to-all(f32[32,1,128]{2,1,0:T(1,128)S(1)} %get-tuple-element.29), channel_id=1, replica_groups=mesh['rows'=32] {'rows'}, dimensions={0} | all-to-all | bytes 32768 | tf_op jit(solution)/shard_map/all_to_all | solution.py:448
  21.9 1.3 %shard_map.33 = (f32[64,640]{1,0:T(8,128)}, f32[64,640]{1,0:T(8,128)}, f32[2,5,40,128]{3,2,1,0:T(8,128)S(1)}, f32[2,5,24,128]{3,2,1,0:T(8,128)S(1)}) custom-call(f32[32,1,128]{2,1,0:T(1,128)S(1)} %all_to_all.5.v_ref, f32[64,640]{1,0:T(8,128)S(1)} %get-tuple-element.30.s0, ...), custom_call_target="tpu_custom_call", output_to_operand_aliasing={{2}: (7, {}), {3}: (8, {})} | custom-call | flops 1000000 | bytes 524288 | tf_op jit(solution)/shard_map/pallas_call | solution.py:400
Async XLA Ops:
  1.9 8.0 %collective-permute-start = (f32[64,128]{1,0:T(8,128)S(1)}, f32[64,128]{1,0:T(8,128)S(1)}, u32[]{:S(2)}, u32[]{:S(2)}) collective-permute-start(f32[64,128]{1,0:T(8,128)S(1)} %get-tuple-element.24), channel_id=1, source_target_pairs={{0,1},{2,3},{4,5},{6,7},{8,9},{10,11},{12,13},{14,15},{16,17},{18,... | collective-permute-start | bytes 98312 | tf_op jit(solution)/shard_map/ppermute | solution.py:430
  2.4 7.5 %collective-permute-start.2 = (f32[64,128]{1,0:T(8,128)S(1)}, f32[64,128]{1,0:T(8,128)S(1)}, u32[]{:S(2)}, u32[]{:S(2)}) collective-permute-start(f32[64,128]{1,0:T(8,128)S(1)} %get-tuple-element.25), channel_id=1, source_target_pairs={{0,1},{2,3},{4,5},{6,7},{8,9},{10,11},{12,13},{14,15},{16,17},{18,... | collective-permute-start | bytes 98312 | tf_op jit(solution)/shard_map/ppermute | solution.py:431
  2.5 7.4 %collective-permute-start.1 = (f32[64,128]{1,0:T(8,128)S(1)}, f32[64,128]{1,0:T(8,128)S(1)}, u32[]{:S(2)}, u32[]{:S(2)}) collective-permute-start(f32[64,128]{1,0:T(8,128)S(1)} %get-tuple-element.25), channel_id=1, source_target_pairs={{1,2},{3,4},{5,6},{7,8},{9,10},{11,12},{13,14},{15,16},{17,18},{19... | collective-permute-start | bytes 98312 | tf_op jit(solution)/shard_map/ppermute | solution.py:429

commit v6 on v5

--- a/solution.py
+++ b/solution.py
@@ -122,13 +122,14 @@
     put(row, z2, 0, 0, sizes[2][0])
 
 
-def relief(upper, middle, lower, width, spacing):
+def relief(upper, middle, lower, width, spacing, sides=None):
     diff = lower - upper
-    ends = lower + upper
-    tall = ends + 2.0 * middle
-    m_e, m_w = east(middle, width), west(middle)
-    d_e, d_w = east(diff, width), west(diff)
-    p = (east(tall, width) - west(tall)) * (1.0 / (8.0 * spacing))
+    if sides is None:
+        tall = lower + upper + 2.0 * middle
+        (d_w, m_w, t_w), (d_e, m_e, t_e) = ([west(v) for v in (diff, middle, tall)], [east(v, width) for v in (diff, middle, tall)])
+    else:
+        (d_w, m_w, t_w), (d_e, m_e, t_e) = ((c - a, b, c + a + 2.0 * b) for a, b, c in sides)
+    p = (t_e - t_w) * (1.0 / (8.0 * spacing))
     q = (d_e + d_w + 2.0 * diff) * (1.0 / (8.0 * spacing))
     inv = 1.0 / (spacing * spacing)
     r = ((m_e - middle) - (middle - m_w)) * inv
@@ -183,10 +184,10 @@
             s_sum = fs if at == 0 else s_sum + fs
             b_sum = fb if at == 0 else b_sum + fb
         acc_ref[k] = s_sum
-        acc_ref[LEVELS + 1 + k] = b_sum
-    for k in range(3, LEVELS + 1):
+        acc_ref[LEVELS + k] = b_sum
+    for k in range(3, LEVELS):
         acc_ref[k] = jnp.zeros((8, 128), f32)
-        acc_ref[LEVELS + 1 + k] = jnp.zeros((8, 128), f32)
+        acc_ref[LEVELS + k] = jnp.zeros((8, 128), f32)
 
 
 def edge_kernel(sizes, mid, z0, z1, z2, r1_ref, r2_ref, r3_ref, acc_ref, s0_in, b0_in,
@@ -246,19 +247,24 @@
     row = row_of(v) - 6
     v = jnp.where(first & (row < 0), v[6:7], jnp.where(last & (row >= h3), v[h3 + 5 : h3 + 6], v))
     w3[0] = v
-    h4, _ = sizes[4]
-    v = cols_coarsen(pad_rows(rows_sum(w3, 0, h4 + 4)), width3)
+    h4, width4 = sizes[4]
+    v = pad_rows(rows_sum(w3, 0, h4 + 4))
     row = row_of(v) - 2
-    v = jnp.where(first & (row < 0), v[2:3], jnp.where(last & (row >= h4), v[h4 + 1 : h4 + 2], v))
-    w4[0, 0:8, :] = v
-    w4[0, 8:16, :] = v
+    column = lane_of(v) & 63
+    for i, step in enumerate((0, -1, 1)):
+        at = 2 * jnp.clip(column + step, 0, width4 - 1)
+        taps = [lanes(v, jnp.clip(at + tap, 0, width3 - 1)) for tap in (-2, -1, 0, 1, 2)]
+        level = (taps[0] + taps[4]) * 0.0625 + (taps[1] + taps[3]) * 0.25 + taps[2] * 0.375
+        level = jnp.where(first & (row < 0), level[2:3], jnp.where(last & (row >= h4), level[h4 + 1 : h4 + 2], level))
+        w4[i, 0:8, :] = level
+        w4[i, 8:16, :] = level
 
     totals = []
 
     def add(k, slope, bend, kept):
         kept = kept & (lane_of(slope) < sizes[k][1])
         totals.append((acc_ref[k] + fold(jnp.where(kept, slope, 0.0)),
-                       acc_ref[LEVELS + 1 + k] + fold(jnp.where(kept, bend * bend, 0.0))))
+                       acc_ref[LEVELS + k] + fold(jnp.where(kept, bend * bend, 0.0))))
 
     def ends(top, top_at, bottom, bottom_at):
         a, b = take(top, top_at, 8), take(bottom, bottom_at - 4, 8)
@@ -276,19 +282,31 @@
         for field, v in enumerate((slope, bend)):
             row = row_of(v)
             v = jnp.where(first & (row == 0), v[1:2], jnp.where(last & (row == 7), v[6:7], v))
-            f[field] = v
+            for c, part in enumerate(cols_refine(split(v), k, width, f.shape[1])):
+                f[field, c] = part
     for k, z, at, f in ((3, w3, 5, f3), (4, w4, 1, f4)):
         h, width = sizes[k]
         rows = -(-(h + 2) // 8) * 8
-        slope, bend = relief(take(z, at - 1, rows), take(z, at, rows), take(z, at + 1, rows), width, float(2**k))
+        if k == 3:
+            slope, bend = relief(take(z, at - 1, rows), take(z, at, rows), take(z, at + 1, rows), width, float(2**k))
+        else:
+            around = [[z[i, at + j : at + j + rows, :] for j in (-1, 0, 1)] for i in range(3)]
+            slope, bend = relief(*around[0], width, float(2**k), around[1:])
         row = row_of(slope) - 1
-        add(k, slope, bend, (row >= 0) & (row < h))
+        if k == 3:
+            add(k, slope, bend, (row >= 0) & (row < h))
+        else:
+            kept = (row >= 0) & (row < h)
+            slope4, bend4 = jnp.where(kept, slope, 0.0), jnp.where(kept, bend * bend, 0.0)
         for field, v in enumerate((slope, bend)):
             v = jnp.where(first & (row < 0), v[1:2], jnp.where(last & (row >= h), v[h : h + 1], v))
             f[field, 0:rows, :] = jnp.where(row <= h, v, 0.0)
     table = jnp.zeros((8, 128), f32)
-    for i, v in enumerate([t[0] for t in totals] + [t[1] for t in totals]):
-        table = jnp.where(lane_of(table) == i, jnp.sum(v, axis=1, keepdims=True), table)
+    lane = lane_of(table)
+    for k, pair in enumerate(totals):
+        for field, v in enumerate(pair):
+            table = jnp.where(lane == 64 * field + width4 + k, jnp.sum(v, axis=1, keepdims=True), table)
+    table = jnp.where((lane & 63) < width4, jnp.where(lane < 64, slope4, bend4), table)
     line = jnp.sum(table, axis=0, keepdims=True)
     sum_ref[...] = jnp.broadcast_to(line.reshape(1, 1, 128), sum_ref.shape)
 
@@ -323,54 +341,54 @@
     return out
 
 
-def finish_kernel(sizes, cells, v_ref, s0, b0, f1, f2, f3, f4, t1_in, t2_in, slope_ref, bend_ref, t1, t2, t3, t4, u1, u2, slope_buf, bend_buf, sems):
+def finish_kernel(sizes, cells, v_ref, s0, b0, f1, f2, f3, f4, t1_in, t2_in, slope_ref, bend_ref, t1, t2, t3, t4, u1, u2, u3, u4, slope_buf, bend_buf, sems):
     h0, width0 = sizes[0]
     count = width0 // 128
-    sums = jnp.sum(v_ref[...], axis=0)
+    sums = jnp.sum(v_ref[...], axis=0, keepdims=True)
     lane = lax.broadcasted_iota(jnp.int32, (1, 128), 1)
+    slot = sizes[LEVELS][1]
     number = jnp.ones((1, 128), f32)
     for k, c in enumerate(cells):
-        number = jnp.where((lane == k) | (lane == k + LEVELS + 1), float(c), number)
+        number = jnp.where((lane & 63) == slot + k, float(c), number)
+    last = [
+        jnp.sum(jnp.where((lane >= at) & (lane < at + slot), sums, 0.0), axis=1, keepdims=True) for at in (0, 64)
+    ]
+    sums = jnp.where(lane == slot + LEVELS, last[0], jnp.where(lane == 64 + slot + LEVELS, last[1], sums))
     mean = sums / number
-    scale = jnp.where(lane <= LEVELS, 1.0 / (mean + EPS), 1.0 / jnp.sqrt(mean + EPS))
-    sub = lax.broadcasted_iota(jnp.int32, (8, 128), 0)
+    scale = jnp.where(lane < 64, 1.0 / (mean + EPS), 1.0 / jnp.sqrt(mean + EPS))
+    for field in range(2):
+        for k, f, t in ((1, f1, t1), (2, f2, t2)):
+            for c in range(count):
+                t[field, c, 0:4, :] = f[field, c, 0:4, :]
+                t[field, c, sizes[k][0] - 2 : sizes[k][0] + 2, :] = f[field, c, 4:8, :]
+        for k, f, t in ((4, f4, t4), (3, f3, t3)):
+            for at in range(0, f.shape[1], 8):
+                for c, v in enumerate(cols_refine(split(f[field, at : at + 8, :]), k, sizes[k][1], count)):
+                    t[field, c, at : at + 8, :] = v
+        for k, t, u in ((1, t1, u1), (2, t2, u2), (3, t3, u3)):
+            f = 1 << k
+            for c in range(count):
+                for at in range(0, sizes[k][0], 8):
+                    before, centre, after = (t[field, c, at + i : at + i + 8, :] for i in range(3))
+                    for s in range(f):
+                        near = abs((s + 0.5) / f - 0.5)
+                        u[field, c, pl.ds(f * at + s, 8, f), :] = (1.0 - near) * centre + near * (before if s < f // 2 else after)
+        pos = (lax.broadcasted_iota(jnp.int32, (8, 128), 0).astype(f32) + 0.5) * 0.0625
+        for c in range(count):
+            for at in range(0, h0, 16):
+                a, b, d = (jnp.broadcast_to(t4[field, c, at // 16 + i : at // 16 + i + 1, :], (8, 128)) for i in range(3))
+                u4[field, c, at : at + 8, :] = (0.5 - pos) * a + (0.5 + pos) * b
+                u4[field, c, at + 8 : at + 16, :] = (1.0 - pos) * b + pos * d
     copies = []
     for field, (base, buf, out) in enumerate(((s0, slope_buf, slope_ref), (b0, bend_buf, bend_ref))):
-        for k, f, t in ((4, f4, t4), (3, f3, t3), (2, f2, t2), (1, f1, t1)):
-            for at in range(0, f.shape[1], 8):
-                for c, v in enumerate(cols_refine(split(f[field, at : at + 8, :]), k, sizes[k][1], count)):
-                    if k > 2:
-                        t[field, c, at : at + 8, :] = v
-                    else:
-                        t[field, c, 0:4, :] = v[0:4]
-                        t[field, c, sizes[k][0] - 2 : sizes[k][0] + 2, :] = v[4:8]
-        c0, c1, c2, c3, c4 = (
-            jnp.broadcast_to(scale[:, i : i + 1], (8, 128)) for i in range(field * (LEVELS + 1), (field + 1) * (LEVELS + 1))
-        )
-        pos = (sub.astype(f32) + 0.5) * 0.125
-        high = sub < 4
-        w3 = (jnp.where(high, 0.5 - pos, 0.0) * c3, jnp.where(high, 0.5 + pos, 1.5 - pos) * c3, jnp.where(high, 0.0, pos - 0.5) * c3)
-        half = pos * 0.5
-        w4 = (((0.5 - half) * c4, (0.5 + half) * c4), ((1.0 - half) * c4, half * c4))
+        weights = [jnp.broadcast_to(scale[:, i : i + 1], (8, 128)) for i in range(64 * field + slot, 64 * field + slot + LEVELS + 1)]
         for part in range(2):
             begin, end = part * h0 // 2, (part + 1) * h0 // 2
             for c in range(count):
-                for k, t, u, scaled in ((1, t1, u1, c1), (2, t2, u2, c2)):
-                    f = 1 << k
-                    near = [abs((s + 0.5) / f - 0.5) * scaled for s in range(f)]
-                    own = [(1.0 - abs((s + 0.5) / f - 0.5)) * scaled for s in range(f)]
-                    for at in range(begin >> k, end >> k, 8):
-                        before, centre, after = (t[field, c, at + i : at + i + 8, :] for i in range(3))
-                        for s in range(f):
-                            u[c, pl.ds(f * at + s, 8, f), :] = own[s] * centre + near[s] * (before if s < f // 2 else after)
                 for at in range(begin, end, 8):
-                    tile = at // 8
-                    total = base[at : at + 8, 128 * c : 128 * c + 128] * c0 + u1[c, at : at + 8, :] + u2[c, at : at + 8, :]
-                    for i in range(3):
-                        total = total + w3[i] * jnp.broadcast_to(t3[field, c, tile + i : tile + i + 1, :], (8, 128))
-                    for i in range(2):
-                        row = (tile + 1) // 2 + i
-                        total = total + w4[tile % 2][i] * jnp.broadcast_to(t4[field, c, row : row + 1, :], (8, 128))
+                    total = base[at : at + 8, 128 * c : 128 * c + 128] * weights[0]
+                    for weight, u in zip(weights[1:], (u1, u2, u3, u4)):
+                        total = total + u[field, c, at : at + 8, :] * weight
                     buf[at : at + 8, 128 * c : 128 * c + 128] = total
             rows = pl.ds(begin, end - begin)
             copy = pltpu.make_async_copy(buf.at[rows], out.at[rows], sems.at[2 * field + part])
@@ -429,9 +447,9 @@
     r2 = lax.ppermute(m2, "rows", pairs2)
     r1 = lax.ppermute(m1, "rows", pairs1)
     r3 = lax.ppermute(m2, "rows", pairs3) if mid else m2
-    acc = (2 * LEVELS + 2, 8, 128)
+    acc = (2 * LEVELS, 8, 128)
     fine = [(2, z_shapes[0][0], -(-(h + 2) // 8) * 8, 128) for h, _ in sizes[1:]]
-    f_shapes = [(2, 8, up128(w)) for _, w in sizes[1:3]] + [(2, -(-(h + 2) // 8) * 8, up128(w)) for h, w in sizes[3:]]
+    f_shapes = [(2, z_shapes[0][0], 8, 128)] * 2 + [(2, -(-(h + 2) // 8) * 8, up128(w)) for h, w in sizes[3:]]
     s0, b0, t1, t2, sums = call(
         functools.partial(inner_kernel, sizes), [grid.shape, grid.shape] + fine[:2] + [acc], flops=10**8
     )(z0, z1, z2)
@@ -442,16 +460,16 @@
         + [pltpu.VMEM(blocks(rows, sizes[k][1]), f32) for k in range(2) for rows in (24, 24)]
         + [pltpu.VMEM(blocks(3 * sizes[2][0], sizes[2][1]), f32)]
         + [pltpu.VMEM(blocks(sizes[3][0] + 16, sizes[3][1]), f32)]
-        + [pltpu.VMEM(blocks(16, sizes[4][1]), f32), pltpu.VMEM((8, width0), f32)],
+        + [pltpu.VMEM((3, 16, 128), f32), pltpu.VMEM((8, width0), f32)],
         aliases={7: 0, 8: 1},
     )(z0, z1, z2, r1, r2, r3, sums, s0, b0)
-    seen = lax.all_to_all(sums, "rows", 0, 0, tiled=True)
+    seen = lax.all_to_all(sums, "rows", 0, 0, tiled=True).reshape(count, 128)
     cells = [count * h * w for h, w in sizes]
     return tuple(
         call(
             functools.partial(finish_kernel, sizes, cells),
             [grid.shape, grid.shape] + fine[:2],
-            [pltpu.VMEM(v, f32) for v in fine[2:] + z_shapes[:1] * 2 + [grid.shape] * 2] + [pltpu.SemaphoreType.DMA((4,))],
+            [pltpu.VMEM(v, f32) for v in fine[2:] + [(2, *z_shapes[0])] * 4 + [grid.shape] * 2] + [pltpu.SemaphoreType.DMA((4,))],
             out_specs=[ANY, ANY, VM, VM],
             aliases={7: 2, 8: 3},
         )(seen, s0, b0, f1, f2, f3, f4, t1, t2)[:2]

time: 23.4 us -> 23.1 us (0.987)
  Pallas kernels: 4.91 us -> 4.63 us
    pallas_call x4, Pallas kernels: 4.91 us -> 4.63 us  [call(): pl.pallas_call(kernel, out_shape=[jax.ShapeDtypeStruct(s, f32) for s in o...]
where the time goes in v6:
time: 23.1 us; the launch traced here: 22.9 us
  blocking collectives  11.2 us (48%)
  starting transfers between devices  6.43 us (28%)
  Pallas kernels  4.63 us (20%)
  between operations  0.67 us (3%)
    all_to_all x1, blocking collectives, local(): seen = lax.all_to_all(sums, 'rows', 0, 0, tiled=True).reshape(count, 128)  11.2 us
    ppermute x1, starting transfers between devices, local(): r2 = lax.ppermute(m2, 'rows', pairs2)  5.8 us
    pallas_call x4, Pallas kernels, call(): pl.pallas_call(kernel, out_shape=[jax.ShapeDtypeStruct(s, f32) for s in o...  4.63 us
    ppermute x1, starting transfers between devices, local(): r1 = lax.ppermute(m1, 'rows', pairs1)  0.56 us
  transfers between devices with their start and end apart: 3, of which 0 were waited for; matrix products, arithmetic and copies ran while one was open for 0% of the time, Pallas kernels for 7%

profile of v6, /device:TPU:0, one launch (start us, length us, event | category | flops | bytes accessed | tf_op | source)
XLA Modules:
  0.0 22.9 jit_solution(3717592748508457878)
XLA Ops:
  0.6 1.2 %shard_map.30 = (f32[64,128]{1,0:T(8,128)S(1)}, f32[64,128]{1,0:T(8,128)S(1)}, f32[5,64,128]{2,1,0:T(8,128)S(1)}, f32[3,32,128]{2,1,0:T(8,128)S(1)}, f32[2,16,128]{2,1,0:T(8,128)S(1)}) custom-call(f32[64,640]{1,0:T(8,128)} %x_ref.1), custom_call_target="tpu_custom_call" | custom-call | flops 1000000 | bytes 524288 | tf_op jit(solution)/shard_map/pallas_call | solution.py:418
  1.9 0.6 %collective-permute-start = (f32[64,128]{1,0:T(8,128)S(1)}, f32[64,128]{1,0:T(8,128)S(1)}, u32[]{:S(2)}, u32[]{:S(2)}) collective-permute-start(f32[64,128]{1,0:T(8,128)S(1)} %get-tuple-element.24), channel_id=1, source_target_pairs={{0,1},{2,3},{4,5},{6,7},{8,9},{10,11},{12,13},{14,15},{16,17},{18,... | collective-permute-start | bytes 98312 | tf_op jit(solution)/shard_map/ppermute | solution.py:448
  2.4 0.1 collective-permute-start.2
  2.5 5.8 %collective-permute-start.1 = (f32[64,128]{1,0:T(8,128)S(1)}, f32[64,128]{1,0:T(8,128)S(1)}, u32[]{:S(2)}, u32[]{:S(2)}) collective-permute-start(f32[64,128]{1,0:T(8,128)S(1)} %get-tuple-element.25), channel_id=1, source_target_pairs={{1,2},{3,4},{5,6},{7,8},{9,10},{11,12},{13,14},{15,16},{17,18},{19... | collective-permute-start | bytes 98312 | tf_op jit(solution)/shard_map/ppermute | solution.py:447
  8.3 1.6 %shard_map.31 = (f32[64,640]{1,0:T(8,128)S(1)}, f32[64,640]{1,0:T(8,128)S(1)}, f32[2,5,40,128]{3,2,1,0:T(8,128)S(1)}, f32[2,5,24,128]{3,2,1,0:T(8,128)S(1)}, f32[8,8,128]{2,1,0:T(8,128)S(1)}) custom-call(f32[5,64,128]{2,1,0:T(8,128)S(1)} %get-tuple-element.21.z0, f32[3,32,128]{2,1,0:T(8,128)S(1)} %get-tuple-element.22.z1, f32[2,16,128]{2,1,0:T(8,128)S(1)} %get-tuple-element.23.z2), custom_call_target="tpu_custom_call" | custom-call | flops 100000000 | bytes 524288 | tf_op jit(solution)/shard_map/pallas_call | solution.py:418
  9.9 0.0 collective-permute-done.r1_ref
  9.9 0.0 collective-permute-done.2.r3_ref
  9.9 0.0 collective-permute-done.1.r2_ref
  9.9 0.7 %shard_map.32 = (f32[64,640]{1,0:T(8,128)S(1)}, f32[64,640]{1,0:T(8,128)S(1)}, f32[2,5,8,128]{3,2,1,0:T(8,128)S(1)}, f32[2,5,8,128]{3,2,1,0:T(8,128)S(1)}, f32[2...) custom-call(f32[5,64,128]{2,1,0:T(8,128)S(1)} %get-tuple-element.21., ...), custom_call_target="tpu_custom_call", output_to_operand_aliasing={{0}: (7, {}), {1}: (8, {})} | custom-call | flops 1000000 | bytes 524288 | tf_op jit(solution)/shard_map/pallas_call | solution.py:418
  10.6 11.2 %all_to_all.5 = f32[32,1,128]{2,1,0:T(1,128)S(1)} all-to-all(f32[32,1,128]{2,1,0:T(1,128)S(1)} %get-tuple-element.29), channel_id=1, replica_groups=mesh['rows'=32] {'rows'}, dimensions={0} | all-to-all | bytes 32768 | tf_op jit(solution)/shard_map/all_to_all | solution.py:466
  21.8 1.1 %shard_map.33 = (f32[64,640]{1,0:T(8,128)}, f32[64,640]{1,0:T(8,128)}, f32[2,5,40,128]{3,2,1,0:T(8,128)S(1)}, f32[2,5,24,128]{3,2,1,0:T(8,128)S(1)}) custom-call(f32[32,128]{1,0:T(8,128)S(1)} %bitcast.1, f32[64,640]{1,0:T(8,128)S(1)} %get-tuple-element.30.s0, f32[64,640]{1,0:T(8,128)S(1)} %get-tuple-element.31.b0, ...), custom_call_target="tpu_custom_call", output_to_operand_aliasing={{2}: (7, {}), {3}: (8, {})} | custom-call | flops 1000000 | bytes 524288 | tf_op jit(solution)/shard_map/pallas_call | solution.py:418
Async XLA Ops:
  1.9 8.0 %collective-permute-start = (f32[64,128]{1,0:T(8,128)S(1)}, f32[64,128]{1,0:T(8,128)S(1)}, u32[]{:S(2)}, u32[]{:S(2)}) collective-permute-start(f32[64,128]{1,0:T(8,128)S(1)} %get-tuple-element.24), channel_id=1, source_target_pairs={{0,1},{2,3},{4,5},{6,7},{8,9},{10,11},{12,13},{14,15},{16,17},{18,... | collective-permute-start | bytes 98312 | tf_op jit(solution)/shard_map/ppermute | solution.py:448
  2.4 7.5 %collective-permute-start.2 = (f32[64,128]{1,0:T(8,128)S(1)}, f32[64,128]{1,0:T(8,128)S(1)}, u32[]{:S(2)}, u32[]{:S(2)}) collective-permute-start(f32[64,128]{1,0:T(8,128)S(1)} %get-tuple-element.25), channel_id=1, source_target_pairs={{0,1},{2,3},{4,5},{6,7},{8,9},{10,11},{12,13},{14,15},{16,17},{18,... | collective-permute-start | bytes 98312 | tf_op jit(solution)/shard_map/ppermute | solution.py:449
  2.5 7.4 %collective-permute-start.1 = (f32[64,128]{1,0:T(8,128)S(1)}, f32[64,128]{1,0:T(8,128)S(1)}, u32[]{:S(2)}, u32[]{:S(2)}) collective-permute-start(f32[64,128]{1,0:T(8,128)S(1)} %get-tuple-element.25), channel_id=1, source_target_pairs={{1,2},{3,4},{5,6},{7,8},{9,10},{11,12},{13,14},{15,16},{17,18},{19... | collective-permute-start | bytes 98312 | tf_op jit(solution)/shard_map/ppermute | solution.py:447

commit v7 on v6

--- a/solution.py
+++ b/solution.py
@@ -190,8 +190,18 @@
         acc_ref[LEVELS + k] = jnp.zeros((8, 128), f32)
 
 
-def edge_kernel(sizes, mid, z0, z1, z2, r1_ref, r2_ref, r3_ref, acc_ref, s0_in, b0_in,
-                s0_ref, b0_ref, f1, f2, f3, f4, sum_ref, up, lo, t0, e0, t1, e1, w2, w3, w4, tmp):
+def rows_refine(t, u, field, k, height):
+    f = 1 << k
+    for c in range(t.shape[1]):
+        for at in range(0, height, 8):
+            before, centre, after = (t[field, c, at + i : at + i + 8, :] for i in range(3))
+            for s in range(f):
+                near = abs((s + 0.5) / f - 0.5)
+                u[field, c, pl.ds(f * at + s, 8, f), :] = (1.0 - near) * centre + near * (before if s < f // 2 else after)
+
+
+def edge_kernel(sizes, mid, z0, z1, z2, r1_ref, r2_ref, r3_ref, acc_ref, s0_in, b0_in, t1_in, t2_in,
+                s0_ref, b0_ref, t1, t2, u1, u2, f3, f4, sum_ref, up, lo, top0, end0, top1, end1, w2, w3, w4, tmp):
     me = lax.axis_index("rows")
     odd = lax.rem(me, 2) == 1
     first, last = me == 0, me == lax.axis_size("rows") - 1
@@ -203,31 +213,31 @@
 
     h0, width0 = sizes[0]
     for c in range(z0.shape[0]):
-        t0[c, 8:16, :] = z0[c, 0:8, :]
-        t0[c, 4:8, :] = jnp.where(first, jnp.broadcast_to(z0[c, 0:1, :], (4, 128)), up[4 * c : 4 * c + 4, :])
-        e0[c, 8:16, :] = z0[c, h0 - 8 : h0, :]
-        e0[c, 16:20, :] = jnp.where(last, jnp.broadcast_to(z0[c, h0 - 1 : h0, :], (4, 128)), lo[4 * c : 4 * c + 4, :])
+        top0[c, 8:16, :] = z0[c, 0:8, :]
+        top0[c, 4:8, :] = jnp.where(first, jnp.broadcast_to(z0[c, 0:1, :], (4, 128)), up[4 * c : 4 * c + 4, :])
+        end0[c, 8:16, :] = z0[c, h0 - 8 : h0, :]
+        end0[c, 16:20, :] = jnp.where(last, jnp.broadcast_to(z0[c, h0 - 1 : h0, :], (4, 128)), lo[4 * c : 4 * c + 4, :])
     base = 4 * z0.shape[0]
     h1, width1 = sizes[1]
-    tmp[0:3, :] = rows_sum(t0, 4, 3)
-    tmp[3:5, :] = rows_sum(e0, 12, 2)
+    tmp[0:3, :] = rows_sum(top0, 4, 3)
+    tmp[3:5, :] = rows_sum(end0, 12, 2)
     edge = cols_coarsen(tmp[...], width0)
     for c in range(z1.shape[0]):
         part = edge[:, 128 * c : 128 * c + 128]
         row0, end = part[1:2], part[3:4]
-        t1[c, 8:16, :] = z1[c, 0:8, :]
-        t1[c, 8:9, :] = row0
-        t1[c, 7:8, :] = jnp.where(first, row0, part[0:1])
-        t1[c, 4:7, :] = jnp.where(first, jnp.broadcast_to(row0, (3, 128)), up[base + 4 * c + 1 : base + 4 * c + 4, :])
-        e1[c, 8:16, :] = z1[c, h1 - 8 : h1, :]
-        e1[c, 15:16, :] = end
-        e1[c, 16:17, :] = jnp.where(last, end, part[4:5])
-        e1[c, 17:21, :] = jnp.where(last, jnp.broadcast_to(end, (4, 128)), lo[base + 4 * c : base + 4 * c + 4, :])
+        top1[c, 8:16, :] = z1[c, 0:8, :]
+        top1[c, 8:9, :] = row0
+        top1[c, 7:8, :] = jnp.where(first, row0, part[0:1])
+        top1[c, 4:7, :] = jnp.where(first, jnp.broadcast_to(row0, (3, 128)), up[base + 4 * c + 1 : base + 4 * c + 4, :])
+        end1[c, 8:16, :] = z1[c, h1 - 8 : h1, :]
+        end1[c, 15:16, :] = end
+        end1[c, 16:17, :] = jnp.where(last, end, part[4:5])
+        end1[c, 17:21, :] = jnp.where(last, jnp.broadcast_to(end, (4, 128)), lo[base + 4 * c : base + 4 * c + 4, :])
     base += 4 * z1.shape[0]
     h2, width2 = sizes[2]
     wq = up128(width1)
-    tmp[0:3, :wq] = rows_sum(t1, 4, 3)
-    tmp[3:6, :wq] = rows_sum(e1, 12, 3)
+    tmp[0:3, :wq] = rows_sum(top1, 4, 3)
+    tmp[3:6, :wq] = rows_sum(end1, 12, 3)
     edge = cols_coarsen(tmp[:, :wq], width1)
     for c in range(z2.shape[0]):
         part = edge[:, 128 * c : 128 * c + 128]
@@ -270,20 +280,22 @@
         a, b = take(top, top_at, 8), take(bottom, bottom_at - 4, 8)
         return jnp.where(row_of(a) < 4, a, b)
 
-    slope, bend = relief(*(ends(t0, 7 + i, e0, 11 + i) for i in range(3)), width0, 1.0)
+    slope, bend = relief(*(ends(top0, 7 + i, end0, 11 + i) for i in range(3)), width0, 1.0)
     for ref, v in ((s0_ref, slope), (b0_ref, bend)):
         ref[0:4, :] = v[0:4]
         ref[h0 - 4 : h0, :] = v[4:8]
     add(0, slope, bend, (row_of(slope) == 0) | (row_of(slope) == 7))
-    for k, top, bottom, top_at, bottom_at, f in ((1, t1, e1, 7, 13, f1), (2, w2, w2, h2 - 1, 2 * h2 - 3, f2)):
+    for k, top, bottom, top_at, bottom_at, t, u in ((1, top1, end1, 7, 13, t1, u1), (2, w2, w2, h2 - 1, 2 * h2 - 3, t2, u2)):
         h, width = sizes[k]
         slope, bend = relief(*(ends(top, top_at - 1 + i, bottom, bottom_at - 1 + i) for i in range(3)), width, float(2**k))
         add(k, slope, bend, (row_of(slope) > 0) & (row_of(slope) < 7))
         for field, v in enumerate((slope, bend)):
             row = row_of(v)
             v = jnp.where(first & (row == 0), v[1:2], jnp.where(last & (row == 7), v[6:7], v))
-            for c, part in enumerate(cols_refine(split(v), k, width, f.shape[1])):
-                f[field, c] = part
+            for c, part in enumerate(cols_refine(split(v), k, width, t.shape[1])):
+                t[field, c, 0:4, :] = part[0:4]
+                t[field, c, h - 2 : h + 2, :] = part[4:8]
+            rows_refine(t, u, field, k, h)
     for k, z, at, f in ((3, w3, 5, f3), (4, w4, 1, f4)):
         h, width = sizes[k]
         rows = -(-(h + 2) // 8) * 8
@@ -341,7 +353,7 @@
     return out
 
 
-def finish_kernel(sizes, cells, v_ref, s0, b0, f1, f2, f3, f4, t1_in, t2_in, slope_ref, bend_ref, t1, t2, t3, t4, u1, u2, u3, u4, slope_buf, bend_buf, sems):
+def finish_kernel(sizes, cells, v_ref, s0, b0, u1, u2, f3, f4, slope_ref, bend_ref, t3, t4, u3, u4, slope_buf, bend_buf, sems):
     h0, width0 = sizes[0]
     count = width0 // 128
     sums = jnp.sum(v_ref[...], axis=0, keepdims=True)
@@ -357,22 +369,11 @@
     mean = sums / number
     scale = jnp.where(lane < 64, 1.0 / (mean + EPS), 1.0 / jnp.sqrt(mean + EPS))
     for field in range(2):
-        for k, f, t in ((1, f1, t1), (2, f2, t2)):
-            for c in range(count):
-                t[field, c, 0:4, :] = f[field, c, 0:4, :]
-                t[field, c, sizes[k][0] - 2 : sizes[k][0] + 2, :] = f[field, c, 4:8, :]
         for k, f, t in ((4, f4, t4), (3, f3, t3)):
             for at in range(0, f.shape[1], 8):
                 for c, v in enumerate(cols_refine(split(f[field, at : at + 8, :]), k, sizes[k][1], count)):
                     t[field, c, at : at + 8, :] = v
-        for k, t, u in ((1, t1, u1), (2, t2, u2), (3, t3, u3)):
-            f = 1 << k
-            for c in range(count):
-                for at in range(0, sizes[k][0], 8):
-                    before, centre, after = (t[field, c, at + i : at + i + 8, :] for i in range(3))
-                    for s in range(f):
-                        near = abs((s + 0.5) / f - 0.5)
-                        u[field, c, pl.ds(f * at + s, 8, f), :] = (1.0 - near) * centre + near * (before if s < f // 2 else after)
+        rows_refine(t3, u3, field, 3, sizes[3][0])
         pos = (lax.broadcasted_iota(jnp.int32, (8, 128), 0).astype(f32) + 0.5) * 0.0625
         for c in range(count):
             for at in range(0, h0, 16):
@@ -449,11 +450,12 @@
     r3 = lax.ppermute(m2, "rows", pairs3) if mid else m2
     acc = (2 * LEVELS, 8, 128)
     fine = [(2, z_shapes[0][0], -(-(h + 2) // 8) * 8, 128) for h, _ in sizes[1:]]
-    f_shapes = [(2, z_shapes[0][0], 8, 128)] * 2 + [(2, -(-(h + 2) // 8) * 8, up128(w)) for h, w in sizes[3:]]
+    whole = (2, *z_shapes[0])
+    f_shapes = fine[:2] + [whole] * 2 + [(2, -(-(h + 2) // 8) * 8, up128(w)) for h, w in sizes[3:]]
     s0, b0, t1, t2, sums = call(
         functools.partial(inner_kernel, sizes), [grid.shape, grid.shape] + fine[:2] + [acc], flops=10**8
     )(z0, z1, z2)
-    s0, b0, f1, f2, f3, f4, sums = call(
+    s0, b0, _, _, u1, u2, f3, f4, sums = call(
         functools.partial(edge_kernel, sizes, mid),
         [grid.shape, grid.shape] + f_shapes + [(count, 1, 128)],
         [pltpu.VMEM(msg, f32)] * 2
@@ -461,18 +463,17 @@
         + [pltpu.VMEM(blocks(3 * sizes[2][0], sizes[2][1]), f32)]
         + [pltpu.VMEM(blocks(sizes[3][0] + 16, sizes[3][1]), f32)]
         + [pltpu.VMEM((3, 16, 128), f32), pltpu.VMEM((8, width0), f32)],
-        aliases={7: 0, 8: 1},
-    )(z0, z1, z2, r1, r2, r3, sums, s0, b0)
+        aliases={7: 0, 8: 1, 9: 2, 10: 3},
+    )(z0, z1, z2, r1, r2, r3, sums, s0, b0, t1, t2)
     seen = lax.all_to_all(sums, "rows", 0, 0, tiled=True).reshape(count, 128)
     cells = [count * h * w for h, w in sizes]
     return tuple(
         call(
             functools.partial(finish_kernel, sizes, cells),
-            [grid.shape, grid.shape] + fine[:2],
-            [pltpu.VMEM(v, f32) for v in fine[2:] + [(2, *z_shapes[0])] * 4 + [grid.shape] * 2] + [pltpu.SemaphoreType.DMA((4,))],
-            out_specs=[ANY, ANY, VM, VM],
-            aliases={7: 2, 8: 3},
-        )(seen, s0, b0, f1, f2, f3, f4, t1, t2)[:2]
+            [grid.shape, grid.shape],
+            [pltpu.VMEM(v, f32) for v in fine[2:] + [whole] * 2 + [grid.shape] * 2] + [pltpu.SemaphoreType.DMA((4,))],
+            out_specs=[ANY, ANY],
+        )(seen, s0, b0, u1, u2, f3, f4)
     )
 
 

time: 23.1 us -> 23.1 us (level)
  no operation moved by 1% of the time
where the time goes in v7:
time: 23.1 us; the launch traced here: 22.9 us
  blocking collectives  11.2 us (48%)
  starting transfers between devices  6.43 us (28%)
  Pallas kernels  4.63 us (20%)
  between operations  0.67 us (3%)
    all_to_all x1, blocking collectives, local(): seen = lax.all_to_all(sums, 'rows', 0, 0, tiled=True).reshape(count, 128)  11.2 us
    ppermute x1, starting transfers between devices, local(): r2 = lax.ppermute(m2, 'rows', pairs2)  5.8 us
    pallas_call x4, Pallas kernels, call(): pl.pallas_call(kernel, out_shape=[jax.ShapeDtypeStruct(s, f32) for s in o...  4.63 us
    ppermute x1, starting transfers between devices, local(): r1 = lax.ppermute(m1, 'rows', pairs1)  0.56 us
  transfers between devices with their start and end apart: 3, of which 0 were waited for; matrix products, arithmetic and copies ran while one was open for 0% of the time, Pallas kernels for 7%

profile of v7, /device:TPU:0, one launch (start us, length us, event | category | flops | bytes accessed | tf_op | source)
XLA Modules:
  0.0 22.9 jit_solution(16127086186374997286)
XLA Ops:
  0.6 1.2 %shard_map.30 = (f32[64,128]{1,0:T(8,128)S(1)}, f32[64,128]{1,0:T(8,128)S(1)}, f32[5,64,128]{2,1,0:T(8,128)S(1)}, f32[3,32,128]{2,1,0:T(8,128)S(1)}, f32[2,16,128]{2,1,0:T(8,128)S(1)}) custom-call(f32[64,640]{1,0:T(8,128)} %x_ref.1), custom_call_target="tpu_custom_call" | custom-call | flops 1000000 | bytes 524288 | tf_op jit(solution)/shard_map/pallas_call | solution.py:419
  1.9 0.6 %collective-permute-start = (f32[64,128]{1,0:T(8,128)S(1)}, f32[64,128]{1,0:T(8,128)S(1)}, u32[]{:S(2)}, u32[]{:S(2)}) collective-permute-start(f32[64,128]{1,0:T(8,128)S(1)} %get-tuple-element.22), channel_id=1, source_target_pairs={{0,1},{2,3},{4,5},{6,7},{8,9},{10,11},{12,13},{14,15},{16,17},{18,... | collective-permute-start | bytes 98312 | tf_op jit(solution)/shard_map/ppermute | solution.py:449
  2.4 0.1 collective-permute-start.2
  2.5 5.8 %collective-permute-start.1 = (f32[64,128]{1,0:T(8,128)S(1)}, f32[64,128]{1,0:T(8,128)S(1)}, u32[]{:S(2)}, u32[]{:S(2)}) collective-permute-start(f32[64,128]{1,0:T(8,128)S(1)} %get-tuple-element.23), channel_id=1, source_target_pairs={{1,2},{3,4},{5,6},{7,8},{9,10},{11,12},{13,14},{15,16},{17,18},{19... | collective-permute-start | bytes 98312 | tf_op jit(solution)/shard_map/ppermute | solution.py:448
  8.3 1.6 %shard_map.31 = (f32[64,640]{1,0:T(8,128)S(1)}, f32[64,640]{1,0:T(8,128)S(1)}, f32[2,5,40,128]{3,2,1,0:T(8,128)S(1)}, f32[2,5,24,128]{3,2,1,0:T(8,128)S(1)}, f32[8,8,128]{2,1,0:T(8,128)S(1)}) custom-call(f32[5,64,128]{2,1,0:T(8,128)S(1)} %get-tuple-element.19.z0, f32[3,32,128]{2,1,0:T(8,128)S(1)} %get-tuple-element.20.z1, f32[2,16,128]{2,1,0:T(8,128)S(1)} %get-tuple-element.21.z2), custom_call_target="tpu_custom_call" | custom-call | flops 100000000 | bytes 524288 | tf_op jit(solution)/shard_map/pallas_call | solution.py:419
  9.9 0.0 collective-permute-done.r1_ref
  9.9 0.0 collective-permute-done.2.r3_ref
  9.9 0.0 collective-permute-done.1.r2_ref
  9.9 0.7 %shard_map.32 = (f32[64,640]{1,0:T(8,128)S(1)}, f32[64,640]{1,0:T(8,128)S(1)}, f32[2,5,40,128]{3,2,1,0:T(8,128)S(1)}, f32[2,5,24,128]{3,2,1,0:T(8,128)S(1)}, f32...) custom-call(f32[5,64,128]{2,1,0:T(8,128)S(1)} %get-tuple-element.19., ...), custom_call_target="tpu_custom_call", output_to_operand_aliasing={{0}: (7, {}), {1}: (8, {}), {2}: (9, {}), {3}: (10, {})} | custom-call | flops 1000000 | bytes 524288 | tf_op jit(solution)/shard_map/pallas_call | solution.py:419
  10.6 11.2 %all_to_all.5 = f32[32,1,128]{2,1,0:T(1,128)S(1)} all-to-all(f32[32,1,128]{2,1,0:T(1,128)S(1)} %get-tuple-element.29), channel_id=1, replica_groups=mesh['rows'=32] {'rows'}, dimensions={0} | all-to-all | bytes 32768 | tf_op jit(solution)/shard_map/all_to_all | solution.py:468
  21.8 1.1 %shard_map.33 = (f32[64,640]{1,0:T(8,128)}, f32[64,640]{1,0:T(8,128)}) custom-call(f32[32,128]{1,0:T(8,128)S(1)} %bitcast.1, f32[64,640]{1,0:T(8,128)S(1)} %get-tuple-element.30.s0, f32[64,640]{1,0:T(8,128)S(1)} %get-tuple-element.31.b0, f32[2,5,64,128]{3,2,1,0:T(8,128)S(1)} %get-tuple-element.32.u1, f32[2,5,64,128]{3,2,1,0:T(8,128)S(1)} %get-tuple-element.33.u2, ...), custom_call_target="tpu_custom_call" | custom-call | flops 1000000 | bytes 524288 | tf_op jit(solution)/shard_map/pallas_call | solution.py:419
Async XLA Ops:
  1.9 8.0 %collective-permute-start = (f32[64,128]{1,0:T(8,128)S(1)}, f32[64,128]{1,0:T(8,128)S(1)}, u32[]{:S(2)}, u32[]{:S(2)}) collective-permute-start(f32[64,128]{1,0:T(8,128)S(1)} %get-tuple-element.22), channel_id=1, source_target_pairs={{0,1},{2,3},{4,5},{6,7},{8,9},{10,11},{12,13},{14,15},{16,17},{18,... | collective-permute-start | bytes 98312 | tf_op jit(solution)/shard_map/ppermute | solution.py:449
  2.4 7.5 %collective-permute-start.2 = (f32[64,128]{1,0:T(8,128)S(1)}, f32[64,128]{1,0:T(8,128)S(1)}, u32[]{:S(2)}, u32[]{:S(2)}) collective-permute-start(f32[64,128]{1,0:T(8,128)S(1)} %get-tuple-element.23), channel_id=1, source_target_pairs={{0,1},{2,3},{4,5},{6,7},{8,9},{10,11},{12,13},{14,15},{16,17},{18,... | collective-permute-start | bytes 98312 | tf_op jit(solution)/shard_map/ppermute | solution.py:450
  2.5 7.4 %collective-permute-start.1 = (f32[64,128]{1,0:T(8,128)S(1)}, f32[64,128]{1,0:T(8,128)S(1)}, u32[]{:S(2)}, u32[]{:S(2)}) collective-permute-start(f32[64,128]{1,0:T(8,128)S(1)} %get-tuple-element.23), channel_id=1, source_target_pairs={{1,2},{3,4},{5,6},{7,8},{9,10},{11,12},{13,14},{15,16},{17,18},{19... | collective-permute-start | bytes 98312 | tf_op jit(solution)/shard_map/ppermute | solution.py:448

commit v8 on v7

--- a/solution.py
+++ b/solution.py
@@ -52,11 +52,19 @@
         ref[c, at : at + v.shape[0], :] = v[:, 128 * c : 128 * c + 128]
 
 
+def head(a, b, c):
+    return (a * 0.0625 + b * 0.25) + c * 0.375
+
+
+def tail(d, e):
+    return d * 0.25 + e * 0.0625
+
+
 def rows_sum(ref, start, count):
     out = []
     for c in range(ref.shape[0]):
         part = [ref[c, pl.ds(start + a, count, 2), :] for a in range(5)]
-        out.append((part[0] + part[4]) * 0.0625 + (part[1] + part[3]) * 0.25 + part[2] * 0.375)
+        out.append(head(*part[:3]) + tail(*part[3:]))
     return jnp.concatenate(out, axis=1)
 
 
@@ -93,7 +101,7 @@
     return out[0] if len(out) == 1 else jnp.concatenate(out, axis=1)
 
 
-def pyramid_kernel(sizes, x_ref, m1_ref, m2_ref, z0, z1, z2, tmp, sems):
+def pyramid_kernel(sizes, x_ref, m1_ref, m2_ref, z0, z1, z2, tmp, below, above, sems):
     copies = [
         pltpu.make_async_copy(x_ref.at[:, pl.ds(128 * c, 128)], z0.at[c], sems.at[c]) for c in range(z0.shape[0])
     ]
@@ -104,22 +112,32 @@
     for copy in copies:
         copy.wait()
 
-    def put(row, z, top_at, bottom_at, count):
-        for c in range(z.shape[0]):
-            top, bottom = z[c, top_at : top_at + count, :], z[c, bottom_at : bottom_at + count, :]
-            m1_ref[row : row + count, :] = jnp.where(odd, top, bottom)
-            m2_ref[row : row + count, :] = jnp.where(odd, bottom, top)
-            row += count
-        return row
-
-    row = put(0, z0, 0, h - 4, 4)
+    for c in range(z0.shape[0]):
+        above[3 * c : 3 * c + 3, :] = z0[c, 0:3, :]
+        w = [z0[c, h - 4 + i : h - 3 + i, :] for i in range(4)]
+        below[3 * c : 3 * c + 1, :] = head(*w[:3])
+        below[3 * c + 1 : 3 * c + 2, :] = w[2] * 0.0625 + w[3] * 0.25
+        below[3 * c + 2 : 3 * c + 3, :] = w[3]
+    row = 3 * z0.shape[0]
     for k, z in ((0, z1), (1, z2)):
         half, wp = sizes[k + 1][0], up128(sizes[k][1])
         low = k + 1
         tmp[low : half - 1, :wp] = rows_sum((z0, z1)[k], 2 * low - 2, half - 1 - low)
         store(z, 0, cols_coarsen(tmp[0:half, :wp], sizes[k][1]))
-    row = put(row, z1, 1, sizes[1][0] - 5, 4)
-    put(row, z2, 0, 0, sizes[2][0])
+    h1, h2 = sizes[1][0], sizes[2][0]
+    at = row
+    for c in range(z1.shape[0]):
+        above[row + 4 * c : row + 4 * c + 4, :] = z1[c, 1:5, :]
+        w = [z1[c, h1 - 4 + i : h1 - 3 + i, :] for i in range(3)]
+        below[at : at + 1, :] = head(*w)
+        below[at + 1 : at + 2, :] = w[2]
+        at += 2
+    row += 4 * z1.shape[0]
+    for c in range(z2.shape[0]):
+        above[row + 9 * c : row + 9 * c + 9, :] = z2[c, 2:11, :]
+        below[at + 13 * c : at + 13 * c + 13, :] = z2[c, h2 - 14 : h2 - 1, :]
+    m1_ref[...] = jnp.where(odd, above[...], below[...])
+    m2_ref[...] = jnp.where(odd, below[...], above[...])
 
 
 def relief(upper, middle, lower, width, spacing, sides=None):
@@ -213,13 +231,17 @@
 
     h0, width0 = sizes[0]
     for c in range(z0.shape[0]):
+        block = slice(128 * c, 128 * c + 128)
+        w = [z0[c, i : i + 1, :] for i in range(3)]
         top0[c, 8:16, :] = z0[c, 0:8, :]
-        top0[c, 4:8, :] = jnp.where(first, jnp.broadcast_to(z0[c, 0:1, :], (4, 128)), up[4 * c : 4 * c + 4, :])
+        top0[c, 7:8, :] = jnp.where(first, w[0], up[3 * c + 2 : 3 * c + 3, :])
+        tmp[0:1, block] = up[3 * c : 3 * c + 1, :] + tail(up[3 * c + 2 : 3 * c + 3, :], w[0])
+        start = jnp.where(first, w[0] * 0.0625 + w[0] * 0.25, up[3 * c + 1 : 3 * c + 2, :])
+        tmp[1:2, block] = (start + w[0] * 0.375) + tail(w[1], w[2])
         end0[c, 8:16, :] = z0[c, h0 - 8 : h0, :]
-        end0[c, 16:20, :] = jnp.where(last, jnp.broadcast_to(z0[c, h0 - 1 : h0, :], (4, 128)), lo[4 * c : 4 * c + 4, :])
-    base = 4 * z0.shape[0]
+        end0[c, 16:19, :] = jnp.where(last, jnp.broadcast_to(z0[c, h0 - 1 : h0, :], (3, 128)), lo[3 * c : 3 * c + 3, :])
+    base = 3 * z0.shape[0]
     h1, width1 = sizes[1]
-    tmp[0:3, :] = rows_sum(top0, 4, 3)
     tmp[3:5, :] = rows_sum(end0, 12, 2)
     edge = cols_coarsen(tmp[...], width0)
     for c in range(z1.shape[0]):
@@ -228,24 +250,26 @@
         top1[c, 8:16, :] = z1[c, 0:8, :]
         top1[c, 8:9, :] = row0
         top1[c, 7:8, :] = jnp.where(first, row0, part[0:1])
-        top1[c, 4:7, :] = jnp.where(first, jnp.broadcast_to(row0, (3, 128)), up[base + 4 * c + 1 : base + 4 * c + 4, :])
+        top1[c, 6:7, :] = jnp.where(first, row0, up[base + 2 * c + 1 : base + 2 * c + 2, :])
         end1[c, 8:16, :] = z1[c, h1 - 8 : h1, :]
         end1[c, 15:16, :] = end
         end1[c, 16:17, :] = jnp.where(last, end, part[4:5])
         end1[c, 17:21, :] = jnp.where(last, jnp.broadcast_to(end, (4, 128)), lo[base + 4 * c : base + 4 * c + 4, :])
-    base += 4 * z1.shape[0]
     h2, width2 = sizes[2]
     wq = up128(width1)
-    tmp[0:3, :wq] = rows_sum(top1, 4, 3)
+    for c in range(z1.shape[0]):
+        tmp[0:1, 128 * c : 128 * c + 128] = up[base + 2 * c : base + 2 * c + 1, :] + tail(top1[c, 7:8, :], top1[c, 8:9, :])
+    tmp[1:3, :wq] = rows_sum(top1, 6, 2)
     tmp[3:6, :wq] = rows_sum(end1, 12, 3)
     edge = cols_coarsen(tmp[:, :wq], width1)
     for c in range(z2.shape[0]):
         part = edge[:, 128 * c : 128 * c + 128]
         row0, end = part[1:2], part[3:4]
-        at = base + h2 * c
-        w2[c, 0:h2, :] = jnp.where(first, jnp.broadcast_to(row0, (h2, 128)), up[at : at + h2, :])
+        at = base + 2 * z1.shape[0] + 13 * c
+        w2[c, h2 - 14 : h2 - 1, :] = jnp.where(first, jnp.broadcast_to(row0, (13, 128)), up[at : at + 13, :])
         w2[c, h2 : 2 * h2, :] = z2[c]
-        w2[c, 2 * h2 : 3 * h2, :] = jnp.where(last, jnp.broadcast_to(end, (h2, 128)), lo[at : at + h2, :])
+        at = base + 4 * z1.shape[0] + 9 * c
+        w2[c, 2 * h2 + 2 : 2 * h2 + 11, :] = jnp.where(last, jnp.broadcast_to(end, (9, 128)), lo[at : at + 9, :])
         w2[c, h2 - 1 : h2, :] = jnp.where(first, row0, part[0:1])
         w2[c, h2 : h2 + 2, :] = part[1:3]
         w2[c, 2 * h2 - 1 : 2 * h2, :] = end
@@ -437,11 +461,12 @@
         return (up128(width) // 128, -(-rows // 8) * 8, 128)
 
     z_shapes = [blocks(*size) for size in sizes]
-    msg = (4 * z_shapes[0][0] + 4 * z_shapes[1][0] + sizes[2][0] * z_shapes[2][0], 128)
+    rows = 3 * z_shapes[0][0] + max(2 * z_shapes[1][0] + 13 * z_shapes[2][0], 4 * z_shapes[1][0] + 9 * z_shapes[2][0])
+    msg = (-(-rows // 8) * 8, 128)
     m1, m2, z0, z1, z2 = call(
         functools.partial(pyramid_kernel, sizes),
         [msg, msg] + z_shapes[:3],
-        [pltpu.VMEM((h0 // 2, width0), f32), pltpu.SemaphoreType.DMA((z_shapes[0][0],))],
+        [pltpu.VMEM((h0 // 2, width0), f32)] + [pltpu.VMEM(msg, f32)] * 2 + [pltpu.SemaphoreType.DMA((z_shapes[0][0],))],
         in_specs=[pl.BlockSpec(memory_space=pltpu.HBM)],
     )(pltpu.with_memory_space_constraint(grid, pltpu.HBM))
     pairs1, pairs2, pairs3, mid = halo_pairs(count)

time: 23.1 us -> 23.1 us (level)
  no operation moved by 1% of the time
where the time goes in v8:
time: 23.1 us; the launch traced here: 22.9 us
  blocking collectives  11.1 us (48%)
  starting transfers between devices  6.43 us (28%)
  Pallas kernels  4.65 us (20%)
  between operations  0.67 us (3%)
    all_to_all x1, blocking collectives, local(): seen = lax.all_to_all(sums, 'rows', 0, 0, tiled=True).reshape(count, 128)  11.1 us
    ppermute x1, starting transfers between devices, local(): r2 = lax.ppermute(m2, 'rows', pairs2)  5.8 us
    pallas_call x4, Pallas kernels, call(): pl.pallas_call(kernel, out_shape=[jax.ShapeDtypeStruct(s, f32) for s in o...  4.65 us
    ppermute x1, starting transfers between devices, local(): r1 = lax.ppermute(m1, 'rows', pairs1)  0.56 us
  transfers between devices with their start and end apart: 3, of which 0 were waited for; matrix products, arithmetic and copies ran while one was open for 0% of the time, Pallas kernels for 7%

profile of v8, /device:TPU:0, one launch (start us, length us, event | category | flops | bytes accessed | tf_op | source)
XLA Modules:
  0.0 22.9 jit_solution(7156206643386909107)
XLA Ops:
  0.6 1.2 %shard_map.30 = (f32[48,128]{1,0:T(8,128)S(1)}, f32[48,128]{1,0:T(8,128)S(1)}, f32[5,64,128]{2,1,0:T(8,128)S(1)}, f32[3,32,128]{2,1,0:T(8,128)S(1)}, f32[2,16,128]{2,1,0:T(8,128)S(1)}) custom-call(f32[64,640]{1,0:T(8,128)} %x_ref.1), custom_call_target="tpu_custom_call" | custom-call | flops 1000000 | bytes 524288 | tf_op jit(solution)/shard_map/pallas_call | solution.py:443
  1.9 0.6 %collective-permute-start = (f32[48,128]{1,0:T(8,128)S(1)}, f32[48,128]{1,0:T(8,128)S(1)}, u32[]{:S(2)}, u32[]{:S(2)}) collective-permute-start(f32[48,128]{1,0:T(8,128)S(1)} %get-tuple-element.22), channel_id=1, source_target_pairs={{0,1},{2,3},{4,5},{6,7},{8,9},{10,11},{12,13},{14,15},{16,17},{18,... | collective-permute-start | bytes 73736 | tf_op jit(solution)/shard_map/ppermute | solution.py:474
  2.4 0.1 collective-permute-start.2
  2.5 5.8 %collective-permute-start.1 = (f32[48,128]{1,0:T(8,128)S(1)}, f32[48,128]{1,0:T(8,128)S(1)}, u32[]{:S(2)}, u32[]{:S(2)}) collective-permute-start(f32[48,128]{1,0:T(8,128)S(1)} %get-tuple-element.23), channel_id=1, source_target_pairs={{1,2},{3,4},{5,6},{7,8},{9,10},{11,12},{13,14},{15,16},{17,18},{19... | collective-permute-start | bytes 73736 | tf_op jit(solution)/shard_map/ppermute | solution.py:473
  8.3 1.6 %shard_map.31 = (f32[64,640]{1,0:T(8,128)S(1)}, f32[64,640]{1,0:T(8,128)S(1)}, f32[2,5,40,128]{3,2,1,0:T(8,128)S(1)}, f32[2,5,24,128]{3,2,1,0:T(8,128)S(1)}, f32[8,8,128]{2,1,0:T(8,128)S(1)}) custom-call(f32[5,64,128]{2,1,0:T(8,128)S(1)} %get-tuple-element.19.z0, f32[3,32,128]{2,1,0:T(8,128)S(1)} %get-tuple-element.20.z1, f32[2,16,128]{2,1,0:T(8,128)S(1)} %get-tuple-element.21.z2), custom_call_target="tpu_custom_call" | custom-call | flops 100000000 | bytes 524288 | tf_op jit(solution)/shard_map/pallas_call | solution.py:443
  9.9 0.0 collective-permute-done.r1_ref
  9.9 0.0 collective-permute-done.2.r3_ref
  9.9 0.0 collective-permute-done.1.r2_ref
  9.9 0.7 %shard_map.32 = (f32[64,640]{1,0:T(8,128)S(1)}, f32[64,640]{1,0:T(8,128)S(1)}, f32[2,5,40,128]{3,2,1,0:T(8,128)S(1)}, f32[2,5,24,128]{3,2,1,0:T(8,128)S(1)}, f32...) custom-call(f32[5,64,128]{2,1,0:T(8,128)S(1)} %get-tuple-element.19., ...), custom_call_target="tpu_custom_call", output_to_operand_aliasing={{0}: (7, {}), {1}: (8, {}), {2}: (9, {}), {3}: (10, {})} | custom-call | flops 1000000 | bytes 524288 | tf_op jit(solution)/shard_map/pallas_call | solution.py:443
  10.7 11.1 %all_to_all.5 = f32[32,1,128]{2,1,0:T(1,128)S(1)} all-to-all(f32[32,1,128]{2,1,0:T(1,128)S(1)} %get-tuple-element.29), channel_id=1, replica_groups=mesh['rows'=32] {'rows'}, dimensions={0} | all-to-all | bytes 32768 | tf_op jit(solution)/shard_map/all_to_all | solution.py:493
  21.8 1.1 %shard_map.33 = (f32[64,640]{1,0:T(8,128)}, f32[64,640]{1,0:T(8,128)}) custom-call(f32[32,128]{1,0:T(8,128)S(1)} %bitcast.1, f32[64,640]{1,0:T(8,128)S(1)} %get-tuple-element.30.s0, f32[64,640]{1,0:T(8,128)S(1)} %get-tuple-element.31.b0, f32[2,5,64,128]{3,2,1,0:T(8,128)S(1)} %get-tuple-element.32.u1, f32[2,5,64,128]{3,2,1,0:T(8,128)S(1)} %get-tuple-element.33.u2, ...), custom_call_target="tpu_custom_call" | custom-call | flops 1000000 | bytes 524288 | tf_op jit(solution)/shard_map/pallas_call | solution.py:443
Async XLA Ops:
  1.9 8.0 %collective-permute-start = (f32[48,128]{1,0:T(8,128)S(1)}, f32[48,128]{1,0:T(8,128)S(1)}, u32[]{:S(2)}, u32[]{:S(2)}) collective-permute-start(f32[48,128]{1,0:T(8,128)S(1)} %get-tuple-element.22), channel_id=1, source_target_pairs={{0,1},{2,3},{4,5},{6,7},{8,9},{10,11},{12,13},{14,15},{16,17},{18,... | collective-permute-start | bytes 73736 | tf_op jit(solution)/shard_map/ppermute | solution.py:474
  2.4 7.5 %collective-permute-start.2 = (f32[48,128]{1,0:T(8,128)S(1)}, f32[48,128]{1,0:T(8,128)S(1)}, u32[]{:S(2)}, u32[]{:S(2)}) collective-permute-start(f32[48,128]{1,0:T(8,128)S(1)} %get-tuple-element.23), channel_id=1, source_target_pairs={{0,1},{2,3},{4,5},{6,7},{8,9},{10,11},{12,13},{14,15},{16,17},{18,... | collective-permute-start | bytes 73736 | tf_op jit(solution)/shard_map/ppermute | solution.py:475
  2.5 7.4 %collective-permute-start.1 = (f32[48,128]{1,0:T(8,128)S(1)}, f32[48,128]{1,0:T(8,128)S(1)}, u32[]{:S(2)}, u32[]{:S(2)}) collective-permute-start(f32[48,128]{1,0:T(8,128)S(1)} %get-tuple-element.23), channel_id=1, source_target_pairs={{1,2},{3,4},{5,6},{7,8},{9,10},{11,12},{13,14},{15,16},{17,18},{19... | collective-permute-start | bytes 73736 | tf_op jit(solution)/shard_map/ppermute | solution.py:473

commit v9 on v8

--- a/solution.py
+++ b/solution.py
@@ -336,7 +336,11 @@
             slope4, bend4 = jnp.where(kept, slope, 0.0), jnp.where(kept, bend * bend, 0.0)
         for field, v in enumerate((slope, bend)):
             v = jnp.where(first & (row < 0), v[1:2], jnp.where(last & (row >= h), v[h : h + 1], v))
-            f[field, 0:rows, :] = jnp.where(row <= h, v, 0.0)
+            if k == 3:
+                f[field] = v[0:8]
+                f4[field, sizes[4][0] + 2 :, :] = pad_rows(v[8 : h + 2])[0 : 6 - sizes[4][0]]
+            else:
+                f[field, 0 : h + 2, :] = v[0 : h + 2]
     table = jnp.zeros((8, 128), f32)
     lane = lane_of(table)
     for k, pair in enumerate(totals):
@@ -377,6 +381,21 @@
     return out
 
 
+def last_refine(sizes, v, count):
+    lane, coarse = lane_of(v), row_of(v) < sizes[LEVELS][0] + 2
+    f = jnp.where(coarse, 1 << LEVELS, 1 << (LEVELS - 1))
+    phase = lane & (f - 1)
+    step = jnp.where(phase < f >> 1, -1, 1)
+    other = jnp.abs((phase.astype(f32) + 0.5) * jnp.where(coarse, 2.0**-LEVELS, 2.0 ** (1 - LEVELS)) - 0.5)
+    end = jnp.where(coarse, sizes[LEVELS][1] - 1, sizes[LEVELS - 1][1] - 1)
+    out = []
+    for c in range(count):
+        centre = jnp.where(coarse, (128 * c + lane) >> LEVELS, (128 * c + lane) >> (LEVELS - 1))
+        near = jnp.clip(centre + step, 0, end)
+        out.append((1.0 - other) * lanes(v, centre) + other * lanes(v, near))
+    return out
+
+
 def finish_kernel(sizes, cells, v_ref, s0, b0, u1, u2, f3, f4, slope_ref, bend_ref, t3, t4, u3, u4, slope_buf, bend_buf, sems):
     h0, width0 = sizes[0]
     count = width0 // 128
@@ -393,10 +412,11 @@
     mean = sums / number
     scale = jnp.where(lane < 64, 1.0 / (mean + EPS), 1.0 / jnp.sqrt(mean + EPS))
     for field in range(2):
-        for k, f, t in ((4, f4, t4), (3, f3, t3)):
-            for at in range(0, f.shape[1], 8):
-                for c, v in enumerate(cols_refine(split(f[field, at : at + 8, :]), k, sizes[k][1], count)):
-                    t[field, c, at : at + 8, :] = v
+        for c, v in enumerate(cols_refine([f3[field]], 3, sizes[3][1], count)):
+            t3[field, c, 0:8, :] = v
+        for c, v in enumerate(last_refine(sizes, f4[field], count)):
+            t4[field, c] = v
+            t3[field, c, 8 : sizes[3][0] + 2, :] = v[sizes[4][0] + 2 : sizes[4][0] + sizes[3][0] - 4]
         rows_refine(t3, u3, field, 3, sizes[3][0])
         pos = (lax.broadcasted_iota(jnp.int32, (8, 128), 0).astype(f32) + 0.5) * 0.0625
         for c in range(count):
@@ -476,7 +496,7 @@
     acc = (2 * LEVELS, 8, 128)
     fine = [(2, z_shapes[0][0], -(-(h + 2) // 8) * 8, 128) for h, _ in sizes[1:]]
     whole = (2, *z_shapes[0])
-    f_shapes = fine[:2] + [whole] * 2 + [(2, -(-(h + 2) // 8) * 8, up128(w)) for h, w in sizes[3:]]
+    f_shapes = fine[:2] + [whole] * 2 + [(2, 8, up128(w)) for _, w in sizes[3:]]
     s0, b0, t1, t2, sums = call(
         functools.partial(inner_kernel, sizes), [grid.shape, grid.shape] + fine[:2] + [acc], flops=10**8
     )(z0, z1, z2)

time: 23.1 us -> 23 us (level)
  no operation moved by 1% of the time
where the time goes in v9:
time: 23 us; the launch traced here: 22.8 us
  blocking collectives  11.1 us (48%)
  starting transfers between devices  6.43 us (28%)
  Pallas kernels  4.58 us (20%)
  between operations  0.67 us (3%)
    all_to_all x1, blocking collectives, local(): seen = lax.all_to_all(sums, 'rows', 0, 0, tiled=True).reshape(count, 128)  11.1 us
    ppermute x1, starting transfers between devices, local(): r2 = lax.ppermute(m2, 'rows', pairs2)  5.8 us
    pallas_call x4, Pallas kernels, call(): pl.pallas_call(kernel, out_shape=[jax.ShapeDtypeStruct(s, f32) for s in o...  4.58 us
    ppermute x1, starting transfers between devices, local(): r1 = lax.ppermute(m1, 'rows', pairs1)  0.56 us
  transfers between devices with their start and end apart: 3, of which 0 were waited for; matrix products, arithmetic and copies ran while one was open for 0% of the time, Pallas kernels for 7%

profile of v9, /device:TPU:0, one launch (start us, length us, event | category | flops | bytes accessed | tf_op | source)
XLA Modules:
  0.0 22.8 jit_solution(15556242090035877483)
XLA Ops:
  0.6 1.2 %shard_map.30 = (f32[48,128]{1,0:T(8,128)S(1)}, f32[48,128]{1,0:T(8,128)S(1)}, f32[5,64,128]{2,1,0:T(8,128)S(1)}, f32[3,32,128]{2,1,0:T(8,128)S(1)}, f32[2,16,128]{2,1,0:T(8,128)S(1)}) custom-call(f32[64,640]{1,0:T(8,128)} %x_ref.1), custom_call_target="tpu_custom_call" | custom-call | flops 1000000 | bytes 524288 | tf_op jit(solution)/shard_map/pallas_call | solution.py:463
  1.9 0.6 %collective-permute-start = (f32[48,128]{1,0:T(8,128)S(1)}, f32[48,128]{1,0:T(8,128)S(1)}, u32[]{:S(2)}, u32[]{:S(2)}) collective-permute-start(f32[48,128]{1,0:T(8,128)S(1)} %get-tuple-element.22), channel_id=1, source_target_pairs={{0,1},{2,3},{4,5},{6,7},{8,9},{10,11},{12,13},{14,15},{16,17},{18,... | collective-permute-start | bytes 73736 | tf_op jit(solution)/shard_map/ppermute | solution.py:494
  2.4 0.1 collective-permute-start.2
  2.5 5.8 %collective-permute-start.1 = (f32[48,128]{1,0:T(8,128)S(1)}, f32[48,128]{1,0:T(8,128)S(1)}, u32[]{:S(2)}, u32[]{:S(2)}) collective-permute-start(f32[48,128]{1,0:T(8,128)S(1)} %get-tuple-element.23), channel_id=1, source_target_pairs={{1,2},{3,4},{5,6},{7,8},{9,10},{11,12},{13,14},{15,16},{17,18},{19... | collective-permute-start | bytes 73736 | tf_op jit(solution)/shard_map/ppermute | solution.py:493
  8.3 1.6 %shard_map.31 = (f32[64,640]{1,0:T(8,128)S(1)}, f32[64,640]{1,0:T(8,128)S(1)}, f32[2,5,40,128]{3,2,1,0:T(8,128)S(1)}, f32[2,5,24,128]{3,2,1,0:T(8,128)S(1)}, f32[8,8,128]{2,1,0:T(8,128)S(1)}) custom-call(f32[5,64,128]{2,1,0:T(8,128)S(1)} %get-tuple-element.19.z0, f32[3,32,128]{2,1,0:T(8,128)S(1)} %get-tuple-element.20.z1, f32[2,16,128]{2,1,0:T(8,128)S(1)} %get-tuple-element.21.z2), custom_call_target="tpu_custom_call" | custom-call | flops 100000000 | bytes 524288 | tf_op jit(solution)/shard_map/pallas_call | solution.py:463
  9.9 0.0 collective-permute-done.r1_ref
  9.9 0.0 collective-permute-done.2.r3_ref
  9.9 0.0 collective-permute-done.1.r2_ref
  9.9 0.7 %shard_map.32 = (f32[64,640]{1,0:T(8,128)S(1)}, f32[64,640]{1,0:T(8,128)S(1)}, f32[2,5,40,128]{3,2,1,0:T(8,128)S(1)}, f32[2,5,24,128]{3,2,1,0:T(8,128)S(1)}, f32...) custom-call(f32[5,64,128]{2,1,0:T(8,128)S(1)} %get-tuple-element.19., ...), custom_call_target="tpu_custom_call", output_to_operand_aliasing={{0}: (7, {}), {1}: (8, {}), {2}: (9, {}), {3}: (10, {})} | custom-call | flops 1000000 | bytes 524288 | tf_op jit(solution)/shard_map/pallas_call | solution.py:463
  10.7 11.1 %all_to_all.5 = f32[32,1,128]{2,1,0:T(1,128)S(1)} all-to-all(f32[32,1,128]{2,1,0:T(1,128)S(1)} %get-tuple-element.29), channel_id=1, replica_groups=mesh['rows'=32] {'rows'}, dimensions={0} | all-to-all | bytes 32768 | tf_op jit(solution)/shard_map/all_to_all | solution.py:513
  21.8 1.0 %shard_map.33 = (f32[64,640]{1,0:T(8,128)}, f32[64,640]{1,0:T(8,128)}) custom-call(f32[32,128]{1,0:T(8,128)S(1)} %bitcast.1, f32[64,640]{1,0:T(8,128)S(1)} %get-tuple-element.30.s0, f32[64,640]{1,0:T(8,128)S(1)} %get-tuple-element.31.b0, f32[2,5,64,128]{3,2,1,0:T(8,128)S(1)} %get-tuple-element.32.u1, f32[2,5,64,128]{3,2,1,0:T(8,128)S(1)} %get-tuple-element.33.u2, ...), custom_call_target="tpu_custom_call" | custom-call | flops 1000000 | bytes 524288 | tf_op jit(solution)/shard_map/pallas_call | solution.py:463
Async XLA Ops:
  1.9 8.0 %collective-permute-start = (f32[48,128]{1,0:T(8,128)S(1)}, f32[48,128]{1,0:T(8,128)S(1)}, u32[]{:S(2)}, u32[]{:S(2)}) collective-permute-start(f32[48,128]{1,0:T(8,128)S(1)} %get-tuple-element.22), channel_id=1, source_target_pairs={{0,1},{2,3},{4,5},{6,7},{8,9},{10,11},{12,13},{14,15},{16,17},{18,... | collective-permute-start | bytes 73736 | tf_op jit(solution)/shard_map/ppermute | solution.py:494
  2.4 7.5 %collective-permute-start.2 = (f32[48,128]{1,0:T(8,128)S(1)}, f32[48,128]{1,0:T(8,128)S(1)}, u32[]{:S(2)}, u32[]{:S(2)}) collective-permute-start(f32[48,128]{1,0:T(8,128)S(1)} %get-tuple-element.23), channel_id=1, source_target_pairs={{0,1},{2,3},{4,5},{6,7},{8,9},{10,11},{12,13},{14,15},{16,17},{18,... | collective-permute-start | bytes 73736 | tf_op jit(solution)/shard_map/ppermute | solution.py:495
  2.5 7.4 %collective-permute-start.1 = (f32[48,128]{1,0:T(8,128)S(1)}, f32[48,128]{1,0:T(8,128)S(1)}, u32[]{:S(2)}, u32[]{:S(2)}) collective-permute-start(f32[48,128]{1,0:T(8,128)S(1)} %get-tuple-element.23), channel_id=1, source_target_pairs={{1,2},{3,4},{5,6},{7,8},{9,10},{11,12},{13,14},{15,16},{17,18},{19... | collective-permute-start | bytes 73736 | tf_op jit(solution)/shard_map/ppermute | solution.py:493

commit v10 on v9

--- a/solution.py
+++ b/solution.py
@@ -159,9 +159,10 @@
     root = jnp.sqrt(base)
     y = jnp.sqrt(steep) / (1.0 + root)
     y2 = y * y
-    acc = ATAN[-1]
-    for c in ATAN[-2::-1]:
-        acc = acc * y2 + c
+    y4 = y2 * y2
+    y8 = y4 * y4
+    pairs = [ATAN[i] + ATAN[i + 1] * y2 for i in range(0, 8, 2)]
+    acc = (pairs[0] + pairs[1] * y4) + ((pairs[2] + pairs[3] * y4) + ATAN[8] * y8) * y8
     slope = 2.0 * y * acc
     bend = -(pp * r + 2.0 * (p * q) * u + qq * t) / (base * root)
     return slope, bend

time: 23 us -> 23.1 us (level)
  no operation moved by 1% of the time
where the time goes in v10:
time: 23.1 us; the launch traced here: 22.8 us
  blocking collectives  11.2 us (48%)
  starting transfers between devices  6.43 us (28%)
  Pallas kernels  4.58 us (20%)
  between operations  0.67 us (3%)
    all_to_all x1, blocking collectives, local(): seen = lax.all_to_all(sums, 'rows', 0, 0, tiled=True).reshape(count, 128)  11.2 us
    ppermute x1, starting transfers between devices, local(): r2 = lax.ppermute(m2, 'rows', pairs2)  5.8 us
    pallas_call x4, Pallas kernels, call(): pl.pallas_call(kernel, out_shape=[jax.ShapeDtypeStruct(s, f32) for s in o...  4.58 us
    ppermute x1, starting transfers between devices, local(): r1 = lax.ppermute(m1, 'rows', pairs1)  0.56 us
  transfers between devices with their start and end apart: 3, of which 0 were waited for; matrix products, arithmetic and copies ran while one was open for 0% of the time, Pallas kernels for 7%

profile of v10, /device:TPU:0, one launch (start us, length us, event | category | flops | bytes accessed | tf_op | source)
XLA Modules:
  0.0 22.8 jit_solution(8818256667716267311)
XLA Ops:
  0.6 1.2 %shard_map.30 = (f32[48,128]{1,0:T(8,128)S(1)}, f32[48,128]{1,0:T(8,128)S(1)}, f32[5,64,128]{2,1,0:T(8,128)S(1)}, f32[3,32,128]{2,1,0:T(8,128)S(1)}, f32[2,16,128]{2,1,0:T(8,128)S(1)}) custom-call(f32[64,640]{1,0:T(8,128)} %x_ref.1), custom_call_target="tpu_custom_call" | custom-call | flops 1000000 | bytes 524288 | tf_op jit(solution)/shard_map/pallas_call | solution.py:464
  1.9 0.6 %collective-permute-start = (f32[48,128]{1,0:T(8,128)S(1)}, f32[48,128]{1,0:T(8,128)S(1)}, u32[]{:S(2)}, u32[]{:S(2)}) collective-permute-start(f32[48,128]{1,0:T(8,128)S(1)} %get-tuple-element.22), channel_id=1, source_target_pairs={{0,1},{2,3},{4,5},{6,7},{8,9},{10,11},{12,13},{14,15},{16,17},{18,... | collective-permute-start | bytes 73736 | tf_op jit(solution)/shard_map/ppermute | solution.py:495
  2.4 0.1 collective-permute-start.2
  2.5 5.8 %collective-permute-start.1 = (f32[48,128]{1,0:T(8,128)S(1)}, f32[48,128]{1,0:T(8,128)S(1)}, u32[]{:S(2)}, u32[]{:S(2)}) collective-permute-start(f32[48,128]{1,0:T(8,128)S(1)} %get-tuple-element.23), channel_id=1, source_target_pairs={{1,2},{3,4},{5,6},{7,8},{9,10},{11,12},{13,14},{15,16},{17,18},{19... | collective-permute-start | bytes 73736 | tf_op jit(solution)/shard_map/ppermute | solution.py:494
  8.3 1.5 %shard_map.31 = (f32[64,640]{1,0:T(8,128)S(1)}, f32[64,640]{1,0:T(8,128)S(1)}, f32[2,5,40,128]{3,2,1,0:T(8,128)S(1)}, f32[2,5,24,128]{3,2,1,0:T(8,128)S(1)}, f32[8,8,128]{2,1,0:T(8,128)S(1)}) custom-call(f32[5,64,128]{2,1,0:T(8,128)S(1)} %get-tuple-element.19.z0, f32[3,32,128]{2,1,0:T(8,128)S(1)} %get-tuple-element.20.z1, f32[2,16,128]{2,1,0:T(8,128)S(1)} %get-tuple-element.21.z2), custom_call_target="tpu_custom_call" | custom-call | flops 100000000 | bytes 524288 | tf_op jit(solution)/shard_map/pallas_call | solution.py:464
  9.8 0.0 collective-permute-done.r1_ref
  9.9 0.0 collective-permute-done.2.r3_ref
  9.9 0.0 collective-permute-done.1.r2_ref
  9.9 0.8 %shard_map.32 = (f32[64,640]{1,0:T(8,128)S(1)}, f32[64,640]{1,0:T(8,128)S(1)}, f32[2,5,40,128]{3,2,1,0:T(8,128)S(1)}, f32[2,5,24,128]{3,2,1,0:T(8,128)S(1)}, f32...) custom-call(f32[5,64,128]{2,1,0:T(8,128)S(1)} %get-tuple-element.19., ...), custom_call_target="tpu_custom_call", output_to_operand_aliasing={{0}: (7, {}), {1}: (8, {}), {2}: (9, {}), {3}: (10, {})} | custom-call | flops 1000000 | bytes 524288 | tf_op jit(solution)/shard_map/pallas_call | solution.py:464
  10.7 11.2 %all_to_all.5 = f32[32,1,128]{2,1,0:T(1,128)S(1)} all-to-all(f32[32,1,128]{2,1,0:T(1,128)S(1)} %get-tuple-element.29), channel_id=1, replica_groups=mesh['rows'=32] {'rows'}, dimensions={0} | all-to-all | bytes 32768 | tf_op jit(solution)/shard_map/all_to_all | solution.py:514
  21.8 1.0 %shard_map.33 = (f32[64,640]{1,0:T(8,128)}, f32[64,640]{1,0:T(8,128)}) custom-call(f32[32,128]{1,0:T(8,128)S(1)} %bitcast.1, f32[64,640]{1,0:T(8,128)S(1)} %get-tuple-element.30.s0, f32[64,640]{1,0:T(8,128)S(1)} %get-tuple-element.31.b0, f32[2,5,64,128]{3,2,1,0:T(8,128)S(1)} %get-tuple-element.32.u1, f32[2,5,64,128]{3,2,1,0:T(8,128)S(1)} %get-tuple-element.33.u2, ...), custom_call_target="tpu_custom_call" | custom-call | flops 1000000 | bytes 524288 | tf_op jit(solution)/shard_map/pallas_call | solution.py:464
Async XLA Ops:
  1.9 8.0 %collective-permute-start = (f32[48,128]{1,0:T(8,128)S(1)}, f32[48,128]{1,0:T(8,128)S(1)}, u32[]{:S(2)}, u32[]{:S(2)}) collective-permute-start(f32[48,128]{1,0:T(8,128)S(1)} %get-tuple-element.22), channel_id=1, source_target_pairs={{0,1},{2,3},{4,5},{6,7},{8,9},{10,11},{12,13},{14,15},{16,17},{18,... | collective-permute-start | bytes 73736 | tf_op jit(solution)/shard_map/ppermute | solution.py:495
  2.4 7.4 %collective-permute-start.2 = (f32[48,128]{1,0:T(8,128)S(1)}, f32[48,128]{1,0:T(8,128)S(1)}, u32[]{:S(2)}, u32[]{:S(2)}) collective-permute-start(f32[48,128]{1,0:T(8,128)S(1)} %get-tuple-element.23), channel_id=1, source_target_pairs={{0,1},{2,3},{4,5},{6,7},{8,9},{10,11},{12,13},{14,15},{16,17},{18,... | collective-permute-start | bytes 73736 | tf_op jit(solution)/shard_map/ppermute | solution.py:496
  2.5 7.4 %collective-permute-start.1 = (f32[48,128]{1,0:T(8,128)S(1)}, f32[48,128]{1,0:T(8,128)S(1)}, u32[]{:S(2)}, u32[]{:S(2)}) collective-permute-start(f32[48,128]{1,0:T(8,128)S(1)} %get-tuple-element.23), channel_id=1, source_target_pairs={{1,2},{3,4},{5,6},{7,8},{9,10},{11,12},{13,14},{15,16},{17,18},{19... | collective-permute-start | bytes 73736 | tf_op jit(solution)/shard_map/ppermute | solution.py:494
